TPU v7x, 128 devices: a whole 4x4x4 slice. The times are simulated.
128 devices in a mesh: lat: 32 (over y, z, core), fld: 4 (over x).
Axes of the slice: x: 4, y: 4, z: 4, core: 2. Of those that a mesh axis runs over, the one named last changes fastest.
Arguments:
- grid_fields: bfloat16 [96, 1280, 2560], P('fld', 'lat'), may hold values from -6 to 6
- assign: int32 [320], replicated, may hold values from 0 to 319, each once
- limits: int32 [3], replicated, may hold values from 60 to 319, as said below
- legendre: bfloat16 [320, 641, 640], P('lat', None, 'fld'), may hold values from -0.25 to 0.25
- synth_one: bfloat16 [320, 320, 320], P('lat'), may hold values from -0.3125 to 0.3125
- synth_two: bfloat16 [320, 160, 160], P('lat'), may hold values from -0.5 to 0.5
- synth_three: bfloat16 [320, 80, 80], P('lat'), may hold values from -0.625 to 0.625
Outputs:
- spectrum: bfloat16 [96, 2, 320, 641], P('fld', None, 'lat')
- grid_one: float32 [96, 640, 1280], P('fld', 'lat')
- grid_two: float32 [96, 320, 640], P('fld', 'lat')
- grid_three: float32 [96, 160, 320], P('fld', 'lat')
Inputs may be any that keep to these rules, and one draw needn't show every extreme that they name: assign is a permutation; slot q stands for the wavenumbers assign[q] and 639 - assign[q]. limits[0] is 319, limits[2] is 60, and limits[1] lies between 120 and 159.
All inputs are finite; a program needn't handle non-finite values.
Results may differ from a plain program's by a relative error of at most 0.0077.
Values may be sent and summed in bfloat16 or wider, within the bound.
No kernel may reach another device: no remote copies, remote signals or barrier semaphores. Data moves between devices by JAX's collectives and lax.ppermute only.
A program may use at most 128 MiB of HBM per device.

v0:
```python
import math

import numpy as np
import jax
import jax.numpy as jnp
from jax import lax
from jax.experimental import pallas as pl
from jax.experimental.pallas import tpu as pltpu
from jax.sharding import PartitionSpec as P

F32 = jnp.float32
BF16 = jnp.bfloat16

COS_TERMS = (
    1.0,
    -4.93480110168457,
    4.058694839477539,
    -1.3351584672927856,
    0.23502981662750244,
    -0.025358986109495163,
    0.0015939108561724424,
)
SIN_TERMS = (
    3.141592502593994,
    -5.167698860168457,
    2.5499982833862305,
    -0.5985506176948547,
    0.0807478278875351,
    -0.006089475005865097,
)

NT = (((1,), (1,)), ((), ()))
NN = (((1,), (0,)), ((), ()))
VMEM_LIMIT = 60 * 1024 * 1024


def whole(shape):
    return pl.BlockSpec(shape, lambda *_: (0,) * len(shape))


def turn(count, period):
    left = count - period * jnp.floor(count * (1.0 / period) + 0.5)
    place = left * (2.0 / period)
    square = place * place
    cosine = jnp.full_like(square, COS_TERMS[-1])
    for term in COS_TERMS[-2::-1]:
        cosine = cosine * square + term
    sine = jnp.full_like(square, SIN_TERMS[-1])
    for term in SIN_TERMS[-2::-1]:
        sine = sine * square + term
    return cosine, sine * place


def fill_table(meta_ref, column, table_ref, period, width):
    rows_total = table_ref.shape[0]
    step = 64

    def body(k, carry):
        rows = pl.ds(pl.multiple_of(k * step, step), step)
        meta = meta_ref[rows, :]
        wave = meta[:, column : column + 1]
        shift = meta[:, column + 1 : column + 2]
        scale = meta[:, column + 2 : column + 3]
        lane = lax.broadcasted_iota(jnp.int32, (step, 128), 1).astype(F32)
        cos_low, sin_low = turn(lane * wave, period)
        cos_high, sin_high = turn(lane * (wave * 128.0) + shift, period)
        cos_high = cos_high * scale
        sin_high = sin_high * scale
        for a in range(-(-width // 128)):
            size = min(128, width - 128 * a)
            value = cos_high[:, a : a + 1] * cos_low - sin_high[:, a : a + 1] * sin_low
            table_ref[rows, 128 * a : 128 * a + size] = value[:, :size].astype(BF16)
        return carry

    lax.fori_loop(0, rows_total // step, body, 0)


def dft_kernel(meta_ref, grid_ref, out_ref, even_ref, odd_ref, add_ref, sub_ref):
    half = grid_ref.shape[1] // 2
    rows = grid_ref.shape[0]
    fill_table(meta_ref, 0, even_ref, 2 * half, half)
    fill_table(meta_ref, 3, odd_ref, 2 * half, half)

    def fold(k, carry):
        part = pl.ds(pl.multiple_of(k * 64, 64), 64)
        first = grid_ref[part, :half].astype(F32)
        second = grid_ref[part, half:].astype(F32)
        add_ref[part, :] = (first + second).astype(BF16)
        sub_ref[part, :] = (first - second).astype(BF16)
        return carry

    lax.fori_loop(0, rows // 64, fold, 0)

    def block(k, carry):
        part = pl.ds(pl.multiple_of(k * 192, 192), 192)
        even = lax.dot_general(even_ref[part, :], add_ref[...], NT, preferred_element_type=F32)
        odd = lax.dot_general(odd_ref[part, :], sub_ref[...], NT, preferred_element_type=F32)
        for d in range(8):
            one = even[24 * d : 24 * d + 24]
            two = odd[24 * d : 24 * d + 24]
            value = jnp.concatenate([one[:16], one[16:] + two[:8], two[8:]], axis=0)
            out_ref[k * 8 + d, :, :rows] = value.astype(BF16)
        return carry

    lax.fori_loop(0, out_ref.shape[0] // 8, block, 0)


def lanes_kernel(wire_ref, out_ref, north_ref, south_ref):
    fields = north_ref.shape[1] // 40
    lane = lax.broadcasted_iota(jnp.int32, (8, 128), 1)

    def field(f, carry):
        base = pl.multiple_of(jnp.minimum(f * 40 // 128, 6) * 128, 128)
        offset = f * 40 - base
        rows = pl.ds(pl.multiple_of(f * 40, 8), 40)
        for half, target in ((0, north_ref), (16, south_ref)):
            for x in range(4):
                low = [jnp.zeros((8, 128), F32) for _ in range(5)]
                high = None
                for k in range(4):
                    window = wire_ref[half + 4 * x + k, :, pl.ds(base, 256)].astype(F32)
                    shift = lax.rem(40 * k - offset + 256, 128)
                    second = lane + (offset - 40 * k) >= 128
                    inside = (lane >= 40 * k) & (lane < 40 * k + 40)
                    first_rolled = pltpu.roll(window[:, :128], shift, 1)
                    next_rolled = pltpu.roll(window[:, 128:], shift, 1)
                    for t in range(5):
                        one = first_rolled[8 * t : 8 * t + 8]
                        two = next_rolled[8 * t : 8 * t + 8]
                        piece = jnp.where(second, two, one)
                        low[t] = jnp.where(inside, piece, low[t])
                    if k == 3:
                        second = lane + (offset + 8) >= 128
                        high = [
                            jnp.where(
                                lane < 32,
                                jnp.where(
                                    second,
                                    next_rolled[8 * t : 8 * t + 8],
                                    first_rolled[8 * t : 8 * t + 8],
                                ),
                                0.0,
                            )
                            for t in range(5)
                        ]
                target[2 * x, rows, :] = jnp.concatenate(low, axis=0)
                target[2 * x + 1, rows, :] = jnp.concatenate(high, axis=0)
        return carry

    lax.fori_loop(0, fields, field, 0)

    across = lax.broadcasted_iota(jnp.int32, (256, 256), 0)
    along = lax.broadcasted_iota(jnp.int32, (256, 256), 1)
    mirror = jnp.where(across + along == 159, 1.0, 0.0).astype(BF16)

    def fold(k, carry):
        rows = pl.ds(pl.multiple_of(k * 96, 96), 96)
        south = [
            lax.dot_general(
                jnp.concatenate(
                    [south_ref[6 - 2 * x, rows, :], south_ref[7 - 2 * x, rows, :]], axis=1
                ).astype(BF16),
                mirror,
                NN,
                preferred_element_type=F32,
            )
            for x in range(4)
        ]
        for t in range(8):
            second = south[t // 2][:, t % 2 * 128 : t % 2 * 128 + 128]
            first = north_ref[t, rows, :]
            north_ref[t, rows, :] = first + second
            south_ref[t, rows, :] = first - second
        return carry

    lax.fori_loop(0, north_ref.shape[1] // 96, fold, 0)

    def slot(q, carry):
        for x in range(4):
            for t in range(2):
                parts = [
                    source[2 * x + t, pl.ds(g * 10 + q, fields, stride=40), :]
                    for source in (north_ref, south_ref)
                    for g in range(4)
                ]
                part = jnp.concatenate(parts, axis=0).astype(BF16)
                if t:
                    out_ref[q, x, :, 128:] = part[:, :32]
                else:
                    out_ref[q, x, :, :128] = part
        return carry

    lax.fori_loop(0, out_ref.shape[0], slot, 0)


def turn_tables_kernel(one_ref, two_ref, three_ref, out_one, out_two, out_three):
    for source, target, groups in ((one_ref, out_one, 4), (two_ref, out_two, 2), (three_ref, out_three, 1)):
        size = source.shape[1]
        row = lax.broadcasted_iota(jnp.int32, (size, size), 0)
        column = lax.broadcasted_iota(jnp.int32, (size, size), 1)
        b = row // (16 * groups)
        a = (row // 16) % groups
        place = (row % 16) * (5 * groups) + 5 * a + b
        pick = jnp.where(place == column, 1.0, 0.0).astype(BF16)
        target[0] = lax.dot_general(pick, source[0], NT, preferred_element_type=F32).astype(BF16)


def slot_kernel(
    info_ref,
    waves_ref,
    own_ref,
    left_ref,
    right_ref,
    far_low_ref,
    far_high_ref,
    one_ref,
    two_ref,
    three_ref,
    spectrum_ref,
    wire_ref,
    row_ref,
    pack_ref,
):
    q = pl.program_id(0)
    x = info_ref[0]
    p = info_ref[1 + q]

    @pl.when(q == 0)
    def _():
        row_ref[...] = jnp.zeros_like(row_ref)
        pack_ref[...] = jnp.zeros_like(pack_ref)

    far = jnp.where(q < 5, far_low_ref[0], far_high_ref[0])
    total = lax.dot_general(waves_ref[0, x], own_ref[0], NN, preferred_element_type=F32)
    for step, block in ((3, left_ref[0]), (1, right_ref[0]), (2, far)):
        total += lax.dot_general(
            waves_ref[0, (x + step) % 4], block, NN, preferred_element_type=F32
        )
    rank = lax.broadcasted_iota(jnp.int32, (48, 641), 1)
    even_pair = p % 2 == 0
    sym = rank < 321
    place = jnp.where(sym, rank, rank - 321)
    bound = jnp.where(sym, (641 - p) // 2, (640 - p) // 2)
    first = (place < bound) == even_pair
    chosen = jnp.where(
        sym,
        jnp.where(first, total[0:48], total[48:96]),
        jnp.where(first, total[96:144], total[144:192]),
    ).astype(BF16)
    spectrum_ref[0] = chosen
    row_ref[:, :641] = chosen.astype(F32)
    rows = row_ref[...]
    group = 0
    for level, table_ref, count in ((0, one_ref, 4), (1, two_ref, 2), (2, three_ref, 1)):
        size = table_ref.shape[1]
        half = size // 2
        limit = info_ref[11 + level]
        lane = lax.broadcasted_iota(jnp.int32, (48, size), 1)
        is_sym = lane < half
        later = pltpu.roll(rows, 768 - 321 + half, 1)[:, :size]
        order = p + jnp.where(is_sym, 2 * lane, 2 * (lane - half) + 1)
        kept = jnp.where(order <= limit, jnp.where(is_sym, rows[:, :size], later), 0.0)
        both = jnp.concatenate(
            [kept, jnp.where(is_sym, kept, -kept), jnp.zeros((32, size), F32)], axis=0
        ).astype(BF16)
        value = lax.dot_general(table_ref[0], both, NT, preferred_element_type=F32)
        many = 16 * count
        lane = lax.broadcasted_iota(jnp.int32, (many, 128), 1)
        for sign in range(2):
            for c in range(2):
                packed = jnp.zeros((many, 128), F32)
                for b in range(5):
                    part = value[many * b : many * b + many]
                    move = 24 * (b - 2 * sign - c) % 128
                    if move:
                        part = pltpu.roll(part, move, 1)
                    packed = jnp.where((lane >= 24 * b) & (lane < 24 * b + 24), part, packed)
                for a in range(count):
                    start = sign * 16 * 144 + 20 * (group + a) + 10 * c + q
                    pack_ref[pl.ds(start, 16, stride=144), :] = packed[16 * a : 16 * a + 16]
        group += count

    @pl.when(q == pl.num_programs(0) - 1)
    def _():
        for d in range(16):
            wire_ref[d] = pack_ref[144 * d : 144 * d + 144, :].astype(BF16)
            wire_ref[31 - d] = pack_ref[144 * (16 + d) : 144 * (17 + d), :].astype(BF16)


def inverse_table_kernel(meta_ref, one_ref, one_late_ref, two_ref, two_late_ref, three_ref):
    fill_table(meta_ref, 0, one_ref, 1280, 1280)
    fill_table(meta_ref, 3, one_late_ref, 1280, 1280)
    fill_table(meta_ref, 6, two_ref, 640, 640)
    fill_table(meta_ref, 9, two_late_ref, 640, 640)
    fill_table(meta_ref, 12, three_ref, 320, 320)


def inverse_kernel(
    info_ref,
    wire_ref,
    one_ref,
    one_late_ref,
    two_ref,
    two_late_ref,
    three_ref,
    out_one,
    out_two,
    out_three,
):
    late_half = info_ref[0]
    across = lax.broadcasted_iota(jnp.int32, (128, 128), 0)
    along = lax.broadcasted_iota(jnp.int32, (128, 128), 1)
    same = jnp.where(across == along, 1.0, 0.0).astype(BF16)

    def lines(group):
        start = 20 * group // 8 * 8
        part = wire_ref[:, start : start + 24, :].astype(F32)
        part = part.reshape(part.shape[0] * 24, 128).astype(BF16)
        return lax.dot_general(same, part, NT, preferred_element_type=F32).astype(BF16)

    def place(target, a, value):
        last = target.shape[0] - 1
        for b in range(5):
            row = 5 * a + b
            row = jnp.where(late_half == 1, last - row, row)
            target[row] = value[24 * b : 24 * b + 24]

    for target, tables, group, count in (
        (out_one, (one_ref, one_late_ref), 0, 4),
        (out_two, (two_ref, two_late_ref), 4, 2),
        (out_three, (three_ref,), 6, 1),
    ):
        for late, table in enumerate(tables):
            members = [a for a in range(count) if (group + a) % 2 == late]
            left = [lines(group + a) for a in members]
            left = jnp.concatenate(left, axis=0) if len(left) > 1 else left[0]
            value = lax.dot_general(left, table[...], NN, preferred_element_type=F32)
            for k, a in enumerate(members):
                place(target, a, value[128 * k : 128 * k + 128])


def call(kernel, out_shape, **kw):
    return pl.pallas_call(
        kernel,
        out_shape=out_shape,
        compiler_params=pltpu.CompilerParams(vmem_limit_bytes=VMEM_LIMIT),
        **kw,
    )


def spread(pairs, early):
    spare = jnp.zeros((pairs.shape[0], 4), F32)
    parts = [pairs, pairs, spare] if early else [spare, pairs, pairs]
    return jnp.concatenate(parts, axis=1).reshape(-1)


def steady(first, second, early):
    parts = [first] * 10 + [second] * 10
    parts = parts + [0.0] * 4 if early else [0.0] * 4 + parts
    return jnp.asarray(np.tile(np.asarray(parts, np.float32), 32))


def on_device(grid_fields, assign, limits, legendre, synth_one, synth_two, synth_three):
    fields, rows, lon = grid_fields.shape
    lat_at = lax.axis_index("lat")
    fld_at = lax.axis_index("fld")
    pairs = assign.reshape(32, 10)
    even = jnp.where(pairs % 2 == 0, pairs, 639 - pairs).astype(F32)
    odd = 639.0 - even
    scale = 1.0 / math.sqrt(lon)
    meta = jnp.stack(
        [
            spread(even, True),
            steady(0.0, lon / 4.0, True),
            steady(scale, scale, True),
            spread(odd, False),
            steady(0.0, lon / 4.0, False),
            steady(scale, scale, False),
        ],
        axis=1,
    )

    own = jnp.transpose(legendre, (0, 2, 1))
    right = [(k, (k + 1) % 4) for k in range(4)]
    left = [(k, (k + 3) % 4) for k in range(4)]
    from_left = lax.ppermute(own, "fld", right)
    from_right = lax.ppermute(own, "fld", left)
    far_low = lax.ppermute(from_left[:5], "fld", right)
    far_high = lax.ppermute(from_right[5:], "fld", left)

    wire = call(
        dft_kernel,
        jax.ShapeDtypeStruct((32, 40, 1024), BF16),
        scratch_shapes=[
            pltpu.VMEM((768, lon // 2), BF16),
            pltpu.VMEM((768, lon // 2), BF16),
            pltpu.VMEM((fields * rows, lon // 2), BF16),
            pltpu.VMEM((fields * rows, lon // 2), BF16),
        ],
        name="dft",
    )(meta, grid_fields.reshape(fields * rows, lon))
    assign_after, synth_one, synth_two, synth_three, wire = lax.optimization_barrier(
        (assign, synth_one, synth_two, synth_three, wire)
    )
    wire = lax.all_to_all(wire, "lat", split_axis=0, concat_axis=0, tiled=True)

    turned = call(
        turn_tables_kernel,
        [jax.ShapeDtypeStruct(t.shape, BF16) for t in (synth_one, synth_two, synth_three)],
        grid=(10,),
        in_specs=[
            pl.BlockSpec((1,) + t.shape[1:], lambda q: (q, 0, 0))
            for t in (synth_one, synth_two, synth_three)
        ],
        out_specs=[
            pl.BlockSpec((1,) + t.shape[1:], lambda q: (q, 0, 0))
            for t in (synth_one, synth_two, synth_three)
        ],
        name="turn_tables",
    )(synth_one, synth_two, synth_three)

    pairs = assign_after.reshape(32, 10)
    plain = pairs.astype(F32)
    weight = jnp.where(pairs == 0, 1.0, 2.0).astype(F32)
    columns = []
    for size in (1280, 640, 320):
        for early in (True, False) if size > 320 else (True,):
            columns += [
                spread(plain, early),
                steady(0.0, size / 4.0, early),
                spread(weight * (1.0 / math.sqrt(size)), early),
            ]
    inverse_meta = jnp.stack(columns, axis=1)
    tables = call(
        inverse_table_kernel,
        [jax.ShapeDtypeStruct((768, n), BF16) for n in (1280, 1280, 640, 640, 320)],
        name="inverse_tables",
    )(inverse_meta)

    waves = call(
        lanes_kernel,
        jax.ShapeDtypeStruct((10, 4, 192, 160), BF16),
        scratch_shapes=[
            pltpu.VMEM((8, fields * rows, 128), F32),
            pltpu.VMEM((8, fields * rows, 128), F32),
        ],
        name="lanes",
    )(wire)

    info = jnp.concatenate(
        [
            fld_at.reshape(1),
            lax.dynamic_slice_in_dim(assign, lat_at * 10, 10),
            limits,
        ]
    )
    block = pl.BlockSpec((1, 160, 641), lambda q, *_: (q, 0, 0))
    spectrum, level_wire = call(
        slot_kernel,
        [
            jax.ShapeDtypeStruct((10, 2 * fields, 641), BF16),
            jax.ShapeDtypeStruct((32, 144, 128), BF16),
        ],
        grid_spec=pltpu.PrefetchScalarGridSpec(
            num_scalar_prefetch=1,
            grid=(10,),
            in_specs=[
                pl.BlockSpec((1, 4, 192, 160), lambda q, *_: (q, 0, 0, 0)),
                block,
                block,
                block,
                pl.BlockSpec((1, 160, 641), lambda q, *_: (jnp.minimum(q, 4), 0, 0)),
                pl.BlockSpec((1, 160, 641), lambda q, *_: (jnp.maximum(q - 5, 0), 0, 0)),
            ]
            + [pl.BlockSpec((1,) + t.shape[1:], lambda q, *_: (q, 0, 0)) for t in turned],
            out_specs=[
                pl.BlockSpec((1, 2 * fields, 641), lambda q, *_: (q, 0, 0)),
                pl.BlockSpec((32, 144, 128), lambda q, *_: (0, 0, 0)),
            ],
            scratch_shapes=[
                pltpu.VMEM((48, 768), F32),
                pltpu.VMEM((32 * 144, 128), F32),
            ],
        ),
        name="slots",
    )(info, waves, own, from_left, from_right, far_low, far_high, *turned)

    level_wire = lax.all_to_all(level_wire, "lat", split_axis=0, concat_axis=0, tiled=True)
    late_half = (lat_at >= 16).astype(jnp.int32).reshape(1)
    vmem = pl.BlockSpec(memory_space=pltpu.VMEM)
    grids = call(
        inverse_kernel,
        [
            jax.ShapeDtypeStruct((20, fields, 1280), F32),
            jax.ShapeDtypeStruct((10, fields, 640), F32),
            jax.ShapeDtypeStruct((5, fields, 320), F32),
        ],
        in_specs=[pl.BlockSpec(memory_space=pltpu.SMEM)] + [vmem] * 6,
        out_specs=[vmem] * 3,
        name="inverse",
    )(late_half, level_wire, *tables)
    grids = [jnp.transpose(g, (1, 0, 2)) for g in grids]
    spectrum = jnp.transpose(spectrum.reshape(10, 2, fields, 641), (2, 1, 0, 3))
    return (spectrum, *grids)


def solution(mesh):
    return jax.shard_map(
        on_device,
        mesh=mesh,
        in_specs=(
            P("fld", "lat", None),
            P(),
            P(),
            P("lat", None, "fld"),
            P("lat", None, None),
            P("lat", None, None),
            P("lat", None, None),
        ),
        out_specs=(
            P("fld", None, "lat", None),
            P("fld", "lat", None),
            P("fld", "lat", None),
            P("fld", "lat", None),
        ),
        check_vma=False,
    )
```

profile of v0, /device:TPU:1, one launch (start us, length us, event | category | flops | bytes accessed | tf_op | source)
XLA Modules:
  0.0 150.7 jit_solution(11206940122259836450)
XLA Ops:
  0.6 2.1 %collective-permute-start = (bf16[10,160,641]{2,1,0:T(8,128)(2,1)}, bf16[10,160,641]{2,1,0:T(8,128)(2,1)}, u32[]{:S(2)}, u32[]{:S(2)}) collective-permute-start(bf16[10,160,641]{2,1,0:T(8,128)(2,1)} %bitcast.12), channel_id=1, source_target_pairs={{0,1},{1,2},{2,3},{3,0},{4,5},{5,6},{6,7},{7,4},{8,9},{9,10},{10,1... | collective-permute-start | bytes 6153608 | tf_op jit(solution)/shard_map/ppermute | solution.py:386
  2.7 1.4 collective-permute-start.1
  4.1 0.8 reshape.39
  5.0 0.1 stack_reshape.30
  5.2 0.8 stack.37
  5.9 0.9 copy.34.meta_ref
  6.9 20.3 %dft.1 = bf16[32,40,1024]{2,1,0:T(8,128)(2,1)} custom-call(f32[768,6]{1,0:T(8,128)} %copy.34.meta_ref, bf16[960,2560]{1,0:T(8,128)(2,1)} %bitcast.11), custom_call_target="tpu_custom_call" | custom-call | tf_op jit(solution)/shard_map/dft/pallas_call | solution.py:391
  27.2 9.4 %all-to-all-start = ((bf16[32,40,1024]{2,1,0:T(8,128)(2,1)}), bf16[32,40,1024]{2,1,0:T(8,128)(2,1)S(1)}, u32[]{:S(2)}, u32[]{:S(2)}) async-start(bf16[32,40,1024]{2,1,0:T(8,128)(2,1)} %dft.1), calls=%async_computation | async-start | bytes 5242880 | tf_op jit(solution)/shard_map/all_to_all | solution.py:405
  36.7 20.3 %collective-permute-done.left_ref = bf16[10,160,641]{2,1,0:T(8,128)(2,1)} collective-permute-done((bf16[10,160,641]{2,1,0:T(8,128)(2,1)}, bf16[10,160,641]{2,1,0:T(8,128)(2,1)}, u32[]{:S(2)}, u32[]{:S(2)}) %collective-permute-start) | collective-permute-done | bytes 2051232 | tf_op jit(solution)/shard_map/ppermute | solution.py:386
  57.0 2.4 %slice.8 = bf16[5,160,641]{2,1,0:T(8,128)(2,1)} slice(bf16[10,160,641]{2,1,0:T(8,128)(2,1)} %collective-permute-done.left_ref), slice={[0:5], [0:160], [0:641]} | slice | bytes 2051200 | tf_op jit(solution)/shard_map/slice | solution.py:388
  59.4 0.3 collective-permute-start.2
  59.7 2.4 %slice.9 = bf16[5,160,641]{2,1,0:T(8,128)(2,1)} slice(bf16[10,160,641]{2,1,0:T(8,128)(2,1)} %collective-permute-done.1.right_ref), slice={[5:10], [0:160], [0:641]} | slice | bytes 2051200 | tf_op jit(solution)/shard_map/slice | solution.py:389
  62.1 2.4 %collective-permute-start.3 = (bf16[5,160,641]{2,1,0:T(8,128)(2,1)}, bf16[5,160,641]{2,1,0:T(8,128)(2,1)}, u32[]{:S(2)}, u32[]{:S(2)}) collective-permute-start(bf16[5,160,641]{2,1,0:T(8,128)(2,1)} %slice.9), channel_id=1, source_target_pairs={{0,3},{1,0},{2,1},{3,2},{4,7},{5,4},{6,5},{7,6},{8,11},{9,8},{10,9... | collective-permute-start | bytes 3076808 | tf_op jit(solution)/shard_map/ppermute | solution.py:389
  64.6 8.6 %turn_tables.1 = (bf16[10,320,320]{2,1,0:T(8,128)(2,1)}, bf16[10,160,160]{2,1,0:T(8,128)(2,1)}, bf16[10,80,80]{2,1,0:T(8,128)(2,1)}) custom-call(bf16[10,320,320]{2,1,0:T(8,128)(2,1)} %one_ref, bf16[10,160,160]{2,1,0:T(8,128)(2,1)} %two_ref, bf16[10,80,80]{2,1,0:T(8,128)(2,1)} %three_ref), custom_call_target="tpu_custom_call" | custom-call | tf_op jit(solution)/shard_map/turn_tables/pallas_call | solution.py:407
  73.2 0.7 pad_add_fusion.info_ref
  73.9 1.5 %copy-done = bf16[32,40,1024]{2,1,0:T(8,128)(2,1)} copy-done((bf16[32,40,1024]{2,1,0:T(8,128)(2,1)}, bf16[32,40,1024]{2,1,0:T(8,128)(2,1)S(1)}, u32[]{:S(2)}) %copy-start) | copy-done | bytes 2621464
  75.4 13.1 %lanes.1.waves_ref = bf16[10,4,192,160]{3,2,1,0:T(8,128)(2,1)} custom-call(bf16[32,40,1024]{2,1,0:T(8,128)(2,1)} %copy-done), custom_call_target="tpu_custom_call" | custom-call | tf_op jit(solution)/shard_map/lanes/pallas_call | solution.py:440
  88.6 0.7 collective-permute-done.3.far_high_ref
  89.3 16.5 %slots.1 = (bf16[10,48,641]{2,1,0:T(8,128)(2,1)}, bf16[32,144,128]{2,1,0:T(8,128)(2,1)}) custom-call(s32[14]{0:T(128)} %pad_add_fusion.info_ref, bf16[10,4,192,160]{3,2,1,0:T(8,128)(2,1)} %lanes.1.waves_ref, bf16[10,160,641]{2,1,0:T(8,128)(2,1)} %bitcast.14, bf16[10,160,641]{2,1,0:T(8,128)(2,1)} %collective-permute-done.left_ref, ...), custom_call_target="tpu_custom_call" | custom-call | tf_op jit(solution)/shard_map/slots/pallas_call | solution.py:458
  105.9 11.2 %all-to-all-start.1 = ((bf16[32,144,128]{2,1,0:T(8,128)(2,1)}), bf16[32,144,128]{2,1,0:T(8,128)(2,1)S(1)}, u32[]{:S(2)}, u32[]{:S(2)}) async-start(bf16[32,144,128]{2,1,0:T(8,128)(2,1)} %get-tuple-element.30), calls=%async_computation.1 | async-start | bytes 2359296 | tf_op jit(solution)/shard_map/all_to_all | solution.py:488
  117.2 0.1 mul.30
  117.3 0.1 mul.33
  117.4 0.1 convert_element_type.12
  117.5 0.1 fusion.6
  117.7 0.1 mul.28
  117.9 0.1 stack_reshape.33
  118.5 0.1 stack.43
  118.6 0.9 copy.36.meta_ref
  119.5 21.9 %inverse_tables.1 = (bf16[768,1280]{1,0:T(8,128)(2,1)}, bf16[768,1280]{1,0:T(8,128)(2,1)}, bf16[768,640]{1,0:T(8,128)(2,1)}, bf16[768,640]{1,0:T(8,128)(2,1)}, bf16[768,320]{1,0:T(8,128)(2,1)}) custom-call(f32[768,15]{1,0:T(8,128)} %copy.36.meta_ref), custom_call_target="tpu_custom_call" | custom-call | tf_op jit(solution)/shard_map/inverse_tables/pallas_call | solution.py:434
  141.4 1.4 copy.38
  142.9 1.0 copy-done.1
  143.9 6.8 %inverse.1 = (f32[20,24,1280]{2,1,0:T(8,128)}, f32[10,24,640]{2,1,0:T(8,128)}, f32[5,24,320]{2,1,0:T(8,128)}) custom-call(s32[1]{0:T(128)} %bitcast.5.info_ref, bf16[32,144,128]{2,1,0:T(8,128)(2,1)} %copy-done.1, bf16[768,1280]{1,0:T(8,128)(2,1)} %get-tuple-element.32.one_ref, bf16[768,1280]{1,0:T(8,128)(2,1)} %get-tuple-element.33.one_late_ref, ...), custom_call_target="tpu_custom_call" | custom-call | tf_op jit(solution)/shard_map/inverse/pallas_call | solution.py:491
  (37 shorter events, 1.0 us)
Async XLA Ops:
  0.6 56.4 %collective-permute-start = (bf16[10,160,641]{2,1,0:T(8,128)(2,1)}, bf16[10,160,641]{2,1,0:T(8,128)(2,1)}, u32[]{:S(2)}, u32[]{:S(2)}) collective-permute-start(bf16[10,160,641]{2,1,0:T(8,128)(2,1)} %bitcast.12), channel_id=1, source_target_pairs={{0,1},{1,2},{2,3},{3,0},{4,5},{5,6},{6,7},{7,4},{8,9},{9,10},{10,1... | collective-permute-start | bytes 6153608 | tf_op jit(solution)/shard_map/ppermute | solution.py:386
  2.7 56.9 %collective-permute-start.1 = (bf16[10,160,641]{2,1,0:T(8,128)(2,1)}, bf16[10,160,641]{2,1,0:T(8,128)(2,1)}, u32[]{:S(2)}, u32[]{:S(2)}) collective-permute-start(bf16[10,160,641]{2,1,0:T(8,128)(2,1)} %bitcast.13), channel_id=1, source_target_pairs={{0,3},{1,0},{2,1},{3,2},{4,7},{5,4},{6,5},{7,6},{8,11},{9,8},{10,9... | collective-permute-start | bytes 6153608 | tf_op jit(solution)/shard_map/ppermute | solution.py:387
  27.2 46.7 %all-to-all-start = ((bf16[32,40,1024]{2,1,0:T(8,128)(2,1)}), bf16[32,40,1024]{2,1,0:T(8,128)(2,1)S(1)}, u32[]{:S(2)}, u32[]{:S(2)}) async-start(bf16[32,40,1024]{2,1,0:T(8,128)(2,1)} %dft.1), calls=%async_computation | async-start | bytes 5242880 | tf_op jit(solution)/shard_map/all_to_all | solution.py:405
  36.7 27.8 %copy-start.3 = (s32[320]{0:T(512)S(1)}, s32[320]{0:T(512)}, u32[]{:S(2)}) copy-start(s32[320]{0:T(512)} %param.17) | copy-start | bytes 3844
  59.4 13.8 %copy-start.9 = (s32[3]{0:T(128)S(1)}, s32[3]{0:T(128)}, u32[]{:S(2)}) copy-start(s32[3]{0:T(128)} %param.18) | copy-start | bytes 40
  59.4 29.2 %collective-permute-start.2 = (bf16[5,160,641]{2,1,0:T(8,128)(2,1)}, bf16[5,160,641]{2,1,0:T(8,128)(2,1)}, u32[]{:S(2)}, u32[]{:S(2)}) collective-permute-start(bf16[5,160,641]{2,1,0:T(8,128)(2,1)} %slice.8), channel_id=1, source_target_pairs={{0,1},{1,2},{2,3},{3,0},{4,5},{5,6},{6,7},{7,4},{8,9},{9,10},{10,1... | collective-permute-start | bytes 3076808 | tf_op jit(solution)/shard_map/ppermute | solution.py:388
  62.1 27.2 %collective-permute-start.3 = (bf16[5,160,641]{2,1,0:T(8,128)(2,1)}, bf16[5,160,641]{2,1,0:T(8,128)(2,1)}, u32[]{:S(2)}, u32[]{:S(2)}) collective-permute-start(bf16[5,160,641]{2,1,0:T(8,128)(2,1)} %slice.9), channel_id=1, source_target_pairs={{0,3},{1,0},{2,1},{3,2},{4,7},{5,4},{6,5},{7,6},{8,11},{9,8},{10,9... | collective-permute-start | bytes 3076808 | tf_op jit(solution)/shard_map/ppermute | solution.py:389
  73.9 1.5 %copy-start = (bf16[32,40,1024]{2,1,0:T(8,128)(2,1)}, bf16[32,40,1024]{2,1,0:T(8,128)(2,1)S(1)}, u32[]{:S(2)}) copy-start(bf16[32,40,1024]{2,1,0:T(8,128)(2,1)S(1)} %all-to-all-done.wire_ref) | copy-start | bytes 7864324
  105.8 12.6 %copy-start.4 = (f32[768,1]{0,1:T(1,128)S(1)}, f32[768,1]{0,1:T(1,128)}, u32[]{:S(2)}) copy-start(f32[768,1]{0,1:T(1,128)} %constant.84) | copy-start | bytes 9220
  105.8 12.6 %copy-start.5 = (f32[768,1]{0,1:T(1,128)S(1)}, f32[768,1]{0,1:T(1,128)}, u32[]{:S(2)}) copy-start(f32[768,1]{0,1:T(1,128)} %constant.85) | copy-start | bytes 9220
  105.8 12.6 %copy-start.6 = (f32[768,1]{0,1:T(1,128)S(1)}, f32[768,1]{0,1:T(1,128)}, u32[]{:S(2)}) copy-start(f32[768,1]{0,1:T(1,128)} %constant.86) | copy-start | bytes 9220
  105.8 12.6 %copy-start.7 = (f32[768,1]{0,1:T(1,128)S(1)}, f32[768,1]{0,1:T(1,128)}, u32[]{:S(2)}) copy-start(f32[768,1]{0,1:T(1,128)} %constant.87) | copy-start | bytes 9220
  105.9 12.6 %copy-start.8 = (f32[768,1]{0,1:T(1,128)S(1)}, f32[768,1]{0,1:T(1,128)}, u32[]{:S(2)}) copy-start(f32[768,1]{0,1:T(1,128)} %constant.88) | copy-start | bytes 9220
  105.9 35.6 %copy-start.2 = (bf16[10,48,641]{2,1,0:T(8,128)(2,1)S(1)}, bf16[10,48,641]{2,1,0:T(8,128)(2,1)}, u32[]{:S(2)}) copy-start(bf16[10,48,641]{2,1,0:T(8,128)(2,1)} %get-tuple-element.29) | copy-start | bytes 1846084
  105.9 37.0 %all-to-all-start.1 = ((bf16[32,144,128]{2,1,0:T(8,128)(2,1)}), bf16[32,144,128]{2,1,0:T(8,128)(2,1)S(1)}, u32[]{:S(2)}, u32[]{:S(2)}) async-start(bf16[32,144,128]{2,1,0:T(8,128)(2,1)} %get-tuple-element.30), calls=%async_computation.1 | async-start | bytes 2359296 | tf_op jit(solution)/shard_map/all_to_all | solution.py:488
  142.9 1.0 copy-start.1
where the time goes:
time: 152 us; the launch traced here: 151 us
  Pallas kernels  87.3 us (57%)
  starting transfers between devices  26.8 us (18%)
  waiting for transfers between devices  21 us (14%)
  local copies, waits for them, and re-layouts  13.6 us (9%)
    pallas_call x1, Pallas kernels, on_device(): call(inverse_table_kernel, [jax.ShapeDtypeStruct((768, n), BF16) for n in...  21.9 us
    pallas_call x1, Pallas kernels, on_device(): call(dft_kernel, jax.ShapeDtypeStruct((32, 40, 1024), BF16), scratch_shap...  20.3 us
    ppermute x1, waiting for transfers between devices, on_device(): from_left = lax.ppermute(own, 'fld', right)  20.3 us
    pallas_call x1, Pallas kernels, on_device(): call(slot_kernel, [jax.ShapeDtypeStruct((10, 2 * fields, 641), BF16), jax...  16.5 us
    pallas_call x1, Pallas kernels, on_device(): call(lanes_kernel, jax.ShapeDtypeStruct((10, 4, 192, 160), BF16), scratch...  13.1 us
    all_to_all x1, starting transfers between devices, on_device(): lax.all_to_all(level_wire, 'lat', split_axis=0, concat_axis=0, tiled=True)  11.2 us
    all_to_all x1, starting transfers between devices, on_device(): wire = lax.all_to_all(wire, 'lat', split_axis=0, concat_axis=0, tiled=True)  9.44 us
    pallas_call x1, Pallas kernels, on_device(): call(turn_tables_kernel, [jax.ShapeDtypeStruct(t.shape, BF16) for t in (s...  8.65 us
  transfers between devices with their start and end apart: 6, of which 2 were waited for; matrix products, arithmetic and copies ran while one was open for 8% of the time, Pallas kernels for 42%

commit v1 on v0

v1 whole, which is shorter than its diff:
```python
import functools
import math

import jax
import jax.numpy as jnp
from jax import lax
from jax.experimental import pallas as pl
from jax.experimental.pallas import tpu as pltpu
from jax.sharding import PartitionSpec as P

F32 = jnp.float32
BF16 = jnp.bfloat16

COS_TERMS = (
    1.0,
    -4.93480110168457,
    4.058694839477539,
    -1.3351584672927856,
    0.23502981662750244,
    -0.025358986109495163,
    0.0015939108561724424,
)
SIN_TERMS = (
    3.141592502593994,
    -5.167698860168457,
    2.5499982833862305,
    -0.5985506176948547,
    0.0807478278875351,
    -0.006089475005865097,
)

NT = (((1,), (1,)), ((), ()))
NN = (((1,), (0,)), ((), ()))


def whole(shape):
    return pl.BlockSpec(shape, lambda *_: (0,) * len(shape))


def turn(count, period):
    left = count - period * jnp.floor(count * (1.0 / period) + 0.5)
    place = left * (2.0 / period)
    square = place * place
    cosine = jnp.full_like(square, COS_TERMS[-1])
    for term in COS_TERMS[-2::-1]:
        cosine = cosine * square + term
    sine = jnp.full_like(square, SIN_TERMS[-1])
    for term in SIN_TERMS[-2::-1]:
        sine = sine * square + term
    return cosine, sine * place


def fill_table(wave, shift, scale, high_cos, high_sin, table_ref, period):
    count, width = table_ref.shape
    step = 16
    many = count // step
    low = lax.broadcasted_iota(jnp.int32, (step, width), 0).astype(F32)
    low_cos, low_sin = turn(low * wave, period)
    high = lax.broadcasted_iota(jnp.int32, (many, width), 0).astype(F32)
    first, second = turn(high * (wave * float(step)) + shift, period)
    high_cos[:many, :] = first * scale
    high_sin[:many, :] = second * scale

    def body(k, carry):
        value = high_cos[pl.ds(k, 1), :] * low_cos - high_sin[pl.ds(k, 1), :] * low_sin
        table_ref[pl.ds(pl.multiple_of(k * step, step), step), :] = value.astype(BF16)
        return carry

    lax.fori_loop(0, many, body, 0)


def identity(size):
    across = lax.broadcasted_iota(jnp.int32, (size, size), 0)
    along = lax.broadcasted_iota(jnp.int32, (size, size), 1)
    return jnp.where(across == along, 1.0, 0.0).astype(BF16)


def dft_kernel(waves_ref, grid_ref, out_ref, even_ref, odd_ref, add_ref, sub_ref, turned_ref, high_cos, high_sin):
    half = grid_ref.shape[1] // 2
    rows = grid_ref.shape[0]
    lane = lax.broadcasted_iota(jnp.int32, (1, 768), 1).astype(F32)
    lane = lane - 24.0 * jnp.floor((lane + 0.5) * (1.0 / 24.0))
    size = 1.0 / math.sqrt(2 * half)
    for at, table_ref, first in ((0, even_ref, 0.0), (1, odd_ref, 4.0)):
        valid = (lane >= first) & (lane < first + 20.0)
        fill_table(
            waves_ref[at : at + 1, :],
            jnp.where(lane >= first + 10.0, half / 2.0, 0.0),
            jnp.where(valid, size, 0.0),
            high_cos,
            high_sin,
            table_ref,
            2 * half,
        )

    def fold(k, carry):
        part = pl.ds(pl.multiple_of(k * 64, 64), 64)
        first = grid_ref[part, :half].astype(F32)
        second = grid_ref[part, half:].astype(F32)
        add_ref[part, :] = (first + second).astype(BF16)
        sub_ref[part, :] = (first - second).astype(BF16)
        return carry

    lax.fori_loop(0, rows // 64, fold, 0)
    same = identity(128)

    def block(k, carry):
        results = []
        for table_ref, folded_ref in ((even_ref, add_ref), (odd_ref, sub_ref)):
            for t in range(3):
                columns = pl.ds(pl.multiple_of(k * 384 + 128 * t, 128), 128)
                turned_ref[128 * t : 128 * t + 128, :] = lax.dot_general(
                    same, table_ref[:, columns], NT, preferred_element_type=F32
                ).astype(BF16)
            results.append(
                lax.dot_general(turned_ref[...], folded_ref[...], NT, preferred_element_type=F32)
            )
        even, odd = results
        for d in range(16):
            one = even[24 * d : 24 * d + 24]
            two = odd[24 * d : 24 * d + 24]
            value = jnp.concatenate([one[:16], one[16:] + two[:8], two[8:]], axis=0)
            out_ref[k * 16 + d, :, :rows] = value.astype(BF16)
        return carry

    lax.fori_loop(0, out_ref.shape[0] // 16, block, 0)


def pack_kernel(block_ref, low_ref, high_ref, last_ref):
    q = pl.program_id(0)
    value = block_ref[0]
    lane = lax.broadcasted_iota(jnp.int32, (160, 128), 1)
    last = jnp.where(lane == 0, value[:, 640:].astype(F32), 0.0)
    last = pltpu.roll(last, q, 1)

    @pl.when(q == 0)
    def _():
        last_ref[...] = last

    @pl.when(q > 0)
    def _():
        last_ref[...] += last

    @pl.when(q < 5)
    def _():
        low_ref[pl.ds(pl.multiple_of(q * 160, 160), 160), :] = value[:, :640]

    @pl.when(q >= 5)
    def _():
        high_ref[pl.ds(pl.multiple_of(q * 160 - 800, 160), 160), :] = value[:, :640]

    @pl.when(q == 9)
    def _():
        for t in range(5):
            low_ref[800:832, 128 * t : 128 * t + 128] = last_ref[32 * t : 32 * t + 32, :].astype(BF16)


def lanes_kernel(wire_ref, out_ref, north_ref, south_ref):
    fields = north_ref.shape[1] // 40
    lane = lax.broadcasted_iota(jnp.int32, (40, 128), 1)

    def field(f, carry):
        base = pl.multiple_of(jnp.minimum(f * 40 // 128, 6) * 128, 128)
        offset = f * 40 - base
        rows = pl.ds(pl.multiple_of(f * 40, 8), 40)
        for half, target in ((0, north_ref), (16, south_ref)):
            for x in range(4):
                low = None
                for k in range(4):
                    window = wire_ref[half + 4 * x + k, :, pl.ds(base, 256)]
                    shift = lax.rem(40 * k - offset + 256, 128)
                    first = pltpu.roll(window[:, :128], shift, 1)
                    second = pltpu.roll(window[:, 128:], shift, 1)
                    piece = jnp.where(lane + (offset - 40 * k) >= 128, second, first)
                    low = piece if low is None else jnp.where(lane >= 40 * k, piece, low)
                high = jnp.where(lane + (offset + 8) >= 128, second, first)
                high = jnp.where(lane < 32, high, jnp.zeros_like(high))
                target[2 * x, rows, :] = low.astype(F32)
                target[2 * x + 1, rows, :] = high.astype(F32)
        return carry

    lax.fori_loop(0, fields, field, 0)

    across = lax.broadcasted_iota(jnp.int32, (256, 256), 0)
    along = lax.broadcasted_iota(jnp.int32, (256, 256), 1)
    mirror = jnp.where(across + along == 159, 1.0, 0.0).astype(BF16)

    def fold(k, carry):
        rows = pl.ds(pl.multiple_of(k * 96, 96), 96)
        south = [
            lax.dot_general(
                jnp.concatenate(
                    [south_ref[6 - 2 * x, rows, :], south_ref[7 - 2 * x, rows, :]], axis=1
                ).astype(BF16),
                mirror,
                NN,
                preferred_element_type=F32,
            )
            for x in range(4)
        ]
        for t in range(8):
            second = south[t // 2][:, t % 2 * 128 : t % 2 * 128 + 128]
            first = north_ref[t, rows, :]
            north_ref[t, rows, :] = first + second
            south_ref[t, rows, :] = first - second
        return carry

    lax.fori_loop(0, north_ref.shape[1] // 96, fold, 0)

    def slot(q, carry):
        for x in range(4):
            for t in range(2):
                parts = [
                    source[2 * x + t, pl.ds(g * 10 + q, fields, stride=40), :]
                    for source in (north_ref, south_ref)
                    for g in range(4)
                ]
                part = jnp.concatenate(parts, axis=0).astype(BF16)
                if t:
                    out_ref[q, x, :, 128:] = part[:, :32]
                else:
                    out_ref[q, x, :, :128] = part
        return carry

    lax.fori_loop(0, out_ref.shape[0], slot, 0)


def turn_tables_kernel(one_ref, two_ref, three_ref, out_one, out_two, out_three, *picks):
    levels = ((one_ref, out_one, 4), (two_ref, out_two, 2), (three_ref, out_three, 1))

    @pl.when(pl.program_id(0) == 0)
    def _():
        for pick_ref, (source, _, groups) in zip(picks, levels):
            size = source.shape[1]
            row = lax.broadcasted_iota(jnp.int32, (size, size), 0)
            column = lax.broadcasted_iota(jnp.int32, (size, size), 1)
            b = row // (16 * groups)
            a = (row // 16) % groups
            place = (row % 16) * (5 * groups) + 5 * a + b
            pick_ref[...] = jnp.where(place == column, 1.0, 0.0).astype(BF16)

    for pick_ref, (source, target, _) in zip(picks, levels):
        target[0] = lax.dot_general(
            pick_ref[...], source[0], NT, preferred_element_type=F32
        ).astype(BF16)


def slot_kernel(
    first_slot,
    info_ref,
    waves_ref,
    own_ref,
    left_ref,
    right_ref,
    far_ref,
    own_last,
    left_last,
    right_last,
    far_last,
    one_ref,
    two_ref,
    three_ref,
    spectrum_ref,
    wire_ref,
    pack_ref,
):
    q = pl.program_id(0)
    slot = q + first_slot
    x = info_ref[0]
    p = info_ref[1 + slot]

    @pl.when(q == 0)
    def _():
        for row in (70, 71):
            pack_ref[pl.ds(row, 32, stride=72), :] = jnp.zeros((32, 128), F32)

    total = None
    for step, block_ref, last_ref in (
        (0, own_ref, own_last),
        (3, left_ref, left_last),
        (1, right_ref, right_last),
        (2, far_ref, far_last),
    ):
        last = jnp.concatenate([last_ref[:, 128 * t : 128 * t + 128] for t in range(5)], axis=0)
        block = jnp.concatenate([block_ref[...], last], axis=1)
        term = lax.dot_general(
            waves_ref[0, (x + step) % 4], block, NN, preferred_element_type=F32
        )
        total = term if total is None else total + term
    total = jnp.concatenate(
        [total[:, :640], pltpu.roll(total[:, 640:], lax.rem(128 - slot, 128), 1)], axis=1
    )
    rank = lax.broadcasted_iota(jnp.int32, (48, 768), 1)
    even_pair = p % 2 == 0
    sym = rank < 321
    place = jnp.where(sym, rank, rank - 321)
    bound = jnp.where(sym, (641 - p) // 2, (640 - p) // 2)
    first = (place < bound) == even_pair
    chosen = jnp.where(
        sym,
        jnp.where(first, total[0:48], total[48:96]),
        jnp.where(first, total[96:144], total[144:192]),
    ).astype(BF16)
    spectrum_ref[0] = chosen[:, :641]
    rows = chosen.astype(F32)
    group = 0
    for level, table_ref, count in ((0, one_ref, 4), (1, two_ref, 2), (2, three_ref, 1)):
        size = table_ref.shape[1]
        half = size // 2
        limit = info_ref[11 + level]
        lane = lax.broadcasted_iota(jnp.int32, (48, size), 1)
        is_sym = lane < half
        later = pltpu.roll(rows, 768 - 321 + half, 1)[:, :size]
        order = p + jnp.where(is_sym, 2 * lane, 2 * (lane - half) + 1)
        kept = jnp.where(order <= limit, jnp.where(is_sym, rows[:, :size], later), 0.0)
        both = jnp.concatenate(
            [kept, jnp.where(is_sym, kept, -kept), jnp.zeros((32, size), F32)], axis=0
        ).astype(BF16)
        value = lax.dot_general(table_ref[0], both, NT, preferred_element_type=F32)
        many = 16 * count
        lane = lax.broadcasted_iota(jnp.int32, (many, 128), 1)
        for sign in range(2):
            for c in range(2):
                packed = jnp.zeros((many, 128), F32)
                for b in range(5):
                    part = value[many * b : many * b + many]
                    move = 24 * (b - 2 * sign - c) % 128
                    if move:
                        part = pltpu.roll(part, move, 1)
                    packed = jnp.where((lane >= 24 * b) & (lane < 24 * b + 24), part, packed)
                for a in range(count):
                    start = sign * 16 * 72 + 10 * (group + a) + 5 * c + q
                    pack_ref[pl.ds(start, 16, stride=72), :] = packed[16 * a : 16 * a + 16]
        group += count

    @pl.when(q == pl.num_programs(0) - 1)
    def _():
        for d in range(16):
            wire_ref[d] = pack_ref[72 * d : 72 * d + 72, :].astype(BF16)
            wire_ref[31 - d] = pack_ref[72 * (16 + d) : 72 * (17 + d), :].astype(BF16)


def inverse_table_kernel(waves_ref, one_ref, two_ref, three_ref, high_cos, high_sin):
    wave = waves_ref[0:1, :]
    lane = lax.broadcasted_iota(jnp.int32, (1, 1024), 1) & 15
    weight = jnp.where(lane < 10, jnp.where(wave == 0.0, 1.0, 2.0), 0.0)
    for table_ref in (one_ref, two_ref, three_ref):
        period = table_ref.shape[0]
        shift = jnp.where(lane >= 5, period / 4.0, 0.0)
        scale = weight * (1.0 / math.sqrt(period))
        fill_table(wave, shift, scale, high_cos, high_sin, table_ref, period)


def inverse_kernel(
    info_ref, low_ref, high_ref, one_ref, two_ref, three_ref, out_one, out_two, out_three
):
    late_half = info_ref[0]
    same = identity(128)

    def lines(group):
        start = 10 * group // 8 * 8
        parts = []
        for wire_ref in (low_ref, high_ref):
            part = wire_ref[:, start : start + 16, :].astype(F32)
            if 10 * group > start:
                part = pltpu.roll(part, 16 - (10 * group - start), 1)
            parts.append(part)
        part = jnp.concatenate(parts, axis=1)
        part = part.reshape(part.shape[0] * 32, 128).astype(BF16)
        return lax.dot_general(same, part, NT, preferred_element_type=F32).astype(BF16)

    for target, table, group, count in (
        (out_one, one_ref, 0, 4),
        (out_two, two_ref, 4, 2),
        (out_three, three_ref, 6, 1),
    ):
        left = [lines(group + a) for a in range(count)]
        left = jnp.concatenate(left, axis=0) if count > 1 else left[0]
        value = lax.dot_general(left, table[...], NT, preferred_element_type=F32)
        last = target.shape[0] - 1
        for a in range(count):
            for b in range(5):
                row = 5 * a + b
                row = jnp.where(late_half == 1, last - row, row)
                target[row] = value[128 * a + 24 * b : 128 * a + 24 * b + 24]


def call(kernel, out_shape, limit, **kw):
    return pl.pallas_call(
        kernel,
        out_shape=out_shape,
        compiler_params=pltpu.CompilerParams(vmem_limit_bytes=limit * 1024 * 1024),
        **kw,
    )


def on_device(grid_fields, assign, limits, legendre, synth_one, synth_two, synth_three):
    fields, rows, lon = grid_fields.shape
    lat_at = lax.axis_index("lat")
    fld_at = lax.axis_index("fld")
    vmem = pl.BlockSpec(memory_space=pltpu.VMEM)

    own = jnp.transpose(legendre, (0, 2, 1))
    low, high = call(
        pack_kernel,
        [jax.ShapeDtypeStruct((832, 640), BF16), jax.ShapeDtypeStruct((800, 640), BF16)],
        8,
        grid=(10,),
        in_specs=[pl.BlockSpec((1, 160, 641), lambda q: (q, 0, 0))],
        out_specs=[whole((832, 640)), whole((800, 640))],
        scratch_shapes=[pltpu.VMEM((160, 128), F32)],
        name="pack",
    )(own)
    right = [(k, (k + 1) % 4) for k in range(4)]
    left = [(k, (k + 3) % 4) for k in range(4)]
    low_left = lax.ppermute(low, "fld", right)
    high_right = lax.ppermute(high, "fld", left)
    low_right = lax.ppermute(low, "fld", left)
    high_left = lax.ppermute(high, "fld", right)
    low_far = lax.ppermute(low_left, "fld", right)
    high_far = lax.ppermute(high_right, "fld", left)

    pairs = assign.reshape(32, 10)
    even = jnp.where(pairs % 2 == 0, pairs, 639 - pairs).astype(F32)
    odd = 639.0 - even
    spare = jnp.zeros((32, 4), F32)
    forward_waves = jnp.stack(
        [
            jnp.concatenate([even, even, spare], axis=1),
            jnp.concatenate([spare, odd, odd], axis=1),
        ]
    ).reshape(2, 768)
    wire = call(
        dft_kernel,
        jax.ShapeDtypeStruct((32, 40, 1024), BF16),
        32,
        in_specs=[vmem, vmem],
        out_specs=vmem,
        scratch_shapes=[
            pltpu.VMEM((lon // 2, 768), BF16),
            pltpu.VMEM((lon // 2, 768), BF16),
            pltpu.VMEM((fields * rows, lon // 2), BF16),
            pltpu.VMEM((fields * rows, lon // 2), BF16),
            pltpu.VMEM((384, lon // 2), BF16),
            pltpu.VMEM((80, 768), F32),
            pltpu.VMEM((80, 768), F32),
        ],
        name="dft",
    )(forward_waves, grid_fields.reshape(fields * rows, lon))
    assign_after, synth_one, synth_two, synth_three, wire = lax.optimization_barrier(
        (assign, synth_one, synth_two, synth_three, wire)
    )
    wire = lax.all_to_all(wire, "lat", split_axis=0, concat_axis=0, tiled=True)

    synths = (synth_one, synth_two, synth_three)
    slot_block = [pl.BlockSpec((1,) + t.shape[1:], lambda q: (q, 0, 0)) for t in synths]
    turned = call(
        turn_tables_kernel,
        [jax.ShapeDtypeStruct(t.shape, BF16) for t in synths],
        8,
        grid=(10,),
        in_specs=slot_block,
        out_specs=slot_block,
        scratch_shapes=[pltpu.VMEM(t.shape[1:], BF16) for t in synths],
        name="turn_tables",
    )(*synths)

    plain = assign_after.reshape(32, 10).astype(F32)
    spare = jnp.zeros((32, 6), F32)
    one, two = plain[:, :5], plain[:, 5:]
    inverse_waves = jnp.concatenate([one, one, spare, two, two, spare], axis=1).reshape(1, 1024)
    tables = call(
        inverse_table_kernel,
        [jax.ShapeDtypeStruct((n, 1024), BF16) for n in (1280, 640, 320)],
        12,
        in_specs=[vmem],
        out_specs=[vmem] * 3,
        scratch_shapes=[pltpu.VMEM((80, 1024), F32), pltpu.VMEM((80, 1024), F32)],
        name="inverse_tables",
    )(inverse_waves)

    waves = call(
        lanes_kernel,
        jax.ShapeDtypeStruct((10, 4, 192, 160), BF16),
        22,
        in_specs=[vmem],
        out_specs=vmem,
        scratch_shapes=[
            pltpu.VMEM((8, fields * rows, 128), F32),
            pltpu.VMEM((8, fields * rows, 128), F32),
        ],
        name="lanes",
    )(wire)

    info = jnp.concatenate(
        [fld_at.reshape(1), lax.dynamic_slice_in_dim(assign_after, lat_at * 10, 10), limits]
    )

    def slots(first_slot, blocks):
        lasts = (low, low_left, low_right, low_far)
        return call(
            functools.partial(slot_kernel, first_slot),
            [
                jax.ShapeDtypeStruct((5, 2 * fields, 641), BF16),
                jax.ShapeDtypeStruct((32, 72, 128), BF16),
            ],
            14,
            grid_spec=pltpu.PrefetchScalarGridSpec(
                num_scalar_prefetch=1,
                grid=(5,),
                in_specs=[
                    pl.BlockSpec((1, 4, 192, 160), lambda q, *_: (q + first_slot, 0, 0, 0)),
                ]
                + [pl.BlockSpec((160, 640), lambda q, *_: (q, 0))] * 4
                + [pl.BlockSpec((32, 640), lambda q, *_: (25, 0))] * 4
                + [
                    pl.BlockSpec((1,) + t.shape[1:], lambda q, *_: (q + first_slot, 0, 0))
                    for t in turned
                ],
                out_specs=[
                    pl.BlockSpec((1, 2 * fields, 641), lambda q, *_: (q, 0, 0)),
                    pl.BlockSpec((32, 72, 128), lambda q, *_: (0, 0, 0)),
                ],
                scratch_shapes=[pltpu.VMEM((32 * 72, 128), F32)],
            ),
            name="slots",
        )(info, waves, *blocks, *lasts, *turned)

    first_rows, first_wire = slots(0, (low, low_left, low_right, low_far))
    first_wire = lax.all_to_all(first_wire, "lat", split_axis=0, concat_axis=0, tiled=True)
    later_rows, later_wire = slots(5, (high, high_left, high_right, high_far))
    later_wire = lax.all_to_all(later_wire, "lat", split_axis=0, concat_axis=0, tiled=True)

    late_half = (lat_at >= 16).astype(jnp.int32).reshape(1)
    grids = call(
        inverse_kernel,
        [
            jax.ShapeDtypeStruct((20, fields, 1280), F32),
            jax.ShapeDtypeStruct((10, fields, 640), F32),
            jax.ShapeDtypeStruct((5, fields, 320), F32),
        ],
        24,
        in_specs=[pl.BlockSpec(memory_space=pltpu.SMEM)] + [vmem] * 5,
        out_specs=[vmem] * 3,
        name="inverse",
    )(late_half, first_wire, later_wire, *tables)
    grids = [jnp.transpose(g, (1, 0, 2)) for g in grids]
    spectrum = jnp.concatenate([first_rows, later_rows], axis=0).reshape(10, 2, fields, 641)
    spectrum = jnp.transpose(spectrum, (2, 1, 0, 3))
    return (spectrum, *grids)


def solution(mesh):
    return jax.shard_map(
        on_device,
        mesh=mesh,
        in_specs=(
            P("fld", "lat", None),
            P(),
            P(),
            P("lat", None, "fld"),
            P("lat", None, None),
            P("lat", None, None),
            P("lat", None, None),
        ),
        out_specs=(
            P("fld", None, "lat", None),
            P("fld", "lat", None),
            P("fld", "lat", None),
            P("fld", "lat", None),
        ),
        check_vma=False,
    )
```

time: 152 us -> 146 us (0.961)
  Pallas kernels: 87.3 us -> 51.8 us
  local copies, waits for them, and re-layouts: 13.6 us -> 24.7 us
  waiting for transfers between devices: 21 us -> 30.9 us
  starting transfers between devices: 26.8 us -> 35.6 us
    pallas_call x5 -> x7, Pallas kernels: 80.5 us -> 46.7 us  [the longest x2 15.4 us: slots(): call(functools.partial(slot_kernel, first_slot), [jax.ShapeDtypeStruct((5...]
    unnamed x20 -> x48, local copies, waits for them, and re-layouts: 2.6 us -> 21.9 us
    all_to_all x1 -> x2, starting transfers between devices: 11.2 us -> 19.3 us  [the longest x1 10.5 us: on_device(): lax.all_to_all(first_wire, 'lat', split_axis=0, concat_axis=0, tiled=True)]
    ppermute x4 -> x6, waiting for transfers between devices: 21 us -> 27.1 us  [the longest x1 22.4 us: on_device(): low_left = lax.ppermute(low, 'fld', right)]
    slice x2 -> x1, local copies, waits for them, and re-layouts: 4.8 us -> 0.07 us  [on_device(): one, two = (plain[:, :5], plain[:, 5:])]
    all_to_all x1 -> x2, waiting for transfers between devices: 0.01 us -> 3.82 us  [the longest x1 3.82 us: on_device(): lax.all_to_all(later_wire, 'lat', split_axis=0, concat_axis=0, tiled=True)]
    another operation x14 -> x2, local copies, waits for them, and re-layouts: 3.54 us -> 0.18 us  [on_device(): jnp.stack([jnp.concatenate([even, even, spare], axis=1), jnp.concatenate(...]
    pallas_call x1, Pallas kernels: 6.79 us -> 5.17 us  [on_device(): call(inverse_kernel, [jax.ShapeDtypeStruct((20, fields, 1280), F32), jax....]
  transfers between devices with their start and end apart: 6 -> 9, of which waited for: 2 -> 4; matrix products, arithmetic and copies ran while one was open for 8% -> 2% of each run, Pallas kernels for 42% -> 25%
where the time goes in v1:
time: 146 us; the launch traced here: 145 us
  Pallas kernels  51.8 us (35%)
  starting transfers between devices  35.6 us (24%)
  waiting for transfers between devices  30.9 us (21%)
  local copies, waits for them, and re-layouts  24.7 us (17%)
    ppermute x1, waiting for transfers between devices, on_device(): low_left = lax.ppermute(low, 'fld', right)  22.4 us
    unnamed x48, local copies, waits for them, and re-layouts  21.9 us
    pallas_call x2, Pallas kernels, slots(): call(functools.partial(slot_kernel, first_slot), [jax.ShapeDtypeStruct((5...  15.4 us
    all_to_all x1, starting transfers between devices, on_device(): lax.all_to_all(first_wire, 'lat', split_axis=0, concat_axis=0, tiled=True)  10.5 us
    pallas_call x1, Pallas kernels, on_device(): call(lanes_kernel, jax.ShapeDtypeStruct((10, 4, 192, 160), BF16), 22, in_...  10.3 us
    pallas_call x1, Pallas kernels, on_device(): call(dft_kernel, jax.ShapeDtypeStruct((32, 40, 1024), BF16), 32, in_specs...  10.1 us
    all_to_all x1, starting transfers between devices, on_device(): wire = lax.all_to_all(wire, 'lat', split_axis=0, concat_axis=0, tiled=True)  9.59 us
    all_to_all x1, starting transfers between devices, on_device(): lax.all_to_all(later_wire, 'lat', split_axis=0, concat_axis=0, tiled=True)  8.8 us
  transfers between devices with their start and end apart: 9, of which 4 were waited for; matrix products, arithmetic and copies ran while one was open for 2% of the time, Pallas kernels for 25%

profile of v1, /device:TPU:1, one launch (start us, length us, event | category | flops | bytes accessed | tf_op | source)
XLA Modules:
  0.0 145.2 jit_solution(12511650901511580568)
XLA Ops:
  1.8 2.4 %copy-done.6 = bf16[24,40,2560]{2,1,0:T(8,128)(2,1)S(1)} copy-done((bf16[24,40,2560]{2,1,0:T(8,128)(2,1)S(1)}, bf16[24,40,2560]{2,1,0:T(8,128)(2,1)}, u32[]{:S(2)}) %copy-start.6) | copy-done | bytes 4915224
  4.1 10.1 %dft.1 = bf16[32,40,1024]{2,1,0:T(8,128)(2,1)S(1)} custom-call(f32[2,768]{1,0:T(2,128)S(1)} %pad_maximum_fusion.3.waves_ref, bf16[960,2560]{1,0:T(8,128)(2,1)S(1)} %bitcast.11), custom_call_target="tpu_custom_call" | custom-call | tf_op jit(solution)/shard_map/dft/pallas_call | solution.py:433
  14.3 1.5 %copy-done.2 = bf16[32,40,1024]{2,1,0:T(8,128)(2,1)} copy-done((bf16[32,40,1024]{2,1,0:T(8,128)(2,1)}, bf16[32,40,1024]{2,1,0:T(8,128)(2,1)S(1)}, u32[]{:S(2)}) %copy-start.2) | copy-done | bytes 2621464
  15.7 9.6 %all-to-all-start = ((bf16[32,40,1024]{2,1,0:T(8,128)(2,1)}), bf16[32,40,1024]{2,1,0:T(8,128)(2,1)S(1)}, u32[]{:S(2)}, u32[]{:S(2)}) async-start(bf16[32,40,1024]{2,1,0:T(8,128)(2,1)} %copy-done.2), calls=%async_computation | async-start | bytes 5242880 | tf_op jit(solution)/shard_map/all_to_all | solution.py:453
  25.3 1.7 %copy-done.7 = bf16[10,641,160]{1,2,0:T(8,128)(2,1)S(1)} copy-done((bf16[10,641,160]{1,2,0:T(8,128)(2,1)S(1)}, bf16[10,641,160]{1,2,0:T(8,128)(2,1)}, u32[]{:S(2)}) %copy-start.7) | copy-done | bytes 2051224
  27.0 3.5 %pack.1 = (bf16[832,640]{1,0:T(8,128)(2,1)}, bf16[800,640]{1,0:T(8,128)(2,1)}) custom-call(bf16[10,160,641]{2,1,0:T(8,128)(2,1)S(1)} %bitcast.12), custom_call_target="tpu_custom_call" | custom-call | tf_op jit(solution)/shard_map/pack/pallas_call | solution.py:404
  30.5 1.2 collective-permute-start
  31.7 1.5 %collective-permute-start.4 = (bf16[800,640]{1,0:T(8,128)(2,1)}, bf16[800,640]{1,0:T(8,128)(2,1)}, u32[]{:S(2)}, u32[]{:S(2)}) collective-permute-start(bf16[800,640]{1,0:T(8,128)(2,1)} %get-tuple-element.34.own_ref), channel_id=1, source_target_pairs={{0,3},{1,0},{2,1},{3,2},{4,7},{5,4},{6,5},{7,6},{8,11},{9,8},{10,9... | collective-permute-start | bytes 3072008 | tf_op jit(solution)/shard_map/ppermute | solution.py:417
  33.2 1.3 collective-permute-start.1
  34.5 22.4 %collective-permute-done.left_ref.left_last = bf16[832,640]{1,0:T(8,128)(2,1)} collective-permute-done((bf16[832,640]{1,0:T(8,128)(2,1)}, bf16[832,640]{1,0:T(8,128)(2,1)}, u32[]{:S(2)}, u32[]{:S(2)}) %collective-permute-start) | collective-permute-done | bytes 1064992 | tf_op jit(solution)/shard_map/ppermute | solution.py:416
  56.9 1.2 collective-permute-start.3
  58.1 1.5 %collective-permute-start.5 = (bf16[800,640]{1,0:T(8,128)(2,1)}, bf16[800,640]{1,0:T(8,128)(2,1)}, u32[]{:S(2)}, u32[]{:S(2)}) collective-permute-start(bf16[800,640]{1,0:T(8,128)(2,1)} %collective-permute-done.4.right_ref), channel_id=1, source_target_pairs={{0,3},{1,0},{2,1},{3,2},{4,7},{5,4},{6,5},{7,6},{8,11},{9,8},{10,9... | collective-permute-start | bytes 3072008 | tf_op jit(solution)/shard_map/ppermute | solution.py:421
  59.7 1.7 %copy-done.8 = bf16[10,320,320]{2,1,0:T(8,128)(2,1)S(1)} copy-done((bf16[10,320,320]{2,1,0:T(8,128)(2,1)S(1)}, bf16[10,320,320]{2,1,0:T(8,128)(2,1)}, u32[]{:S(2)}) %copy-start.8) | copy-done | bytes 2048024
  61.4 1.1 copy-done.11
  63.4 3.8 %turn_tables.1 = (bf16[10,320,320]{2,1,0:T(8,128)(2,1)S(1)}, bf16[10,160,160]{2,1,0:T(8,128)(2,1)S(1)}, bf16[10,80,80]{2,1,0:T(8,128)(2,1)S(1)}) custom-call(bf16[10,320,320]{2,1,0:T(8,128)(2,1)S(1)} %copy-done.8, bf16[10,160,160]{2,1,0:T(8,128)(2,1)S(1)} %copy-done.11, bf16[10,80,80]{2,1,0:T(8,128)(2,1)S(1)} %copy-done.21), custom_call_target="tpu_custom_call" | custom-call | tf_op jit(solution)/shard_map/turn_tables/pallas_call | solution.py:457
  67.2 1.4 copy-done.3
  69.4 10.3 %lanes.1.waves_ref = bf16[10,4,192,160]{3,2,1,0:T(8,128)(2,1)S(1)} custom-call(bf16[32,40,1024]{2,1,0:T(8,128)(2,1)S(1)} %all-to-all-done.wire_ref), custom_call_target="tpu_custom_call" | custom-call | tf_op jit(solution)/shard_map/lanes/pallas_call | solution.py:482
  79.8 2.6 %collective-permute-done.2.far_ref.far_last = bf16[832,640]{1,0:T(8,128)(2,1)} collective-permute-done((bf16[832,640]{1,0:T(8,128)(2,1)}, bf16[832,640]{1,0:T(8,128)(2,1)}, u32[]{:S(2)}, u32[]{:S(2)}) %collective-permute-start.2) | collective-permute-done | bytes 1064992 | tf_op jit(solution)/shard_map/ppermute | solution.py:420
  82.4 7.8 %slots.2 = (bf16[5,48,641]{2,1,0:T(8,128)(2,1)S(1)}, bf16[32,72,128]{2,1,0:T(8,128)(2,1)S(1)}) custom-call(s32[14]{0:T(128)S(1)} %pad_add_fusion.info_ref, bf16[10,4,192,160]{3,2,1,0:T(8,128)(2,1)S(1)} %lanes.1.waves_ref, bf16[832,640]{1,0:T(8,128)(2,1)} %get-tuple-element.26.own_ref.own_last, bf16[832,640]{1,0:T(8,128)(2,1)} %collective-permute-done.left_ref.left_last, ...), custom_call_target="tpu_custom_call" | custom-call | tf_op jit(solution)/shard_map/slots/pallas_call | solution.py:501
  91.8 10.5 %all-to-all-start.1 = ((bf16[32,72,128]{2,1,0:T(8,128)(2,1)}), bf16[32,72,128]{2,1,0:T(8,128)(2,1)}, u32[]{:S(2)}, u32[]{:S(2)}) async-start(bf16[32,72,128]{2,1,0:T(8,128)(2,1)} %copy-done.18), calls=%async_computation.1 | async-start | bytes 1179648 | tf_op jit(solution)/shard_map/all_to_all | solution.py:530
  102.3 2.0 %collective-permute-done.3.left_ref = bf16[800,640]{1,0:T(8,128)(2,1)} collective-permute-done((bf16[800,640]{1,0:T(8,128)(2,1)}, bf16[800,640]{1,0:T(8,128)(2,1)}, u32[]{:S(2)}, u32[]{:S(2)}) %collective-permute-start.3) | collective-permute-done | bytes 1024032 | tf_op jit(solution)/shard_map/ppermute | solution.py:419
  104.4 2.1 %copy-done.1 = bf16[10,4,192,160]{3,2,1,0:T(8,128)(2,1)S(1)} copy-done((bf16[10,4,192,160]{3,2,1,0:T(8,128)(2,1)S(1)}, bf16[10,4,192,160]{3,2,1,0:T(8,128)(2,1)}, u32[]{:S(2)}) %copy-start.1) | copy-done | bytes 2457624
  107.4 7.6 %slots.3 = (bf16[5,48,641]{2,1,0:T(8,128)(2,1)S(1)}, bf16[32,72,128]{2,1,0:T(8,128)(2,1)S(1)}) custom-call(s32[14]{0:T(128)S(1)} %pad_add_fusion.info_ref, bf16[10,4,192,160]{3,2,1,0:T(8,128)(2,1)S(1)} %copy-done.1, bf16[800,640]{1,0:T(8,128)(2,1)} %get-tuple-element.34.own_ref, bf16[800,640]{1,0:T(8,128)(2,1)} %collective-permute-done.3.left_ref, ...), custom_call_target="tpu_custom_call" | custom-call | tf_op jit(solution)/shard_map/slots/pallas_call | solution.py:501
  116.6 8.8 %all-to-all-start.2 = ((bf16[32,72,128]{2,1,0:T(8,128)(2,1)}), bf16[32,72,128]{2,1,0:T(8,128)(2,1)S(1)}, u32[]{:S(2)}, u32[]{:S(2)}) async-start(bf16[32,72,128]{2,1,0:T(8,128)(2,1)} %copy-done.17), calls=%async_computation.2 | async-start | bytes 1179648 | tf_op jit(solution)/shard_map/all_to_all | solution.py:532
  125.8 3.5 %inverse_tables.1 = (bf16[1280,1024]{1,0:T(8,128)(2,1)S(1)}, bf16[640,1024]{1,0:T(8,128)(2,1)S(1)}, bf16[320,1024]{1,0:T(8,128)(2,1)S(1)}) custom-call(f32[1,1024]{1,0:T(1,128)S(1)} %reshape.41.waves_ref), custom_call_target="tpu_custom_call" | custom-call | tf_op jit(solution)/shard_map/inverse_tables/pallas_call | solution.py:472
  129.3 1.0 copy-done.9
  131.2 1.2 pad_maximum_fusion
  132.4 1.4 copy.14
  133.8 3.8 %all-to-all-done.2.high_ref = bf16[32,72,128]{2,1,0:T(8,128)(2,1)S(1)} async-done(((bf16[32,72,128]{2,1,0:T(8,128)(2,1)}), bf16[32,72,128]{2,1,0:T(8,128)(2,1)S(1)}, u32[]{:S(2)}, u32[]{:S(2)}) %all-to-all-start.2) | async-done | bytes 589856 | tf_op jit(solution)/shard_map/all_to_all | solution.py:532
  137.6 1.3 copy-done.10
  139.0 1.1 copy-done.16
  140.0 5.2 %inverse.1 = (f32[20,24,1280]{2,1,0:T(8,128)}, f32[10,24,640]{2,1,0:T(8,128)}, f32[5,24,320]{2,1,0:T(8,128)}) custom-call(s32[1]{0:T(128)} %bitcast.5.info_ref, bf16[32,72,128]{2,1,0:T(8,128)(2,1)} %all-to-all-done.1.low_ref, bf16[32,72,128]{2,1,0:T(8,128)(2,1)S(1)} %all-to-all-done.2.high_ref, bf16[1280,1024]{1,0:T(8,128)(2,1)S(1)} %get-tuple-element.38.one_ref, ...), custom_call_target="tpu_custom_call" | custom-call | tf_op jit(solution)/shard_map/inverse/pallas_call | solution.py:535
  (59 shorter events, 8.1 us)
Async XLA Ops:
  1.7 2.4 %copy-start.6 = (bf16[24,40,2560]{2,1,0:T(8,128)(2,1)S(1)}, bf16[24,40,2560]{2,1,0:T(8,128)(2,1)}, u32[]{:S(2)}) copy-start(bf16[24,40,2560]{2,1,0:T(8,128)(2,1)} %param.7) | copy-start | bytes 14745604
  14.3 1.5 %copy-start.2 = (bf16[32,40,1024]{2,1,0:T(8,128)(2,1)}, bf16[32,40,1024]{2,1,0:T(8,128)(2,1)S(1)}, u32[]{:S(2)}) copy-start(bf16[32,40,1024]{2,1,0:T(8,128)(2,1)S(1)} %dft.1) | copy-start | bytes 7864324
  15.7 53.7 %all-to-all-start = ((bf16[32,40,1024]{2,1,0:T(8,128)(2,1)}), bf16[32,40,1024]{2,1,0:T(8,128)(2,1)S(1)}, u32[]{:S(2)}, u32[]{:S(2)}) async-start(bf16[32,40,1024]{2,1,0:T(8,128)(2,1)} %copy-done.2), calls=%async_computation | async-start | bytes 5242880 | tf_op jit(solution)/shard_map/all_to_all | solution.py:453
  25.3 1.7 %copy-start.7 = (bf16[10,641,160]{1,2,0:T(8,128)(2,1)S(1)}, bf16[10,641,160]{1,2,0:T(8,128)(2,1)}, u32[]{:S(2)}) copy-start(bf16[10,641,160]{1,2,0:T(8,128)(2,1)} %param.10) | copy-start | bytes 6153604
  27.0 32.6 %copy-start.22 = (s32[320]{0:T(512)S(1)}, s32[320]{0:T(512)}, u32[]{:S(2)}) copy-start(s32[320]{0:T(512)} %param.8) | copy-start | bytes 3844
  27.0 42.3 %copy-start.23 = (s32[3]{0:T(128)S(1)}, s32[3]{0:T(128)}, u32[]{:S(2)}) copy-start(s32[3]{0:T(128)} %param.9) | copy-start | bytes 40
  30.5 26.4 %collective-permute-start = (bf16[832,640]{1,0:T(8,128)(2,1)}, bf16[832,640]{1,0:T(8,128)(2,1)}, u32[]{:S(2)}, u32[]{:S(2)}) collective-permute-start(bf16[832,640]{1,0:T(8,128)(2,1)} %get-tuple-element.26.own_ref.own_last), channel_id=1, source_target_pairs={{0,1},{1,2},{2,3},{3,0},{4,5},{5,6},{6,7},{7,4},{8,9},{9,10},{10,1... | collective-permute-start | bytes 3194888 | tf_op jit(solution)/shard_map/ppermute | solution.py:416
  31.7 26.4 %collective-permute-start.4 = (bf16[800,640]{1,0:T(8,128)(2,1)}, bf16[800,640]{1,0:T(8,128)(2,1)}, u32[]{:S(2)}, u32[]{:S(2)}) collective-permute-start(bf16[800,640]{1,0:T(8,128)(2,1)} %get-tuple-element.34.own_ref), channel_id=1, source_target_pairs={{0,3},{1,0},{2,1},{3,2},{4,7},{5,4},{6,5},{7,6},{8,11},{9,8},{10,9... | collective-permute-start | bytes 3072008 | tf_op jit(solution)/shard_map/ppermute | solution.py:417
  33.2 46.6 %collective-permute-start.1 = (bf16[832,640]{1,0:T(8,128)(2,1)}, bf16[832,640]{1,0:T(8,128)(2,1)}, u32[]{:S(2)}, u32[]{:S(2)}) collective-permute-start(bf16[832,640]{1,0:T(8,128)(2,1)} %get-tuple-element.26.own_ref.own_last), channel_id=1, source_target_pairs={{0,3},{1,0},{2,1},{3,2},{4,7},{5,4},{6,5},{7,6},{8,11},{9,8},{10,9... | collective-permute-start | bytes 3194888 | tf_op jit(solution)/shard_map/ppermute | solution.py:418
  56.9 25.5 %collective-permute-start.2 = (bf16[832,640]{1,0:T(8,128)(2,1)}, bf16[832,640]{1,0:T(8,128)(2,1)}, u32[]{:S(2)}, u32[]{:S(2)}) collective-permute-start(bf16[832,640]{1,0:T(8,128)(2,1)} %collective-permute-done.left_ref.left_last), channel_id=1, source_target_pairs={{0,1},{1,2},{2,3},{3,0},{4,5},{5,6},{6,7},{7,4},{8,9},{9,10},{10,1... | collective-permute-start | bytes 3194888 | tf_op jit(solution)/shard_map/ppermute | solution.py:420
  56.9 47.4 %collective-permute-start.3 = (bf16[800,640]{1,0:T(8,128)(2,1)}, bf16[800,640]{1,0:T(8,128)(2,1)}, u32[]{:S(2)}, u32[]{:S(2)}) collective-permute-start(bf16[800,640]{1,0:T(8,128)(2,1)} %get-tuple-element.34.own_ref), channel_id=1, source_target_pairs={{0,1},{1,2},{2,3},{3,0},{4,5},{5,6},{6,7},{7,4},{8,9},{9,10},{10,1... | collective-permute-start | bytes 3072008 | tf_op jit(solution)/shard_map/ppermute | solution.py:419
  58.1 46.2 %collective-permute-start.5 = (bf16[800,640]{1,0:T(8,128)(2,1)}, bf16[800,640]{1,0:T(8,128)(2,1)}, u32[]{:S(2)}, u32[]{:S(2)}) collective-permute-start(bf16[800,640]{1,0:T(8,128)(2,1)} %collective-permute-done.4.right_ref), channel_id=1, source_target_pairs={{0,3},{1,0},{2,1},{3,2},{4,7},{5,4},{6,5},{7,6},{8,11},{9,8},{10,9... | collective-permute-start | bytes 3072008 | tf_op jit(solution)/shard_map/ppermute | solution.py:421
  59.7 1.7 %copy-start.8 = (bf16[10,320,320]{2,1,0:T(8,128)(2,1)S(1)}, bf16[10,320,320]{2,1,0:T(8,128)(2,1)}, u32[]{:S(2)}) copy-start(bf16[10,320,320]{2,1,0:T(8,128)(2,1)} %one_ref) | copy-start | bytes 6144004
  61.4 1.1 copy-start.11
  62.5 0.9 copy-start.21
  67.2 1.4 copy-start.3
  69.4 13.0 %copy-start.4 = (bf16[10,320,320]{2,1,0:T(8,128)(2,1)S(1)}, bf16[10,320,320]{2,1,0:T(8,128)(2,1)}, u32[]{:S(2)}) copy-start(bf16[10,320,320]{2,1,0:T(8,128)(2,1)} %copy-done.3) | copy-start | bytes 6144004
  69.4 13.0 %copy-start.13 = (bf16[10,80,80]{2,1,0:T(8,128)(2,1)S(1)}, bf16[10,80,80]{2,1,0:T(8,128)(2,1)}, u32[]{:S(2)}) copy-start(bf16[10,80,80]{2,1,0:T(8,128)(2,1)} %copy-done.12) | copy-start | bytes 384004
  79.8 10.5 %copy-start = (bf16[10,4,192,160]{3,2,1,0:T(8,128)(2,1)}, bf16[10,4,192,160]{3,2,1,0:T(8,128)(2,1)S(1)}, u32[]{:S(2)}) copy-start(bf16[10,4,192,160]{3,2,1,0:T(8,128)(2,1)S(1)} %lanes.1.waves_ref) | copy-start | bytes 7372804
  82.4 21.9 %copy-start.5 = (bf16[10,320,320]{2,1,0:T(8,128)(2,1)S(1)}, bf16[10,320,320]{2,1,0:T(8,128)(2,1)}, u32[]{:S(2)}) copy-start(bf16[10,320,320]{2,1,0:T(8,128)(2,1)} %copy-done.3) | copy-start | bytes 6144004
  90.2 0.8 copy-start.18
  91.0 0.7 copy-start.19
  91.8 24.8 %all-to-all-start.1 = ((bf16[32,72,128]{2,1,0:T(8,128)(2,1)}), bf16[32,72,128]{2,1,0:T(8,128)(2,1)}, u32[]{:S(2)}, u32[]{:S(2)}) async-start(bf16[32,72,128]{2,1,0:T(8,128)(2,1)} %copy-done.18), calls=%async_computation.1 | async-start | bytes 1179648 | tf_op jit(solution)/shard_map/all_to_all | solution.py:530
  104.4 2.1 %copy-start.1 = (bf16[10,4,192,160]{3,2,1,0:T(8,128)(2,1)S(1)}, bf16[10,4,192,160]{3,2,1,0:T(8,128)(2,1)}, u32[]{:S(2)}) copy-start(bf16[10,4,192,160]{3,2,1,0:T(8,128)(2,1)} %copy-done) | copy-start | bytes 7372804
  106.5 0.9 copy-start.14
  115.0 0.8 copy-start.17
  115.8 0.7 copy-start.20
  116.6 21.1 %all-to-all-start.2 = ((bf16[32,72,128]{2,1,0:T(8,128)(2,1)}), bf16[32,72,128]{2,1,0:T(8,128)(2,1)S(1)}, u32[]{:S(2)}, u32[]{:S(2)}) async-start(bf16[32,72,128]{2,1,0:T(8,128)(2,1)} %copy-done.17), calls=%async_computation.2 | async-start | bytes 1179648 | tf_op jit(solution)/shard_map/all_to_all | solution.py:532
  129.3 1.1 copy-start.9
  130.4 0.8 copy-start.15
  137.6 1.3 copy-start.10
  139.0 1.1 copy-start.16
  (1 other events, 0.7 us)

commit v2 on v1

v2 whole, which is shorter than its diff:
```python
import math

import jax
import jax.numpy as jnp
from jax import lax
from jax.experimental import pallas as pl
from jax.experimental.pallas import tpu as pltpu
from jax.sharding import PartitionSpec as P


F32 = jnp.float32
BF16 = jnp.bfloat16

COS_TERMS = (
    1.0,
    -4.93480110168457,
    4.058694839477539,
    -1.3351584672927856,
    0.23502981662750244,
    -0.025358986109495163,
    0.0015939108561724424,
)
SIN_TERMS = (
    3.141592502593994,
    -5.167698860168457,
    2.5499982833862305,
    -0.5985506176948547,
    0.0807478278875351,
    -0.006089475005865097,
)

NT = (((1,), (1,)), ((), ()))
NN = (((1,), (0,)), ((), ()))


def whole(shape):
    return pl.BlockSpec(shape, lambda *_: (0,) * len(shape))


def turn(count, period):
    left = count - period * jnp.floor(count * (1.0 / period) + 0.5)
    place = left * (2.0 / period)
    square = place * place
    cosine = jnp.full_like(square, COS_TERMS[-1])
    for term in COS_TERMS[-2::-1]:
        cosine = cosine * square + term
    sine = jnp.full_like(square, SIN_TERMS[-1])
    for term in SIN_TERMS[-2::-1]:
        sine = sine * square + term
    return cosine, sine * place


def fill_table(wave, shift, scale, high_cos, high_sin, table_ref, period):
    count, width = table_ref.shape
    step = 16
    many = count // step
    low = lax.broadcasted_iota(jnp.int32, (step, width), 0).astype(F32)
    low_cos, low_sin = turn(low * wave, period)
    high = lax.broadcasted_iota(jnp.int32, (many, width), 0).astype(F32)
    first, second = turn(high * (wave * float(step)) + shift, period)
    high_cos[:many, :] = first * scale
    high_sin[:many, :] = second * scale

    def body(k, carry):
        value = high_cos[pl.ds(k, 1), :] * low_cos - high_sin[pl.ds(k, 1), :] * low_sin
        table_ref[pl.ds(pl.multiple_of(k * step, step), step), :] = value.astype(BF16)
        return carry

    lax.fori_loop(0, many, body, 0)


def identity(size):
    across = lax.broadcasted_iota(jnp.int32, (size, size), 0)
    along = lax.broadcasted_iota(jnp.int32, (size, size), 1)
    return jnp.where(across == along, 1.0, 0.0).astype(BF16)


def dft_kernel(
    waves_ref,
    grid_hbm,
    wire_hbm,
    grid_ref,
    out_ref,
    even_ref,
    odd_ref,
    add_ref,
    sub_ref,
    turned_ref,
    high_cos,
    high_sin,
    in_sem,
    out_sem,
):
    half = grid_hbm.shape[1] // 2
    rows = grid_hbm.shape[0]
    incoming = pltpu.make_async_copy(grid_hbm, grid_ref, in_sem)
    incoming.start()
    lane = lax.broadcasted_iota(jnp.int32, (1, 768), 1).astype(F32)
    lane = lane - 24.0 * jnp.floor((lane + 0.5) * (1.0 / 24.0))
    size = 1.0 / math.sqrt(2 * half)
    for at, table_ref, first in ((0, even_ref, 0.0), (1, odd_ref, 4.0)):
        valid = (lane >= first) & (lane < first + 20.0)
        fill_table(
            waves_ref[at : at + 1, :],
            jnp.where(lane >= first + 10.0, half / 2.0, 0.0),
            jnp.where(valid, size, 0.0),
            high_cos,
            high_sin,
            table_ref,
            2 * half,
        )
    incoming.wait()

    def fold(k, carry):
        part = pl.ds(pl.multiple_of(k * 64, 64), 64)
        first = grid_ref[part, :half].astype(F32)
        second = grid_ref[part, half:].astype(F32)
        add_ref[part, :] = (first + second).astype(BF16)
        sub_ref[part, :] = (first - second).astype(BF16)
        return carry

    lax.fori_loop(0, rows // 64, fold, 0)
    same = identity(128)
    leaving = []
    for k in range(2):
        results = []
        for table_ref, folded_ref in ((even_ref, add_ref), (odd_ref, sub_ref)):
            for t in range(3):
                columns = slice(k * 384 + 128 * t, k * 384 + 128 * t + 128)
                turned_ref[128 * t : 128 * t + 128, :] = lax.dot_general(
                    same, table_ref[:, columns], NT, preferred_element_type=F32
                ).astype(BF16)
            results.append(
                lax.dot_general(turned_ref[...], folded_ref[...], NT, preferred_element_type=F32)
            )
        even, odd = results
        for d in range(16):
            one = even[24 * d : 24 * d + 24]
            two = odd[24 * d : 24 * d + 24]
            value = jnp.concatenate([one[:16], one[16:] + two[:8], two[8:]], axis=0)
            out_ref[k * 16 + d, :, :rows] = value.astype(BF16)
        part = pl.ds(16 * k, 16)
        leaving.append(pltpu.make_async_copy(out_ref.at[part], wire_hbm.at[part], out_sem.at[k]))
        leaving[-1].start()
    for copy in leaving:
        copy.wait()


def pack_kernel(block_ref, low_ref, high_ref, last_ref):
    step = pl.program_id(0)
    lane = lax.broadcasted_iota(jnp.int32, (160, 128), 1)
    last = jnp.zeros((160, 128), F32)
    for k in range(2):
        q = 2 * step + k
        value = block_ref[k]
        last += pltpu.roll(jnp.where(lane == 0, value[:, 640:].astype(F32), 0.0), q, 1)

        @pl.when(q < 5)
        def _():
            low_ref[pl.ds(pl.multiple_of(q * 160, 160), 160), :] = value[:, :640]

        @pl.when(q >= 5)
        def _():
            high_ref[pl.ds(pl.multiple_of(q * 160 - 800, 160), 160), :] = value[:, :640]

    @pl.when(step == 0)
    def _():
        last_ref[...] = last

    @pl.when(step > 0)
    def _():
        last_ref[...] += last

    @pl.when(step == 4)
    def _():
        for t in range(5):
            low_ref[800:832, 128 * t : 128 * t + 128] = last_ref[32 * t : 32 * t + 32, :].astype(BF16)


def lanes_kernel(wire_ref, out_ref, north_ref, south_ref):
    fields = north_ref.shape[1] // 40
    lane = lax.broadcasted_iota(jnp.int32, (40, 128), 1)

    def field(f, carry):
        base = pl.multiple_of(jnp.minimum(f * 40 // 128, 6) * 128, 128)
        offset = f * 40 - base
        rows = pl.ds(pl.multiple_of(f * 40, 8), 40)
        for half, target in ((0, north_ref), (16, south_ref)):
            rolled = {}
            for t in range(5):
                tile = None
                for k in range(128 * t // 40, min(15, (128 * t + 127) // 40) + 1):
                    if k not in rolled:
                        window = wire_ref[half + k, :, pl.ds(base, 256)]
                        shift = lax.rem(40 * k % 128 - offset + 256, 128)
                        rolled[k] = (
                            pltpu.roll(window[:, :128], shift, 1),
                            pltpu.roll(window[:, 128:], shift, 1),
                        )
                    start = 40 * k - 128 * t
                    piece = jnp.where(lane + (offset - start) >= 128, rolled[k][1], rolled[k][0])
                    tile = piece if tile is None else jnp.where(lane >= start, piece, tile)
                target[t, rows, :] = tile.astype(F32)
        return carry

    lax.fori_loop(0, fields, field, 0)

    across = lax.broadcasted_iota(jnp.int32, (128, 128), 0)
    along = lax.broadcasted_iota(jnp.int32, (128, 128), 1)
    mirror = jnp.where(across + along == 127, 1.0, 0.0).astype(BF16)

    def fold(k, carry):
        rows = pl.ds(pl.multiple_of(k * 96, 96), 96)
        south = [
            lax.dot_general(
                south_ref[4 - t, rows, :].astype(BF16), mirror, NN, preferred_element_type=F32
            )
            for t in range(5)
        ]
        for t in range(5):
            first = north_ref[t, rows, :]
            north_ref[t, rows, :] = first + south[t]
            south_ref[t, rows, :] = first - south[t]
        return carry

    lax.fori_loop(0, north_ref.shape[1] // 96, fold, 0)

    def slot(q, carry):
        for t in range(5):
            parts = [
                source[t, pl.ds(g * 10 + q, fields, stride=40), :]
                for source in (north_ref, south_ref)
                for g in range(4)
            ]
            out_ref[q, :, 128 * t : 128 * t + 128] = jnp.concatenate(parts, axis=0).astype(BF16)
        return carry

    lax.fori_loop(0, out_ref.shape[0], slot, 0)


def turn_tables_kernel(one_ref, two_ref, three_ref, out_one, out_two, out_three, *picks):
    levels = ((one_ref, out_one, 4), (two_ref, out_two, 2), (three_ref, out_three, 1))

    @pl.when(pl.program_id(0) == 0)
    def _():
        for pick_ref, (source, _, groups) in zip(picks, levels):
            size = source.shape[1]
            row = lax.broadcasted_iota(jnp.int32, (size, size), 0)
            column = lax.broadcasted_iota(jnp.int32, (size, size), 1)
            b = row // (16 * groups)
            a = (row // 16) % groups
            place = (row % 16) * (5 * groups) + 5 * a + b
            pick_ref[...] = jnp.where(place == column, 1.0, 0.0).astype(BF16)

    for pick_ref, (source, target, _) in zip(picks, levels):
        target[0] = lax.dot_general(
            pick_ref[...], source[0], NT, preferred_element_type=F32
        ).astype(BF16)


def slot_kernel(
    info_ref,
    waves_ref,
    own_low,
    left_low,
    right_low,
    far_low,
    own_high,
    left_high,
    right_high,
    far_high,
    one_ref,
    two_ref,
    three_ref,
    spectrum_hbm,
    wire_hbm,
    spectrum_ref,
    block_ref,
    last_ref,
    pack_ref,
    wire_ref,
    spectrum_sem,
    block_sem,
    last_sem,
    wire_sem,
):
    slot = pl.program_id(0)
    x = info_ref[0]
    p = info_ref[1 + slot]
    lows = (own_low, right_low, far_low, left_low)
    highs = (own_high, right_high, far_high, left_high)

    def copies(sources, q, first):
        out = []
        for step, source in enumerate(sources):
            place = pl.multiple_of(((x + step) % 4) * 160, 160)
            out.append(
                pltpu.make_async_copy(
                    source.at[pl.ds(pl.multiple_of((q - first) * 160, 160), 160), :],
                    block_ref.at[q % 2, pl.ds(place, 160), pl.ds(0, 640)],
                    block_sem.at[q % 2, step],
                )
            )
        return out

    def fetch(q):
        @pl.when(q < 5)
        def _():
            for copy in copies(lows, q, 0):
                copy.start()

        @pl.when(q >= 5)
        def _():
            for copy in copies(highs, q, 5):
                copy.start()

    @pl.when(slot == 0)
    def _():
        fetch(slot)
        lasts = [
            pltpu.make_async_copy(
                source.at[pl.ds(800, 32), :], last_ref.at[step], last_sem.at[step]
            )
            for step, source in enumerate(lows)
        ]
        for copy in lasts:
            copy.start()
        for row in range(140, 144):
            pack_ref[pl.ds(row, 32, stride=144), :] = jnp.zeros((32, 128), F32)
        for copy in lasts:
            copy.wait()
        for step in range(4):
            value = last_ref[step]
            value = jnp.concatenate([value[:, 128 * t : 128 * t + 128] for t in range(5)], axis=0)
            place = pl.multiple_of(((x + step) % 4) * 160, 160)
            for k in range(2):
                block_ref[k, pl.ds(place, 160), 640:] = value

    @pl.when(slot < 9)
    def _():
        fetch(slot + 1)

    for copy in copies(lows, slot, slot):
        copy.wait()
    total = lax.dot_general(waves_ref[0], block_ref[slot % 2], NN, preferred_element_type=F32)
    total = jnp.concatenate(
        [total[:, :640], pltpu.roll(total[:, 640:], lax.rem(128 - slot, 128), 1)], axis=1
    )
    rank = lax.broadcasted_iota(jnp.int32, (48, 768), 1)
    even_pair = p % 2 == 0
    sym = rank < 321
    place = jnp.where(sym, rank, rank - 321)
    bound = jnp.where(sym, (641 - p) // 2, (640 - p) // 2)
    first = (place < bound) == even_pair
    chosen = jnp.where(
        sym,
        jnp.where(first, total[0:48], total[48:96]),
        jnp.where(first, total[96:144], total[144:192]),
    ).astype(BF16)
    spectrum_ref[slot] = chosen[:, :641]
    pltpu.make_async_copy(
        spectrum_ref.at[slot], spectrum_hbm.at[slot], spectrum_sem.at[slot]
    ).start()
    rows = chosen.astype(F32)
    group = 0
    for level, table_ref, count in ((0, one_ref, 4), (1, two_ref, 2), (2, three_ref, 1)):
        size = table_ref.shape[1]
        half = size // 2
        limit = info_ref[11 + level]
        lane = lax.broadcasted_iota(jnp.int32, (48, size), 1)
        is_sym = lane < half
        later = pltpu.roll(rows, 768 - 321 + half, 1)[:, :size]
        order = p + jnp.where(is_sym, 2 * lane, 2 * (lane - half) + 1)
        kept = jnp.where(order <= limit, jnp.where(is_sym, rows[:, :size], later), 0.0)
        both = jnp.concatenate(
            [kept, jnp.where(is_sym, kept, -kept), jnp.zeros((32, size), F32)], axis=0
        ).astype(BF16)
        value = lax.dot_general(table_ref[0], both, NT, preferred_element_type=F32)
        many = 16 * count
        lane = lax.broadcasted_iota(jnp.int32, (many, 128), 1)
        for sign in range(2):
            for c in range(2):
                packed = jnp.zeros((many, 128), F32)
                for b in range(5):
                    part = value[many * b : many * b + many]
                    move = 24 * (b - 2 * sign - c) % 128
                    if move:
                        part = pltpu.roll(part, move, 1)
                    packed = jnp.where((lane >= 24 * b) & (lane < 24 * b + 24), part, packed)
                for a in range(count):
                    start = sign * 16 * 144 + 20 * (group + a) + 10 * c + slot
                    pack_ref[pl.ds(start, 16, stride=144), :] = packed[16 * a : 16 * a + 16]
        group += count

    @pl.when(slot == pl.num_programs(0) - 1)
    def _():
        for d in range(16):
            wire_ref[d] = pack_ref[144 * d : 144 * d + 144, :].astype(BF16)
            wire_ref[31 - d] = pack_ref[144 * (16 + d) : 144 * (17 + d), :].astype(BF16)
        leaving = pltpu.make_async_copy(wire_ref, wire_hbm, wire_sem)
        leaving.start()
        for k in range(10):
            pltpu.make_async_copy(
                spectrum_ref.at[k], spectrum_hbm.at[k], spectrum_sem.at[k]
            ).wait()
        leaving.wait()


def inverse_table_kernel(waves_ref, table_ref, high_cos, high_sin):
    wave = waves_ref[0:1, :]
    lane = lax.broadcasted_iota(jnp.int32, (1, 768), 1).astype(F32)
    lane = lane - 24.0 * jnp.floor((lane + 0.5) * (1.0 / 24.0))
    weight = jnp.where(lane < 20.0, jnp.where(wave == 0.0, 1.0, 2.0), 0.0)
    first = 0
    for period in (1280, 640, 320):
        shift = jnp.where(lane >= 10.0, period / 4.0, 0.0)
        scale = weight * (1.0 / math.sqrt(period))
        part = table_ref.at[pl.ds(first, period), :]
        fill_table(wave, shift, scale, high_cos, high_sin, part, period)
        first += period


def inverse_kernel(
    info_ref,
    wire_ref,
    table_ref,
    out_one,
    out_two,
    out_three,
    big_ref,
    mid_ref,
    small_ref,
    out_sem,
):
    late_half = info_ref[0]
    same = identity(128)

    def lines(group):
        start = 20 * group // 8 * 8
        part = wire_ref[:, start : start + 24, :].astype(F32)
        if 20 * group > start:
            part = pltpu.roll(part, 24 - (20 * group - start), 1)
        part = part.reshape(part.shape[0] * 24, 128).astype(BF16)
        return lax.dot_general(same, part, NT, preferred_element_type=F32).astype(BF16)

    def place(target, value, count, last):
        for a in range(count):
            for b in range(5):
                row = 5 * a + b
                row = jnp.where(late_half == 1, last - row, row)
                target[row] = value[128 * a + 24 * b : 128 * a + 24 * b + 24]

    leaving = []

    def leave(source, target):
        copy = pltpu.make_async_copy(source, target, out_sem.at[len(leaving)])
        copy.start()
        leaving.append(copy)

    left = [lines(group) for group in range(7)]
    value = lax.dot_general(left[6], table_ref[1920:, :], NT, preferred_element_type=F32)
    place(small_ref, value, 1, 4)
    leave(small_ref, out_three)
    value = lax.dot_general(
        jnp.concatenate(left[4:6], axis=0),
        table_ref[1280:1920, :],
        NT,
        preferred_element_type=F32,
    )
    place(mid_ref, value, 2, 9)
    leave(mid_ref, out_two)
    left = jnp.concatenate(left[:4], axis=0)
    for n in range(5):
        columns = slice(256 * n, 256 * n + 256)
        value = lax.dot_general(left, table_ref[columns, :], NT, preferred_element_type=F32)
        place(big_ref.at[n], value, 4, 19)
        leave(big_ref.at[n], out_one.at[:, :, pl.ds(256 * n, 256)])
    for copy in leaving:
        copy.wait()


def call(kernel, out_shape, limit, **kw):
    return pl.pallas_call(
        kernel,
        out_shape=out_shape,
        compiler_params=pltpu.CompilerParams(vmem_limit_bytes=limit * 1024 * 1024),
        **kw,
    )


def on_device(grid_fields, assign, limits, legendre, synth_one, synth_two, synth_three):
    fields, rows, lon = grid_fields.shape
    lat_at = lax.axis_index("lat")
    fld_at = lax.axis_index("fld")
    vmem = pl.BlockSpec(memory_space=pltpu.VMEM)

    hbm = pl.BlockSpec(memory_space=pltpu.HBM)
    own = jnp.transpose(legendre, (0, 2, 1))
    low, high = call(
        pack_kernel,
        [jax.ShapeDtypeStruct((832, 640), BF16), jax.ShapeDtypeStruct((800, 640), BF16)],
        60,
        grid=(5,),
        in_specs=[pl.BlockSpec((2, 160, 641), lambda q: (q, 0, 0))],
        out_specs=[whole((832, 640)), whole((800, 640))],
        scratch_shapes=[pltpu.VMEM((160, 128), F32)],
        name="pack",
    )(own)
    low, high, grid_fields, assign = lax.optimization_barrier((low, high, grid_fields, assign))
    right = [(k, (k + 1) % 4) for k in range(4)]
    left = [(k, (k + 3) % 4) for k in range(4)]
    low_left = lax.ppermute(low, "fld", right)
    high_right = lax.ppermute(high, "fld", left)
    low_right = lax.ppermute(low, "fld", left)
    high_left = lax.ppermute(high, "fld", right)
    low_far = lax.ppermute(low_left, "fld", right)
    high_far = lax.ppermute(high_right, "fld", left)

    pairs = assign.reshape(32, 10)
    even = jnp.where(pairs % 2 == 0, pairs, 639 - pairs).astype(F32)
    odd = 639.0 - even
    spare = jnp.zeros((32, 4), F32)
    forward_waves = jnp.stack(
        [
            jnp.concatenate([even, even, spare], axis=1),
            jnp.concatenate([spare, odd, odd], axis=1),
        ]
    ).reshape(2, 768)
    wire = call(
        dft_kernel,
        jax.ShapeDtypeStruct((32, 40, 1024), BF16),
        60,
        in_specs=[vmem, hbm],
        out_specs=hbm,
        scratch_shapes=[
            pltpu.VMEM((fields * rows, lon), BF16),
            pltpu.VMEM((32, 40, 1024), BF16),
            pltpu.VMEM((lon // 2, 768), BF16),
            pltpu.VMEM((lon // 2, 768), BF16),
            pltpu.VMEM((fields * rows, lon // 2), BF16),
            pltpu.VMEM((fields * rows, lon // 2), BF16),
            pltpu.VMEM((384, lon // 2), BF16),
            pltpu.VMEM((80, 768), F32),
            pltpu.VMEM((80, 768), F32),
            pltpu.SemaphoreType.DMA(()),
            pltpu.SemaphoreType.DMA((2,)),
        ],
        name="dft",
    )(forward_waves, grid_fields.reshape(fields * rows, lon))
    assign_after, synth_one, synth_two, synth_three, wire = lax.optimization_barrier(
        (assign, synth_one, synth_two, synth_three, wire)
    )
    wire = lax.all_to_all(wire, "lat", split_axis=0, concat_axis=0, tiled=True)

    synths = (synth_one, synth_two, synth_three)
    slot_block = [pl.BlockSpec((1,) + t.shape[1:], lambda q: (q, 0, 0)) for t in synths]
    turned = call(
        turn_tables_kernel,
        [jax.ShapeDtypeStruct(t.shape, BF16) for t in synths],
        60,
        grid=(10,),
        in_specs=slot_block,
        out_specs=slot_block,
        scratch_shapes=[pltpu.VMEM(t.shape[1:], BF16) for t in synths],
        name="turn_tables",
    )(*synths)

    plain = assign_after.reshape(32, 10).astype(F32)
    spare = jnp.zeros((32, 4), F32)
    inverse_waves = jnp.concatenate([plain, plain, spare], axis=1).reshape(1, 768)
    table = call(
        inverse_table_kernel,
        jax.ShapeDtypeStruct((2240, 768), BF16),
        12,
        in_specs=[vmem],
        out_specs=vmem,
        scratch_shapes=[pltpu.VMEM((80, 768), F32), pltpu.VMEM((80, 768), F32)],
        name="inverse_tables",
    )(inverse_waves)

    waves = call(
        lanes_kernel,
        jax.ShapeDtypeStruct((10, 192, 640), BF16),
        18,
        in_specs=[vmem],
        out_specs=vmem,
        scratch_shapes=[
            pltpu.VMEM((5, fields * rows, 128), F32),
            pltpu.VMEM((5, fields * rows, 128), F32),
        ],
        name="lanes",
    )(wire)

    info = jnp.concatenate(
        [fld_at.reshape(1), lax.dynamic_slice_in_dim(assign_after, lat_at * 10, 10), limits]
    )
    spectrum, level_wire = call(
        slot_kernel,
        [
            jax.ShapeDtypeStruct((10, 2 * fields, 641), BF16),
            jax.ShapeDtypeStruct((32, 144, 128), BF16),
        ],
        18,
        grid_spec=pltpu.PrefetchScalarGridSpec(
            num_scalar_prefetch=1,
            grid=(10,),
            in_specs=[pl.BlockSpec((1, 192, 640), lambda q, *_: (q, 0, 0))]
            + [hbm] * 8
            + [pl.BlockSpec((1,) + t.shape[1:], lambda q, *_: (q, 0, 0)) for t in turned],
            out_specs=[hbm, hbm],
            scratch_shapes=[
                pltpu.VMEM((10, 2 * fields, 641), BF16),
                pltpu.VMEM((2, 640, 768), BF16),
                pltpu.VMEM((4, 32, 640), BF16),
                pltpu.VMEM((32 * 144, 128), F32),
                pltpu.VMEM((32, 144, 128), BF16),
                pltpu.SemaphoreType.DMA((10,)),
                pltpu.SemaphoreType.DMA((2, 4)),
                pltpu.SemaphoreType.DMA((4,)),
                pltpu.SemaphoreType.DMA(()),
            ],
        ),
        name="slots",
    )(
        info,
        waves,
        low,
        low_left,
        low_right,
        low_far,
        high,
        high_left,
        high_right,
        high_far,
        *turned,
    )
    level_wire = lax.all_to_all(level_wire, "lat", split_axis=0, concat_axis=0, tiled=True)

    late_half = (lat_at >= 16).astype(jnp.int32).reshape(1)
    grids = call(
        inverse_kernel,
        [
            jax.ShapeDtypeStruct((20, fields, 1280), F32),
            jax.ShapeDtypeStruct((10, fields, 640), F32),
            jax.ShapeDtypeStruct((5, fields, 320), F32),
        ],
        24,
        in_specs=[pl.BlockSpec(memory_space=pltpu.SMEM), vmem, vmem],
        out_specs=[hbm] * 3,
        scratch_shapes=[
            pltpu.VMEM((5, 20, fields, 256), F32),
            pltpu.VMEM((10, fields, 640), F32),
            pltpu.VMEM((5, fields, 320), F32),
            pltpu.SemaphoreType.DMA((7,)),
        ],
        name="inverse",
    )(late_half, level_wire, table)
    grids = [jnp.transpose(g, (1, 0, 2)) for g in grids]
    spectrum = jnp.transpose(spectrum.reshape(10, 2, fields, 641), (2, 1, 0, 3))
    return (spectrum, *grids)


def solution(mesh):
    return jax.shard_map(
        on_device,
        mesh=mesh,
        in_specs=(
            P("fld", "lat", None),
            P(),
            P(),
            P("lat", None, "fld"),
            P("lat", None, None),
            P("lat", None, None),
            P("lat", None, None),
        ),
        out_specs=(
            P("fld", None, "lat", None),
            P("fld", "lat", None),
            P("fld", "lat", None),
            P("fld", "lat", None),
        ),
        check_vma=False,
    )
```

time: 146 us -> 153 us (1.048)
  waiting for transfers between devices: 30.9 us -> 61.3 us
  local copies, waits for them, and re-layouts: 24.7 us -> 5.13 us
  starting transfers between devices: 35.6 us -> 25.2 us
  Pallas kernels: 51.8 us -> 58.9 us
    ppermute x1, waiting for transfers between devices: 2.03 us -> 26.3 us  [on_device(): high_left = lax.ppermute(high, 'fld', right)]
    unnamed x48 -> x16, local copies, waits for them, and re-layouts: 21.9 us -> 2.03 us
    all_to_all x2 -> x1, starting transfers between devices: 19.3 us -> 8.84 us  [on_device(): lax.all_to_all(level_wire, 'lat', split_axis=0, concat_axis=0, tiled=True)]
    all_to_all x2 -> x1, waiting for transfers between devices: 3.82 us -> 12.6 us  [on_device(): lax.all_to_all(level_wire, 'lat', split_axis=0, concat_axis=0, tiled=True)]
    pallas_call x1, Pallas kernels: 3.76 us -> 8.72 us  [on_device(): call(turn_tables_kernel, [jax.ShapeDtypeStruct(t.shape, BF16) for t in sy...]
    ppermute x1, waiting for transfers between devices: 2.62 us -> 0.01 us  [on_device(): low_far = lax.ppermute(low_left, 'fld', right)]
    pallas_call x1, Pallas kernels: 3.51 us -> 5.47 us  [on_device(): call(pack_kernel, [jax.ShapeDtypeStruct((832, 640), BF16), jax.ShapeDtype...]
    pallas_call x5 -> x4, Pallas kernels: 39.4 us -> 40.3 us  [the longest x1 16.2 us: on_device(): call(slot_kernel, [jax.ShapeDtypeStruct((10, 2 * fields, 641), BF16), jax...]
  transfers between devices with their start and end apart: 9 -> 8, of which waited for: 4 -> 3; matrix products, arithmetic and copies ran while one was open for 2% -> 2% of each run, Pallas kernels for 25% -> 14%
where the time goes in v2:
time: 153 us; the launch traced here: 152 us
  waiting for transfers between devices  61.3 us (40%)
  Pallas kernels  58.9 us (38%)
  starting transfers between devices  25.2 us (16%)
  local copies, waits for them, and re-layouts  5.13 us (3%)
    ppermute x1, waiting for transfers between devices, on_device(): high_left = lax.ppermute(high, 'fld', right)  26.3 us
    ppermute x1, waiting for transfers between devices, on_device(): low_left = lax.ppermute(low, 'fld', right)  22.4 us
    pallas_call x1, Pallas kernels, on_device(): call(slot_kernel, [jax.ShapeDtypeStruct((10, 2 * fields, 641), BF16), jax...  16.2 us
    all_to_all x1, waiting for transfers between devices, on_device(): lax.all_to_all(level_wire, 'lat', split_axis=0, concat_axis=0, tiled=True)  12.6 us
    pallas_call x1, Pallas kernels, on_device(): call(dft_kernel, jax.ShapeDtypeStruct((32, 40, 1024), BF16), 60, in_specs...  11.6 us
    all_to_all x1, starting transfers between devices, on_device(): wire = lax.all_to_all(wire, 'lat', split_axis=0, concat_axis=0, tiled=True)  9.61 us
    pallas_call x1, Pallas kernels, on_device(): call(lanes_kernel, jax.ShapeDtypeStruct((10, 192, 640), BF16), 18, in_spe...  9.56 us
    all_to_all x1, starting transfers between devices, on_device(): lax.all_to_all(level_wire, 'lat', split_axis=0, concat_axis=0, tiled=True)  8.84 us
  transfers between devices with their start and end apart: 8, of which 3 were waited for; matrix products, arithmetic and copies ran while one was open for 2% of the time, Pallas kernels for 14%

profile of v2, /device:TPU:1, one launch (start us, length us, event | category | flops | bytes accessed | tf_op | source)
XLA Modules:
  0.0 152.4 jit_solution(17398594930422491062)
XLA Ops:
  0.6 5.5 %pack.1 = (bf16[832,640]{1,0:T(8,128)(2,1)}, bf16[800,640]{1,0:T(8,128)(2,1)}) custom-call(bf16[10,160,641]{2,1,0:T(8,128)(2,1)} %bitcast.13), custom_call_target="tpu_custom_call" | custom-call | tf_op jit(solution)/shard_map/pack/pallas_call | solution.py:499
  6.1 0.1 reshape.36
  6.3 0.1 pad_maximum_fusion.1
  6.3 0.1 stack.10
  6.4 0.1 stack.9
  6.5 0.6 pad_maximum_fusion.3.waves_ref
  7.1 11.6 %dft.1 = bf16[32,40,1024]{2,1,0:T(8,128)(2,1)} custom-call(f32[2,768]{1,0:T(2,128)} %pad_maximum_fusion.3.waves_ref, bf16[960,2560]{1,0:T(8,128)(2,1)} %bitcast.12), custom_call_target="tpu_custom_call" | custom-call | tf_op jit(solution)/shard_map/dft/pallas_call | solution.py:529
  18.7 9.6 %all-to-all-start = ((bf16[32,40,1024]{2,1,0:T(8,128)(2,1)}), bf16[32,40,1024]{2,1,0:T(8,128)(2,1)S(1)}, u32[]{:S(2)}, u32[]{:S(2)}) async-start(bf16[32,40,1024]{2,1,0:T(8,128)(2,1)} %dft.1), calls=%async_computation | async-start | bytes 5242880 | tf_op jit(solution)/shard_map/all_to_all | solution.py:553
  28.4 0.0 copy-start.7
  28.4 1.3 collective-permute-start
  29.6 1.5 collective-permute-start.4
  31.1 1.3 collective-permute-start.1
  32.4 22.4 %collective-permute-done.left_low = bf16[832,640]{1,0:T(8,128)(2,1)} collective-permute-done((bf16[832,640]{1,0:T(8,128)(2,1)}, bf16[832,640]{1,0:T(8,128)(2,1)}, u32[]{:S(2)}, u32[]{:S(2)}) %collective-permute-start) | collective-permute-done | bytes 1064992 | tf_op jit(solution)/shard_map/ppermute | solution.py:512
  54.8 1.2 collective-permute-start.3
  56.0 0.0 collective-permute-done.4.right_high
  56.0 1.5 collective-permute-start.5
  57.5 0.1 dynamic_slice.3
  57.6 8.7 %turn_tables.1 = (bf16[10,320,320]{2,1,0:T(8,128)(2,1)}, bf16[10,160,160]{2,1,0:T(8,128)(2,1)}, bf16[10,80,80]{2,1,0:T(8,128)(2,1)}) custom-call(bf16[10,320,320]{2,1,0:T(8,128)(2,1)} %one_ref, bf16[10,160,160]{2,1,0:T(8,128)(2,1)} %two_ref, bf16[10,80,80]{2,1,0:T(8,128)(2,1)} %three_ref), custom_call_target="tpu_custom_call" | custom-call | tf_op jit(solution)/shard_map/turn_tables/pallas_call | solution.py:557
  66.3 0.1 pad_add_fusion.info_ref
  66.4 9.6 %lanes.1.waves_ref = bf16[10,192,640]{2,1,0:T(8,128)(2,1)S(1)} custom-call(bf16[32,40,1024]{2,1,0:T(8,128)(2,1)S(1)} %all-to-all-done.wire_ref), custom_call_target="tpu_custom_call" | custom-call | tf_op jit(solution)/shard_map/lanes/pallas_call | solution.py:581
  76.0 26.3 %collective-permute-done.3.left_high = bf16[800,640]{1,0:T(8,128)(2,1)} collective-permute-done((bf16[800,640]{1,0:T(8,128)(2,1)}, bf16[800,640]{1,0:T(8,128)(2,1)}, u32[]{:S(2)}, u32[]{:S(2)}) %collective-permute-start.3) | collective-permute-done | bytes 1024032 | tf_op jit(solution)/shard_map/ppermute | solution.py:515
  102.3 1.1 copy-done.3
  103.4 16.2 %slots.1 = (bf16[10,48,641]{2,1,0:T(8,128)(2,1)S(1)}, bf16[32,144,128]{2,1,0:T(8,128)(2,1)}) custom-call(s32[14]{0:T(128)S(1)} %pad_add_fusion.info_ref, bf16[10,192,640]{2,1,0:T(8,128)(2,1)S(1)} %lanes.1.waves_ref, bf16[832,640]{1,0:T(8,128)(2,1)S(1)} %copy-done.1, bf16[832,640]{1,0:T(8,128)(2,1)} %collective-permute-done.left_low, ...), custom_call_target="tpu_custom_call" | custom-call | tf_op jit(solution)/shard_map/slots/pallas_call | solution.py:597
  119.7 0.9 copy-done.4
  120.5 8.8 %all-to-all-start.1 = ((bf16[32,144,128]{2,1,0:T(8,128)(2,1)}), bf16[32,144,128]{2,1,0:T(8,128)(2,1)}, u32[]{:S(2)}, u32[]{:S(2)}) async-start(bf16[32,144,128]{2,1,0:T(8,128)(2,1)} %get-tuple-element.38), calls=%async_computation.1 | async-start | bytes 2359296 | tf_op jit(solution)/shard_map/all_to_all | solution.py:637
  129.4 0.1 convert_element_type.12
  129.5 0.1 pad_maximum_fusion
  129.6 0.1 reshape.41.waves_ref
  129.7 2.9 %inverse_tables.1.table_ref = bf16[2240,768]{1,0:T(8,128)(2,1)S(1)} custom-call(f32[1,768]{1,0:T(1,128)S(1)} %reshape.41.waves_ref), custom_call_target="tpu_custom_call" | custom-call | tf_op jit(solution)/shard_map/inverse_tables/pallas_call | solution.py:571
  132.6 2.5 %copy.14 = bf16[10,2,24,641]{3,1,0,2:T(2,128)(2,1)} copy(bf16[10,2,24,641]{3,2,1,0:T(8,128)(2,1)} %bitcast.11) | data formatting | bytes 1230720 | tf_op jit(solution)/shard_map/reshape | solution.py:659
  135.2 12.6 %all-to-all-done.1.wire_ref = bf16[32,144,128]{2,1,0:T(8,128)(2,1)} async-done(((bf16[32,144,128]{2,1,0:T(8,128)(2,1)}), bf16[32,144,128]{2,1,0:T(8,128)(2,1)}, u32[]{:S(2)}, u32[]{:S(2)}) %all-to-all-start.1) | async-done | bytes 1179680 | tf_op jit(solution)/shard_map/all_to_all | solution.py:637
  147.8 4.4 %inverse.1 = (f32[20,24,1280]{2,1,0:T(8,128)}, f32[10,24,640]{2,1,0:T(8,128)}, f32[5,24,320]{2,1,0:T(8,128)}) custom-call(s32[1]{0:T(128)} %bitcast.5.info_ref, bf16[32,144,128]{2,1,0:T(8,128)(2,1)} %all-to-all-done.1.wire_ref, bf16[2240,768]{1,0:T(8,128)(2,1)S(1)} %inverse_tables.1.table_ref), custom_call_target="tpu_custom_call" | custom-call | tf_op jit(solution)/shard_map/inverse/pallas_call | solution.py:640
  (21 shorter events, 0.1 us)
Async XLA Ops:
  0.6 5.5 %copy-start.6 = (s32[320]{0:T(512)S(1)}, s32[320]{0:T(512)}, u32[]{:S(2)}) copy-start(s32[320]{0:T(512)} %param.8) | copy-start | bytes 3844
  18.7 47.6 %all-to-all-start = ((bf16[32,40,1024]{2,1,0:T(8,128)(2,1)}), bf16[32,40,1024]{2,1,0:T(8,128)(2,1)S(1)}, u32[]{:S(2)}, u32[]{:S(2)}) async-start(bf16[32,40,1024]{2,1,0:T(8,128)(2,1)} %dft.1), calls=%async_computation | async-start | bytes 5242880 | tf_op jit(solution)/shard_map/all_to_all | solution.py:553
  28.4 37.9 %copy-start.7 = (s32[3]{0:T(128)S(1)}, s32[3]{0:T(128)}, u32[]{:S(2)}) copy-start(s32[3]{0:T(128)} %param.9) | copy-start | bytes 40
  28.4 26.4 %collective-permute-start = (bf16[832,640]{1,0:T(8,128)(2,1)}, bf16[832,640]{1,0:T(8,128)(2,1)}, u32[]{:S(2)}, u32[]{:S(2)}) collective-permute-start(bf16[832,640]{1,0:T(8,128)(2,1)} %get-tuple-element.29.own_low), channel_id=1, source_target_pairs={{0,1},{1,2},{2,3},{3,0},{4,5},{5,6},{6,7},{7,4},{8,9},{9,10},{10,1... | collective-permute-start | bytes 3194888 | tf_op jit(solution)/shard_map/ppermute | solution.py:512
  29.6 26.4 %collective-permute-start.4 = (bf16[800,640]{1,0:T(8,128)(2,1)}, bf16[800,640]{1,0:T(8,128)(2,1)}, u32[]{:S(2)}, u32[]{:S(2)}) collective-permute-start(bf16[800,640]{1,0:T(8,128)(2,1)} %get-tuple-element.30.own_high), channel_id=1, source_target_pairs={{0,3},{1,0},{2,1},{3,2},{4,7},{5,4},{6,5},{7,6},{8,11},{9,8},{10,9... | collective-permute-start | bytes 3072008 | tf_op jit(solution)/shard_map/ppermute | solution.py:513
  31.1 71.1 %collective-permute-start.1 = (bf16[832,640]{1,0:T(8,128)(2,1)}, bf16[832,640]{1,0:T(8,128)(2,1)}, u32[]{:S(2)}, u32[]{:S(2)}) collective-permute-start(bf16[832,640]{1,0:T(8,128)(2,1)} %get-tuple-element.29.own_low), channel_id=1, source_target_pairs={{0,3},{1,0},{2,1},{3,2},{4,7},{5,4},{6,5},{7,6},{8,11},{9,8},{10,9... | collective-permute-start | bytes 3194888 | tf_op jit(solution)/shard_map/ppermute | solution.py:514
  54.8 47.5 %collective-permute-start.2 = (bf16[832,640]{1,0:T(8,128)(2,1)}, bf16[832,640]{1,0:T(8,128)(2,1)}, u32[]{:S(2)}, u32[]{:S(2)}) collective-permute-start(bf16[832,640]{1,0:T(8,128)(2,1)} %collective-permute-done.left_low), channel_id=1, source_target_pairs={{0,1},{1,2},{2,3},{3,0},{4,5},{5,6},{6,7},{7,4},{8,9},{9,10},{10,1... | collective-permute-start | bytes 3194888 | tf_op jit(solution)/shard_map/ppermute | solution.py:516
  54.8 47.4 %collective-permute-start.3 = (bf16[800,640]{1,0:T(8,128)(2,1)}, bf16[800,640]{1,0:T(8,128)(2,1)}, u32[]{:S(2)}, u32[]{:S(2)}) collective-permute-start(bf16[800,640]{1,0:T(8,128)(2,1)} %get-tuple-element.30.own_high), channel_id=1, source_target_pairs={{0,1},{1,2},{2,3},{3,0},{4,5},{5,6},{6,7},{7,4},{8,9},{9,10},{10,1... | collective-permute-start | bytes 3072008 | tf_op jit(solution)/shard_map/ppermute | solution.py:515
  56.0 46.2 %collective-permute-start.5 = (bf16[800,640]{1,0:T(8,128)(2,1)}, bf16[800,640]{1,0:T(8,128)(2,1)}, u32[]{:S(2)}, u32[]{:S(2)}) collective-permute-start(bf16[800,640]{1,0:T(8,128)(2,1)} %collective-permute-done.4.right_high), channel_id=1, source_target_pairs={{0,3},{1,0},{2,1},{3,2},{4,7},{5,4},{6,5},{7,6},{8,11},{9,8},{10,9... | collective-permute-start | bytes 3072008 | tf_op jit(solution)/shard_map/ppermute | solution.py:517
  66.4 35.9 %copy-start.5 = (bf16[10,80,80]{2,1,0:T(8,128)(2,1)S(1)}, bf16[10,80,80]{2,1,0:T(8,128)(2,1)}, u32[]{:S(2)}) copy-start(bf16[10,80,80]{2,1,0:T(8,128)(2,1)} %get-tuple-element.36.three_ref) | copy-start | bytes 384004
  66.4 35.9 %copy-start = (bf16[10,320,320]{2,1,0:T(8,128)(2,1)S(1)}, bf16[10,320,320]{2,1,0:T(8,128)(2,1)}, u32[]{:S(2)}) copy-start(bf16[10,320,320]{2,1,0:T(8,128)(2,1)} %get-tuple-element.34.one_ref) | copy-start | bytes 6144004
  66.4 35.9 %copy-start.1 = (bf16[832,640]{1,0:T(8,128)(2,1)S(1)}, bf16[832,640]{1,0:T(8,128)(2,1)}, u32[]{:S(2)}) copy-start(bf16[832,640]{1,0:T(8,128)(2,1)} %get-tuple-element.29.own_low) | copy-start | bytes 3194884
  66.4 35.9 %copy-start.2 = (bf16[800,640]{1,0:T(8,128)(2,1)S(1)}, bf16[800,640]{1,0:T(8,128)(2,1)}, u32[]{:S(2)}) copy-start(bf16[800,640]{1,0:T(8,128)(2,1)} %get-tuple-element.30.own_high) | copy-start | bytes 3072004
  102.3 1.1 copy-start.3
  119.7 0.9 copy-start.4
  120.5 27.3 %all-to-all-start.1 = ((bf16[32,144,128]{2,1,0:T(8,128)(2,1)}), bf16[32,144,128]{2,1,0:T(8,128)(2,1)}, u32[]{:S(2)}, u32[]{:S(2)}) async-start(bf16[32,144,128]{2,1,0:T(8,128)(2,1)} %get-tuple-element.38), calls=%async_computation.1 | async-start | bytes 2359296 | tf_op jit(solution)/shard_map/all_to_all | solution.py:637

commit v3 on v2

--- a/solution.py
+++ b/solution.py
@@ -33,10 +33,6 @@
 NN = (((1,), (0,)), ((), ()))
 
 
-def whole(shape):
-    return pl.BlockSpec(shape, lambda *_: (0,) * len(shape))
-
-
 def turn(count, period):
     left = count - period * jnp.floor(count * (1.0 / period) + 0.5)
     place = left * (2.0 / period)
@@ -66,7 +62,7 @@
         table_ref[pl.ds(pl.multiple_of(k * step, step), step), :] = value.astype(BF16)
         return carry
 
-    lax.fori_loop(0, many, body, 0)
+    lax.fori_loop(0, many, body, 0, unroll=4)
 
 
 def identity(size):
@@ -76,6 +72,7 @@
 
 
 def dft_kernel(
+    info_ref,
     waves_ref,
     grid_hbm,
     wire_hbm,
@@ -120,7 +117,13 @@
         return carry
 
     lax.fori_loop(0, rows // 64, fold, 0)
+    add_ref[rows:, :] = jnp.zeros((1024 - rows, half), BF16)
+    sub_ref[rows:, :] = jnp.zeros((1024 - rows, half), BF16)
     same = identity(128)
+    turn_by = info_ref[0]
+    shift = lax.rem(turn_by, 128)
+    tile_shift = lax.div(turn_by, 128)
+    lane = lax.broadcasted_iota(jnp.int32, (40, 128), 1)
     leaving = []
     for k in range(2):
         results = []
@@ -138,7 +141,11 @@
             one = even[24 * d : 24 * d + 24]
             two = odd[24 * d : 24 * d + 24]
             value = jnp.concatenate([one[:16], one[16:] + two[:8], two[8:]], axis=0)
-            out_ref[k * 16 + d, :, :rows] = value.astype(BF16)
+            tiles = [pltpu.roll(value[:, 128 * t : 128 * t + 128], shift, 1) for t in range(8)]
+            for t in range(8):
+                tile = jnp.where(lane < shift, tiles[t - 1], tiles[t])
+                place = pl.multiple_of(lax.rem(tile_shift + t, 8) * 128, 128)
+                out_ref[k * 16 + d, :, pl.ds(place, 128)] = tile.astype(BF16)
         part = pl.ds(16 * k, 16)
         leaving.append(pltpu.make_async_copy(out_ref.at[part], wire_hbm.at[part], out_sem.at[k]))
         leaving[-1].start()
@@ -146,64 +153,61 @@
         copy.wait()
 
 
-def pack_kernel(block_ref, low_ref, high_ref, last_ref):
-    step = pl.program_id(0)
+def pack_kernel(block_hbm, low_hbm, high_hbm, low_ref, high_ref, edge_ref, in_sem, out_sem):
+    edge = pltpu.make_async_copy(block_hbm.at[:, :, pl.ds(640, 1)], edge_ref, in_sem.at[10])
+    edge.start()
+    incoming = []
+    for q in range(10):
+        target = low_ref if q < 5 else high_ref
+        incoming.append(
+            pltpu.make_async_copy(
+                block_hbm.at[q, :, pl.ds(0, 640)],
+                target.at[pl.ds(q % 5 * 160, 160), :],
+                in_sem.at[q],
+            )
+        )
+        incoming[-1].start()
+    edge.wait()
     lane = lax.broadcasted_iota(jnp.int32, (160, 128), 1)
     last = jnp.zeros((160, 128), F32)
-    for k in range(2):
-        q = 2 * step + k
-        value = block_ref[k]
-        last += pltpu.roll(jnp.where(lane == 0, value[:, 640:].astype(F32), 0.0), q, 1)
-
-        @pl.when(q < 5)
-        def _():
-            low_ref[pl.ds(pl.multiple_of(q * 160, 160), 160), :] = value[:, :640]
-
-        @pl.when(q >= 5)
-        def _():
-            high_ref[pl.ds(pl.multiple_of(q * 160 - 800, 160), 160), :] = value[:, :640]
-
-    @pl.when(step == 0)
-    def _():
-        last_ref[...] = last
-
-    @pl.when(step > 0)
-    def _():
-        last_ref[...] += last
-
-    @pl.when(step == 4)
-    def _():
-        for t in range(5):
-            low_ref[800:832, 128 * t : 128 * t + 128] = last_ref[32 * t : 32 * t + 32, :].astype(BF16)
+    for q in range(10):
+        last = jnp.where(lane == q, edge_ref[q].astype(F32), last)
+    for t in range(5):
+        low_ref[800:832, 128 * t : 128 * t + 128] = last[32 * t : 32 * t + 32].astype(BF16)
+    for copy in incoming[:5]:
+        copy.wait()
+    low_out = pltpu.make_async_copy(low_ref, low_hbm, out_sem.at[0])
+    low_out.start()
+    for copy in incoming[5:]:
+        copy.wait()
+    high_out = pltpu.make_async_copy(high_ref, high_hbm, out_sem.at[1])
+    high_out.start()
+    low_out.wait()
+    high_out.wait()
 
 
 def lanes_kernel(wire_ref, out_ref, north_ref, south_ref):
     fields = north_ref.shape[1] // 40
     lane = lax.broadcasted_iota(jnp.int32, (40, 128), 1)
-
-    def field(f, carry):
-        base = pl.multiple_of(jnp.minimum(f * 40 // 128, 6) * 128, 128)
-        offset = f * 40 - base
-        rows = pl.ds(pl.multiple_of(f * 40, 8), 40)
+    for f in range(fields):
+        offset = 40 * f % 128
         for half, target in ((0, north_ref), (16, south_ref)):
-            rolled = {}
+            tiles = []
+            for o in range(6 if offset else 5):
+                at = (40 * f // 128 + o) % 8 * 128
+                first = 128 * o - offset
+                tile = None
+                for k in range(max(first // 40, 0), min((first + 127) // 40, 15) + 1):
+                    piece = wire_ref[half + k, :, at : at + 128]
+                    tile = piece if tile is None else jnp.where(lane >= 40 * k - first, piece, tile)
+                tiles.append(tile.astype(F32))
+            if offset:
+                tiles = [pltpu.roll(tile, 128 - offset, 1) for tile in tiles]
+                tiles = [
+                    jnp.where(lane < 128 - offset, tiles[t], tiles[t + 1]) for t in range(5)
+                ]
             for t in range(5):
-                tile = None
-                for k in range(128 * t // 40, min(15, (128 * t + 127) // 40) + 1):
-                    if k not in rolled:
-                        window = wire_ref[half + k, :, pl.ds(base, 256)]
-                        shift = lax.rem(40 * k % 128 - offset + 256, 128)
-                        rolled[k] = (
-                            pltpu.roll(window[:, :128], shift, 1),
-                            pltpu.roll(window[:, 128:], shift, 1),
-                        )
-                    start = 40 * k - 128 * t
-                    piece = jnp.where(lane + (offset - start) >= 128, rolled[k][1], rolled[k][0])
-                    tile = piece if tile is None else jnp.where(lane >= start, piece, tile)
-                target[t, rows, :] = tile.astype(F32)
-        return carry
-
-    lax.fori_loop(0, fields, field, 0)
+                target[t, 40 * f : 40 * f + 40, :] = tiles[t]
 
     across = lax.broadcasted_iota(jnp.int32, (128, 128), 0)
     along = lax.broadcasted_iota(jnp.int32, (128, 128), 1)
@@ -500,10 +504,15 @@
         pack_kernel,
         [jax.ShapeDtypeStruct((832, 640), BF16), jax.ShapeDtypeStruct((800, 640), BF16)],
         60,
-        grid=(5,),
-        in_specs=[pl.BlockSpec((2, 160, 641), lambda q: (q, 0, 0))],
-        out_specs=[whole((832, 640)), whole((800, 640))],
-        scratch_shapes=[pltpu.VMEM((160, 128), F32)],
+        in_specs=[hbm],
+        out_specs=[hbm, hbm],
+        scratch_shapes=[
+            pltpu.VMEM((832, 640), BF16),
+            pltpu.VMEM((800, 640), BF16),
+            pltpu.VMEM((10, 160, 1), BF16),
+            pltpu.SemaphoreType.DMA((11,)),
+            pltpu.SemaphoreType.DMA((2,)),
+        ],
         name="pack",
     )(own)
     low, high, grid_fields, assign = lax.optimization_barrier((low, high, grid_fields, assign))
@@ -530,15 +539,15 @@
         dft_kernel,
         jax.ShapeDtypeStruct((32, 40, 1024), BF16),
         60,
-        in_specs=[vmem, hbm],
+        in_specs=[pl.BlockSpec(memory_space=pltpu.SMEM), vmem, hbm],
         out_specs=hbm,
         scratch_shapes=[
             pltpu.VMEM((fields * rows, lon), BF16),
             pltpu.VMEM((32, 40, 1024), BF16),
             pltpu.VMEM((lon // 2, 768), BF16),
             pltpu.VMEM((lon // 2, 768), BF16),
-            pltpu.VMEM((fields * rows, lon // 2), BF16),
-            pltpu.VMEM((fields * rows, lon // 2), BF16),
+            pltpu.VMEM((1024, lon // 2), BF16),
+            pltpu.VMEM((1024, lon // 2), BF16),
             pltpu.VMEM((384, lon // 2), BF16),
             pltpu.VMEM((80, 768), F32),
             pltpu.VMEM((80, 768), F32),
@@ -546,7 +555,7 @@
             pltpu.SemaphoreType.DMA((2,)),
         ],
         name="dft",
-    )(forward_waves, grid_fields.reshape(fields * rows, lon))
+    )((lat_at % 16 * 40).reshape(1), forward_waves, grid_fields.reshape(fields * rows, lon))
     assign_after, synth_one, synth_two, synth_three, wire = lax.optimization_barrier(
         (assign, synth_one, synth_two, synth_three, wire)
     )
@@ -600,7 +609,7 @@
             jax.ShapeDtypeStruct((10, 2 * fields, 641), BF16),
             jax.ShapeDtypeStruct((32, 144, 128), BF16),
         ],
-        18,
+        60,
         grid_spec=pltpu.PrefetchScalarGridSpec(
             num_scalar_prefetch=1,
             grid=(10,),

time: 153 us -> 149 us (0.974)
  Pallas kernels: 58.9 us -> 50.1 us
  waiting for transfers between devices: 61.3 us -> 65.4 us
    pallas_call x1, Pallas kernels: 9.56 us -> 4.16 us  [on_device(): call(lanes_kernel, jax.ShapeDtypeStruct((10, 192, 640), BF16), 18, in_spe...]
    ppermute x1, waiting for transfers between devices: 26.3 us -> 29.7 us  [on_device(): high_left = lax.ppermute(high, 'fld', right)]
    pallas_call x1, Pallas kernels: 5.47 us -> 2.86 us  [on_device(): call(pack_kernel, [jax.ShapeDtypeStruct((832, 640), BF16), jax.ShapeDtype...]
  transfers between devices with their start and end apart: 8 -> 8, of which waited for: 3 -> 3; matrix products, arithmetic and copies ran while one was open for 2% -> 2% of each run, Pallas kernels for 14% -> 10%
where the time goes in v3:
time: 149 us; the launch traced here: 148 us
  waiting for transfers between devices  65.4 us (44%)
  Pallas kernels  50.1 us (34%)
  starting transfers between devices  25.3 us (17%)
  local copies, waits for them, and re-layouts  4.54 us (3%)
    ppermute x1, waiting for transfers between devices, on_device(): high_left = lax.ppermute(high, 'fld', right)  29.7 us
    ppermute x1, waiting for transfers between devices, on_device(): low_left = lax.ppermute(low, 'fld', right)  22.4 us
    pallas_call x1, Pallas kernels, on_device(): call(slot_kernel, [jax.ShapeDtypeStruct((10, 2 * fields, 641), BF16), jax...  16.3 us
    all_to_all x1, waiting for transfers between devices, on_device(): lax.all_to_all(level_wire, 'lat', split_axis=0, concat_axis=0, tiled=True)  13.2 us
    pallas_call x1, Pallas kernels, on_device(): call(dft_kernel, jax.ShapeDtypeStruct((32, 40, 1024), BF16), 60, in_specs...  11.3 us
    all_to_all x1, starting transfers between devices, on_device(): wire = lax.all_to_all(wire, 'lat', split_axis=0, concat_axis=0, tiled=True)  9.6 us
    all_to_all x1, starting transfers between devices, on_device(): lax.all_to_all(level_wire, 'lat', split_axis=0, concat_axis=0, tiled=True)  9.03 us
    pallas_call x1, Pallas kernels, on_device(): call(turn_tables_kernel, [jax.ShapeDtypeStruct(t.shape, BF16) for t in sy...  8.74 us
  transfers between devices with their start and end apart: 8, of which 3 were waited for; matrix products, arithmetic and copies ran while one was open for 2% of the time, Pallas kernels for 10%

profile of v3, /device:TPU:1, one launch (start us, length us, event | category | flops | bytes accessed | tf_op | source)
XLA Modules:
  0.0 147.7 jit_solution(5063035197696753997)
XLA Ops:
  0.7 2.9 %pack.1 = (bf16[832,640]{1,0:T(8,128)(2,1)}, bf16[800,640]{1,0:T(8,128)(2,1)}) custom-call(bf16[10,160,641]{2,1,0:T(8,128)(2,1)} %bitcast.13), custom_call_target="tpu_custom_call" | custom-call | tf_op jit(solution)/shard_map/pack/pallas_call | solution.py:503
  3.5 0.1 reshape.40
  3.7 0.1 pad_maximum_fusion.1
  3.8 0.1 stack.10
  3.9 0.1 stack.9
  4.0 0.6 pad_maximum_fusion.3.waves_ref
  4.6 11.3 %dft.1 = bf16[32,40,1024]{2,1,0:T(8,128)(2,1)} custom-call(s32[1]{0:T(128)} %bitcast.2.info_ref, f32[2,768]{1,0:T(2,128)} %pad_maximum_fusion.3.waves_ref, bf16[960,2560]{1,0:T(8,128)(2,1)} %bitcast.12), custom_call_target="tpu_custom_call" | custom-call | tf_op jit(solution)/shard_map/dft/pallas_call | solution.py:538
  15.9 9.6 %all-to-all-start = ((bf16[32,40,1024]{2,1,0:T(8,128)(2,1)}), bf16[32,40,1024]{2,1,0:T(8,128)(2,1)S(1)}, u32[]{:S(2)}, u32[]{:S(2)}) async-start(bf16[32,40,1024]{2,1,0:T(8,128)(2,1)} %dft.1), calls=%async_computation | async-start | bytes 5242880 | tf_op jit(solution)/shard_map/all_to_all | solution.py:562
  25.5 0.0 copy-start.2
  25.5 1.3 collective-permute-start
  26.8 1.5 collective-permute-start.4
  28.2 1.3 collective-permute-start.1
  29.5 22.4 %collective-permute-done.left_low = bf16[832,640]{1,0:T(8,128)(2,1)} collective-permute-done((bf16[832,640]{1,0:T(8,128)(2,1)}, bf16[832,640]{1,0:T(8,128)(2,1)}, u32[]{:S(2)}, u32[]{:S(2)}) %collective-permute-start) | collective-permute-done | bytes 1064992 | tf_op jit(solution)/shard_map/ppermute | solution.py:521
  51.9 0.0 collective-permute-start.2
  51.9 1.2 collective-permute-start.3
  53.1 1.5 %collective-permute-start.5 = (bf16[800,640]{1,0:T(8,128)(2,1)}, bf16[800,640]{1,0:T(8,128)(2,1)}, u32[]{:S(2)}, u32[]{:S(2)}) collective-permute-start(bf16[800,640]{1,0:T(8,128)(2,1)} %collective-permute-done.4.right_high), channel_id=1, source_target_pairs={{0,3},{1,0},{2,1},{3,2},{4,7},{5,4},{6,5},{7,6},{8,11},{9,8},{10,9... | collective-permute-start | bytes 3072008 | tf_op jit(solution)/shard_map/ppermute | solution.py:526
  54.6 0.1 dynamic_slice.3
  54.7 8.7 %turn_tables.1 = (bf16[10,320,320]{2,1,0:T(8,128)(2,1)}, bf16[10,160,160]{2,1,0:T(8,128)(2,1)}, bf16[10,80,80]{2,1,0:T(8,128)(2,1)}) custom-call(bf16[10,320,320]{2,1,0:T(8,128)(2,1)} %one_ref, bf16[10,160,160]{2,1,0:T(8,128)(2,1)} %two_ref, bf16[10,80,80]{2,1,0:T(8,128)(2,1)} %three_ref), custom_call_target="tpu_custom_call" | custom-call | tf_op jit(solution)/shard_map/turn_tables/pallas_call | solution.py:566
  63.4 0.6 pad_add_fusion.info_ref
  64.0 4.2 %lanes.1.waves_ref = bf16[10,192,640]{2,1,0:T(8,128)(2,1)S(1)} custom-call(bf16[32,40,1024]{2,1,0:T(8,128)(2,1)S(1)} %all-to-all-done.wire_ref), custom_call_target="tpu_custom_call" | custom-call | tf_op jit(solution)/shard_map/lanes/pallas_call | solution.py:590
  68.2 0.0 copy-start
  68.2 1.4 copy-done
  69.6 29.7 %collective-permute-done.3.left_high = bf16[800,640]{1,0:T(8,128)(2,1)} collective-permute-done((bf16[800,640]{1,0:T(8,128)(2,1)}, bf16[800,640]{1,0:T(8,128)(2,1)}, u32[]{:S(2)}, u32[]{:S(2)}) %collective-permute-start.3) | collective-permute-done | bytes 1024032 | tf_op jit(solution)/shard_map/ppermute | solution.py:524
  99.4 16.3 %slots.1 = (bf16[10,48,641]{2,1,0:T(8,128)(2,1)}, bf16[32,144,128]{2,1,0:T(8,128)(2,1)}) custom-call(s32[14]{0:T(128)} %pad_add_fusion.info_ref, bf16[10,192,640]{2,1,0:T(8,128)(2,1)} %copy-done, bf16[832,640]{1,0:T(8,128)(2,1)} %get-tuple-element.29.own_low, bf16[832,640]{1,0:T(8,128)(2,1)} %collective-permute-done.left_low, ...), custom_call_target="tpu_custom_call" | custom-call | tf_op jit(solution)/shard_map/slots/pallas_call | solution.py:606
  115.7 9.0 %all-to-all-start.1 = ((bf16[32,144,128]{2,1,0:T(8,128)(2,1)}), bf16[32,144,128]{2,1,0:T(8,128)(2,1)}, u32[]{:S(2)}, u32[]{:S(2)}) async-start(bf16[32,144,128]{2,1,0:T(8,128)(2,1)} %get-tuple-element.38), calls=%async_computation.1 | async-start | bytes 2359296 | tf_op jit(solution)/shard_map/all_to_all | solution.py:646
  124.7 0.1 convert_element_type.12
  124.8 0.1 pad_maximum_fusion
  124.9 0.1 reshape.45.waves_ref
  125.0 2.3 %inverse_tables.1.table_ref = bf16[2240,768]{1,0:T(8,128)(2,1)S(1)} custom-call(f32[1,768]{1,0:T(1,128)S(1)} %reshape.45.waves_ref), custom_call_target="tpu_custom_call" | custom-call | tf_op jit(solution)/shard_map/inverse_tables/pallas_call | solution.py:580
  127.4 2.5 %copy.14 = bf16[10,2,24,641]{3,1,0,2:T(2,128)(2,1)} copy(bf16[10,2,24,641]{3,2,1,0:T(8,128)(2,1)} %bitcast.14) | data formatting | bytes 1230720 | tf_op jit(solution)/shard_map/reshape | solution.py:668
  129.9 13.2 %all-to-all-done.1.wire_ref = bf16[32,144,128]{2,1,0:T(8,128)(2,1)} async-done(((bf16[32,144,128]{2,1,0:T(8,128)(2,1)}), bf16[32,144,128]{2,1,0:T(8,128)(2,1)}, u32[]{:S(2)}, u32[]{:S(2)}) %all-to-all-start.1) | async-done | bytes 1179680 | tf_op jit(solution)/shard_map/all_to_all | solution.py:646
  143.1 4.4 %inverse.1 = (f32[20,24,1280]{2,1,0:T(8,128)}, f32[10,24,640]{2,1,0:T(8,128)}, f32[5,24,320]{2,1,0:T(8,128)}) custom-call(s32[1]{0:T(128)} %bitcast.6.info_ref, bf16[32,144,128]{2,1,0:T(8,128)(2,1)} %all-to-all-done.1.wire_ref, bf16[2240,768]{1,0:T(8,128)(2,1)S(1)} %inverse_tables.1.table_ref), custom_call_target="tpu_custom_call" | custom-call | tf_op jit(solution)/shard_map/inverse/pallas_call | solution.py:649
  (11 shorter events, 0.0 us)
Async XLA Ops:
  0.6 2.9 %copy-start.1 = (s32[320]{0:T(512)S(1)}, s32[320]{0:T(512)}, u32[]{:S(2)}) copy-start(s32[320]{0:T(512)} %param.8) | copy-start | bytes 3844
  15.9 48.2 %all-to-all-start = ((bf16[32,40,1024]{2,1,0:T(8,128)(2,1)}), bf16[32,40,1024]{2,1,0:T(8,128)(2,1)S(1)}, u32[]{:S(2)}, u32[]{:S(2)}) async-start(bf16[32,40,1024]{2,1,0:T(8,128)(2,1)} %dft.1), calls=%async_computation | async-start | bytes 5242880 | tf_op jit(solution)/shard_map/all_to_all | solution.py:562
  25.5 38.0 %copy-start.2 = (s32[3]{0:T(128)S(1)}, s32[3]{0:T(128)}, u32[]{:S(2)}) copy-start(s32[3]{0:T(128)} %param.9) | copy-start | bytes 40
  25.5 26.4 %collective-permute-start = (bf16[832,640]{1,0:T(8,128)(2,1)}, bf16[832,640]{1,0:T(8,128)(2,1)}, u32[]{:S(2)}, u32[]{:S(2)}) collective-permute-start(bf16[832,640]{1,0:T(8,128)(2,1)} %get-tuple-element.29.own_low), channel_id=1, source_target_pairs={{0,1},{1,2},{2,3},{3,0},{4,5},{5,6},{6,7},{7,4},{8,9},{9,10},{10,1... | collective-permute-start | bytes 3194888 | tf_op jit(solution)/shard_map/ppermute | solution.py:521
  26.8 26.4 %collective-permute-start.4 = (bf16[800,640]{1,0:T(8,128)(2,1)}, bf16[800,640]{1,0:T(8,128)(2,1)}, u32[]{:S(2)}, u32[]{:S(2)}) collective-permute-start(bf16[800,640]{1,0:T(8,128)(2,1)} %get-tuple-element.30.own_high), channel_id=1, source_target_pairs={{0,3},{1,0},{2,1},{3,2},{4,7},{5,4},{6,5},{7,6},{8,11},{9,8},{10,9... | collective-permute-start | bytes 3072008 | tf_op jit(solution)/shard_map/ppermute | solution.py:522
  28.2 71.1 %collective-permute-start.1 = (bf16[832,640]{1,0:T(8,128)(2,1)}, bf16[832,640]{1,0:T(8,128)(2,1)}, u32[]{:S(2)}, u32[]{:S(2)}) collective-permute-start(bf16[832,640]{1,0:T(8,128)(2,1)} %get-tuple-element.29.own_low), channel_id=1, source_target_pairs={{0,3},{1,0},{2,1},{3,2},{4,7},{5,4},{6,5},{7,6},{8,11},{9,8},{10,9... | collective-permute-start | bytes 3194888 | tf_op jit(solution)/shard_map/ppermute | solution.py:523
  51.9 47.5 %collective-permute-start.2 = (bf16[832,640]{1,0:T(8,128)(2,1)}, bf16[832,640]{1,0:T(8,128)(2,1)}, u32[]{:S(2)}, u32[]{:S(2)}) collective-permute-start(bf16[832,640]{1,0:T(8,128)(2,1)} %collective-permute-done.left_low), channel_id=1, source_target_pairs={{0,1},{1,2},{2,3},{3,0},{4,5},{5,6},{6,7},{7,4},{8,9},{9,10},{10,1... | collective-permute-start | bytes 3194888 | tf_op jit(solution)/shard_map/ppermute | solution.py:525
  51.9 47.4 %collective-permute-start.3 = (bf16[800,640]{1,0:T(8,128)(2,1)}, bf16[800,640]{1,0:T(8,128)(2,1)}, u32[]{:S(2)}, u32[]{:S(2)}) collective-permute-start(bf16[800,640]{1,0:T(8,128)(2,1)} %get-tuple-element.30.own_high), channel_id=1, source_target_pairs={{0,1},{1,2},{2,3},{3,0},{4,5},{5,6},{6,7},{7,4},{8,9},{9,10},{10,1... | collective-permute-start | bytes 3072008 | tf_op jit(solution)/shard_map/ppermute | solution.py:524
  53.1 46.2 %collective-permute-start.5 = (bf16[800,640]{1,0:T(8,128)(2,1)}, bf16[800,640]{1,0:T(8,128)(2,1)}, u32[]{:S(2)}, u32[]{:S(2)}) collective-permute-start(bf16[800,640]{1,0:T(8,128)(2,1)} %collective-permute-done.4.right_high), channel_id=1, source_target_pairs={{0,3},{1,0},{2,1},{3,2},{4,7},{5,4},{6,5},{7,6},{8,11},{9,8},{10,9... | collective-permute-start | bytes 3072008 | tf_op jit(solution)/shard_map/ppermute | solution.py:526
  68.2 1.4 copy-start
  115.7 27.5 %all-to-all-start.1 = ((bf16[32,144,128]{2,1,0:T(8,128)(2,1)}), bf16[32,144,128]{2,1,0:T(8,128)(2,1)}, u32[]{:S(2)}, u32[]{:S(2)}) async-start(bf16[32,144,128]{2,1,0:T(8,128)(2,1)} %get-tuple-element.38), calls=%async_computation.1 | async-start | bytes 2359296 | tf_op jit(solution)/shard_map/all_to_all | solution.py:646

commit v4 on v3

--- a/solution.py
+++ b/solution.py
@@ -153,27 +153,18 @@
         copy.wait()
 
 
-def pack_kernel(block_hbm, low_hbm, high_hbm, low_ref, high_ref, edge_ref, in_sem, out_sem):
-    edge = pltpu.make_async_copy(block_hbm.at[:, :, pl.ds(640, 1)], edge_ref, in_sem.at[10])
-    edge.start()
+def pack_kernel(block_hbm, low_hbm, high_hbm, low_ref, high_ref, in_sem, out_sem):
     incoming = []
     for q in range(10):
         target = low_ref if q < 5 else high_ref
         incoming.append(
             pltpu.make_async_copy(
-                block_hbm.at[q, :, pl.ds(0, 640)],
+                block_hbm.at[q, :, pl.ds(0, 512)],
                 target.at[pl.ds(q % 5 * 160, 160), :],
                 in_sem.at[q],
             )
         )
         incoming[-1].start()
-    edge.wait()
-    lane = lax.broadcasted_iota(jnp.int32, (160, 128), 1)
-    last = jnp.zeros((160, 128), F32)
-    for q in range(10):
-        last = jnp.where(lane == q, edge_ref[q].astype(F32), last)
-    for t in range(5):
-        low_ref[800:832, 128 * t : 128 * t + 128] = last[32 * t : 32 * t + 32].astype(BF16)
     for copy in incoming[:5]:
         copy.wait()
     low_out = pltpu.make_async_copy(low_ref, low_hbm, out_sem.at[0])
@@ -184,6 +175,32 @@
     high_out.start()
     low_out.wait()
     high_out.wait()
+
+
+def pack_rest_kernel(block_hbm, rest_hbm, rest_ref, edge_ref, in_sem, out_sem):
+    edge = pltpu.make_async_copy(block_hbm.at[:, :, pl.ds(640, 1)], edge_ref, in_sem.at[10])
+    edge.start()
+    incoming = []
+    for q in range(10):
+        incoming.append(
+            pltpu.make_async_copy(
+                block_hbm.at[q, :, pl.ds(512, 128)],
+                rest_ref.at[pl.ds(q * 160, 160), :],
+                in_sem.at[q],
+            )
+        )
+        incoming[-1].start()
+    edge.wait()
+    lane = lax.broadcasted_iota(jnp.int32, (160, 128), 1)
+    last = jnp.zeros((160, 128), F32)
+    for q in range(10):
+        last = jnp.where(lane == q, edge_ref[q].astype(F32), last)
+    rest_ref[1600:, :] = last.astype(BF16)
+    for copy in incoming:
+        copy.wait()
+    leaving = pltpu.make_async_copy(rest_ref, rest_hbm, out_sem)
+    leaving.start()
+    leaving.wait()
 
 
 def lanes_kernel(wire_ref, out_ref, north_ref, south_ref):
@@ -262,6 +279,11 @@
         ).astype(BF16)
 
 
+def row_mask(condition, rows):
+    value = jnp.where(condition, 1, 0)
+    return jnp.broadcast_to(value, (rows, value.shape[1])) == 1
+
+
 def slot_kernel(
     info_ref,
     waves_ref,
@@ -280,29 +302,26 @@
     wire_hbm,
     spectrum_ref,
     block_ref,
-    last_ref,
     pack_ref,
     wire_ref,
     spectrum_sem,
     block_sem,
-    last_sem,
     wire_sem,
 ):
-    slot = pl.program_id(0)
+    step = pl.program_id(0)
     x = info_ref[0]
-    p = info_ref[1 + slot]
     lows = (own_low, right_low, far_low, left_low)
     highs = (own_high, right_high, far_high, left_high)
 
     def copies(sources, q, first):
         out = []
-        for step, source in enumerate(sources):
-            place = pl.multiple_of(((x + step) % 4) * 160, 160)
+        for k, source in enumerate(sources):
+            place = pl.multiple_of(((x + k) % 4) * 160, 160)
             out.append(
                 pltpu.make_async_copy(
                     source.at[pl.ds(pl.multiple_of((q - first) * 160, 160), 160), :],
-                    block_ref.at[q % 2, pl.ds(place, 160), pl.ds(0, 640)],
-                    block_sem.at[q % 2, step],
+                    block_ref.at[q % 4, pl.ds(place, 160), :],
+                    block_sem.at[q % 4, k],
                 )
             )
         return out
@@ -318,96 +337,122 @@
             for copy in copies(highs, q, 5):
                 copy.start()
 
-    @pl.when(slot == 0)
+    @pl.when(step == 0)
     def _():
-        fetch(slot)
-        lasts = [
-            pltpu.make_async_copy(
-                source.at[pl.ds(800, 32), :], last_ref.at[step], last_sem.at[step]
-            )
-            for step, source in enumerate(lows)
-        ]
-        for copy in lasts:
-            copy.start()
+        fetch(2 * step)
+        fetch(2 * step + 1)
         for row in range(140, 144):
             pack_ref[pl.ds(row, 32, stride=144), :] = jnp.zeros((32, 128), F32)
-        for copy in lasts:
+
+    @pl.when(step < 4)
+    def _():
+        fetch(2 * step + 2)
+        fetch(2 * step + 3)
+
+    slots = [2 * step, 2 * step + 1]
+    orders = [info_ref[1 + q] for q in slots]
+    for q in slots:
+        for copy in copies(lows, q, q):
             copy.wait()
-        for step in range(4):
-            value = last_ref[step]
-            value = jnp.concatenate([value[:, 128 * t : 128 * t + 128] for t in range(5)], axis=0)
-            place = pl.multiple_of(((x + step) % 4) * 160, 160)
-            for k in range(2):
-                block_ref[k, pl.ds(place, 160), 640:] = value
-
-    @pl.when(slot < 9)
-    def _():
-        fetch(slot + 1)
-
-    for copy in copies(lows, slot, slot):
-        copy.wait()
-    total = lax.dot_general(waves_ref[0], block_ref[slot % 2], NN, preferred_element_type=F32)
-    total = jnp.concatenate(
-        [total[:, :640], pltpu.roll(total[:, 640:], lax.rem(128 - slot, 128), 1)], axis=1
-    )
-    rank = lax.broadcasted_iota(jnp.int32, (48, 768), 1)
-    even_pair = p % 2 == 0
+
+    rank = lax.broadcasted_iota(jnp.int32, (1, 512), 1)
     sym = rank < 321
     place = jnp.where(sym, rank, rank - 321)
-    bound = jnp.where(sym, (641 - p) // 2, (640 - p) // 2)
-    first = (place < bound) == even_pair
-    chosen = jnp.where(
-        sym,
-        jnp.where(first, total[0:48], total[48:96]),
-        jnp.where(first, total[96:144], total[144:192]),
-    ).astype(BF16)
-    spectrum_ref[slot] = chosen[:, :641]
-    pltpu.make_async_copy(
-        spectrum_ref.at[slot], spectrum_hbm.at[slot], spectrum_sem.at[slot]
-    ).start()
-    rows = chosen.astype(F32)
+    all_rows = []
+    for k, (q, p) in enumerate(zip(slots, orders)):
+        low = lax.dot_general(
+            waves_ref[k, :96, :], block_ref[q % 4, :, :256], NN, preferred_element_type=F32
+        )
+        high = lax.dot_general(
+            waves_ref[k], block_ref[q % 4, :, 256:], NN, preferred_element_type=F32
+        )
+        bound = jnp.where(sym, (641 - p) // 2, (640 - p) // 2)
+        first = row_mask((place < bound) == (p % 2 == 0), 48)
+        is_sym = row_mask(sym[:, 256:], 48)
+        low = jnp.where(first[:, :256], low[:48], low[48:])
+        high = jnp.where(
+            is_sym,
+            jnp.where(first[:, 256:], high[0:48], high[48:96]),
+            jnp.where(first[:, 256:], high[96:144], high[144:192]),
+        )
+        chosen = jnp.concatenate([low, high], axis=1).astype(BF16)
+        spectrum_ref[q] = chosen
+        all_rows.append(chosen.astype(F32))
     group = 0
     for level, table_ref, count in ((0, one_ref, 4), (1, two_ref, 2), (2, three_ref, 1)):
         size = table_ref.shape[1]
         half = size // 2
         limit = info_ref[11 + level]
-        lane = lax.broadcasted_iota(jnp.int32, (48, size), 1)
+        lane = lax.broadcasted_iota(jnp.int32, (1, size), 1)
         is_sym = lane < half
-        later = pltpu.roll(rows, 768 - 321 + half, 1)[:, :size]
-        order = p + jnp.where(is_sym, 2 * lane, 2 * (lane - half) + 1)
-        kept = jnp.where(order <= limit, jnp.where(is_sym, rows[:, :size], later), 0.0)
-        both = jnp.concatenate(
-            [kept, jnp.where(is_sym, kept, -kept), jnp.zeros((32, size), F32)], axis=0
-        ).astype(BF16)
-        value = lax.dot_general(table_ref[0], both, NT, preferred_element_type=F32)
+        sym_rows = row_mask(is_sym, 48)
+        extra = jnp.where(is_sym, 2 * lane, 2 * (lane - half) + 1)
         many = 16 * count
-        lane = lax.broadcasted_iota(jnp.int32, (many, 128), 1)
-        for sign in range(2):
-            for c in range(2):
-                packed = jnp.zeros((many, 128), F32)
-                for b in range(5):
-                    part = value[many * b : many * b + many]
-                    move = 24 * (b - 2 * sign - c) % 128
-                    if move:
-                        part = pltpu.roll(part, move, 1)
-                    packed = jnp.where((lane >= 24 * b) & (lane < 24 * b + 24), part, packed)
-                for a in range(count):
-                    start = sign * 16 * 144 + 20 * (group + a) + 10 * c + slot
-                    pack_ref[pl.ds(start, 16, stride=144), :] = packed[16 * a : 16 * a + 16]
+        wide = lax.broadcasted_iota(jnp.int32, (many, 128), 1)
+        for k, (q, p) in enumerate(zip(slots, orders)):
+            rows = all_rows[k]
+            later = pltpu.roll(rows, 512 - 321 + half, 1)[:, :size]
+            keep = row_mask(p + extra <= limit, 48)
+            kept = jnp.where(keep, jnp.where(sym_rows, rows[:, :size], later), 0.0)
+            both = jnp.concatenate(
+                [kept, jnp.where(sym_rows, kept, -kept), jnp.zeros((32, size), F32)], axis=0
+            ).astype(BF16)
+            value = lax.dot_general(table_ref[k], both, NT, preferred_element_type=F32)
+            for sign in range(2):
+                for c in range(2):
+                    packed = None
+                    for b in range(5):
+                        part = value[many * b : many * b + many]
+                        move = 24 * (b - 2 * sign - c) % 128
+                        if move:
+                            part = pltpu.roll(part, move, 1)
+                        packed = part if b == 0 else jnp.where(wide >= 24 * b, part, packed)
+                    for a in range(count):
+                        start = sign * 16 * 144 + 20 * (group + a) + 10 * c + q
+                        pack_ref[pl.ds(start, 16, stride=144), :] = packed[16 * a : 16 * a + 16]
         group += count
 
-    @pl.when(slot == pl.num_programs(0) - 1)
+    @pl.when(step == pl.num_programs(0) - 1)
     def _():
         for d in range(16):
             wire_ref[d] = pack_ref[144 * d : 144 * d + 144, :].astype(BF16)
             wire_ref[31 - d] = pack_ref[144 * (16 + d) : 144 * (17 + d), :].astype(BF16)
-        leaving = pltpu.make_async_copy(wire_ref, wire_hbm, wire_sem)
-        leaving.start()
-        for k in range(10):
-            pltpu.make_async_copy(
-                spectrum_ref.at[k], spectrum_hbm.at[k], spectrum_sem.at[k]
-            ).wait()
-        leaving.wait()
+        leaving = [
+            pltpu.make_async_copy(wire_ref, wire_hbm, wire_sem),
+            pltpu.make_async_copy(spectrum_ref, spectrum_hbm, spectrum_sem),
+        ]
+        for copy in leaving:
+            copy.start()
+        for copy in leaving:
+            copy.wait()
+
+
+def rest_kernel(
+    info_ref, waves_ref, own_ref, left_ref, right_ref, far_ref, out_ref, block_ref, edge_ref
+):
+    x = info_ref[0]
+    for k, source in enumerate((own_ref, right_ref, far_ref, left_ref)):
+        place = pl.multiple_of(((x + k) % 4) * 160, 160)
+        for q in range(10):
+            block_ref[q, pl.ds(place, 160), :] = source[160 * q : 160 * q + 160, :]
+        edge_ref[pl.ds(place, 160), :] = source[1600:, :]
+    rank = lax.broadcasted_iota(jnp.int32, (1, 128), 1) + (512 - 321)
+    lane = lax.broadcasted_iota(jnp.int32, (48, 128), 1)
+
+    def slot(q, carry):
+        p = info_ref[1 + q]
+        left = waves_ref[q, 96:, :]
+        even_pair = p % 2 == 0
+        bound = (640 - p) // 2
+        value = lax.dot_general(left, block_ref[q], NN, preferred_element_type=F32)
+        first = row_mask((rank < bound) == even_pair, 48)
+        out_ref[q, :, :128] = jnp.where(first, value[:48], value[48:]).astype(BF16)
+        value = lax.dot_general(left, edge_ref[...], NN, preferred_element_type=F32)
+        value = jnp.where(((319 < bound) == even_pair) & (lane >= 0), value[:48], value[48:])
+        out_ref[q, :, 128:] = pltpu.roll(value, lax.rem(128 - q, 128), 1)[:, :1].astype(BF16)
+        return carry
+
+    lax.fori_loop(0, 10, slot, 0)
 
 
 def inverse_table_kernel(waves_ref, table_ref, high_cos, high_sin):
@@ -502,15 +547,14 @@
     own = jnp.transpose(legendre, (0, 2, 1))
     low, high = call(
         pack_kernel,
-        [jax.ShapeDtypeStruct((832, 640), BF16), jax.ShapeDtypeStruct((800, 640), BF16)],
+        [jax.ShapeDtypeStruct((800, 512), BF16)] * 2,
         60,
         in_specs=[hbm],
         out_specs=[hbm, hbm],
         scratch_shapes=[
-            pltpu.VMEM((832, 640), BF16),
-            pltpu.VMEM((800, 640), BF16),
-            pltpu.VMEM((10, 160, 1), BF16),
-            pltpu.SemaphoreType.DMA((11,)),
+            pltpu.VMEM((800, 512), BF16),
+            pltpu.VMEM((800, 512), BF16),
+            pltpu.SemaphoreType.DMA((10,)),
             pltpu.SemaphoreType.DMA((2,)),
         ],
         name="pack",
@@ -518,6 +562,7 @@
     low, high, grid_fields, assign = lax.optimization_barrier((low, high, grid_fields, assign))
     right = [(k, (k + 1) % 4) for k in range(4)]
     left = [(k, (k + 3) % 4) for k in range(4)]
+    across = [(k, (k + 2) % 4) for k in range(4)]
     low_left = lax.ppermute(low, "fld", right)
     high_right = lax.ppermute(high, "fld", left)
     low_right = lax.ppermute(low, "fld", left)
@@ -556,10 +601,28 @@
         ],
         name="dft",
     )((lat_at % 16 * 40).reshape(1), forward_waves, grid_fields.reshape(fields * rows, lon))
-    assign_after, synth_one, synth_two, synth_three, wire = lax.optimization_barrier(
-        (assign, synth_one, synth_two, synth_three, wire)
+    assign_after, synth_one, synth_two, synth_three, own, wire = lax.optimization_barrier(
+        (assign, synth_one, synth_two, synth_three, own, wire)
     )
     wire = lax.all_to_all(wire, "lat", split_axis=0, concat_axis=0, tiled=True)
+
+    rest = call(
+        pack_rest_kernel,
+        jax.ShapeDtypeStruct((1760, 128), BF16),
+        60,
+        in_specs=[hbm],
+        out_specs=hbm,
+        scratch_shapes=[
+            pltpu.VMEM((1760, 128), BF16),
+            pltpu.VMEM((10, 160, 1), BF16),
+            pltpu.SemaphoreType.DMA((11,)),
+            pltpu.SemaphoreType.DMA(()),
+        ],
+        name="pack_rest",
+    )(own)
+    rest_left = lax.ppermute(rest, "fld", right)
+    rest_right = lax.ppermute(rest, "fld", left)
+    rest_far = lax.ppermute(rest, "fld", across)
 
     synths = (synth_one, synth_two, synth_three)
     slot_block = [pl.BlockSpec((1,) + t.shape[1:], lambda q: (q, 0, 0)) for t in synths]
@@ -574,19 +637,6 @@
         name="turn_tables",
     )(*synths)
 
-    plain = assign_after.reshape(32, 10).astype(F32)
-    spare = jnp.zeros((32, 4), F32)
-    inverse_waves = jnp.concatenate([plain, plain, spare], axis=1).reshape(1, 768)
-    table = call(
-        inverse_table_kernel,
-        jax.ShapeDtypeStruct((2240, 768), BF16),
-        12,
-        in_specs=[vmem],
-        out_specs=vmem,
-        scratch_shapes=[pltpu.VMEM((80, 768), F32), pltpu.VMEM((80, 768), F32)],
-        name="inverse_tables",
-    )(inverse_waves)
-
     waves = call(
         lanes_kernel,
         jax.ShapeDtypeStruct((10, 192, 640), BF16),
@@ -606,26 +656,24 @@
     spectrum, level_wire = call(
         slot_kernel,
         [
-            jax.ShapeDtypeStruct((10, 2 * fields, 641), BF16),
+            jax.ShapeDtypeStruct((10, 2 * fields, 512), BF16),
             jax.ShapeDtypeStruct((32, 144, 128), BF16),
         ],
         60,
         grid_spec=pltpu.PrefetchScalarGridSpec(
             num_scalar_prefetch=1,
-            grid=(10,),
-            in_specs=[pl.BlockSpec((1, 192, 640), lambda q, *_: (q, 0, 0))]
+            grid=(5,),
+            in_specs=[pl.BlockSpec((2, 192, 640), lambda q, *_: (q, 0, 0))]
             + [hbm] * 8
-            + [pl.BlockSpec((1,) + t.shape[1:], lambda q, *_: (q, 0, 0)) for t in turned],
+            + [pl.BlockSpec((2,) + t.shape[1:], lambda q, *_: (q, 0, 0)) for t in turned],
             out_specs=[hbm, hbm],
             scratch_shapes=[
-                pltpu.VMEM((10, 2 * fields, 641), BF16),
-                pltpu.VMEM((2, 640, 768), BF16),
-                pltpu.VMEM((4, 32, 640), BF16),
+                pltpu.VMEM((10, 2 * fields, 512), BF16),
+                pltpu.VMEM((4, 640, 512), BF16),
                 pltpu.VMEM((32 * 144, 128), F32),
                 pltpu.VMEM((32, 144, 128), BF16),
-                pltpu.SemaphoreType.DMA((10,)),
-                pltpu.SemaphoreType.DMA((2, 4)),
-                pltpu.SemaphoreType.DMA((4,)),
+                pltpu.SemaphoreType.DMA(()),
+                pltpu.SemaphoreType.DMA((4, 4)),
                 pltpu.SemaphoreType.DMA(()),
             ],
         ),
@@ -643,7 +691,31 @@
         high_far,
         *turned,
     )
+    info, waves, level_wire = lax.optimization_barrier((info, waves, level_wire))
+    rest_spectrum = call(
+        rest_kernel,
+        jax.ShapeDtypeStruct((10, 2 * fields, 129), BF16),
+        16,
+        in_specs=[pl.BlockSpec(memory_space=pltpu.SMEM)] + [vmem] * 5,
+        out_specs=vmem,
+        scratch_shapes=[pltpu.VMEM((10, 640, 128), BF16), pltpu.VMEM((640, 128), BF16)],
+        name="rest",
+    )(info, waves, rest, rest_left, rest_right, rest_far)
     level_wire = lax.all_to_all(level_wire, "lat", split_axis=0, concat_axis=0, tiled=True)
+    assign_late, rest_spectrum = lax.optimization_barrier((assign, rest_spectrum))
+    plain = assign_late.reshape(32, 10).astype(F32)
+    spare = jnp.zeros((32, 4), F32)
+    inverse_waves = jnp.concatenate([plain, plain, spare], axis=1).reshape(1, 768)
+    table = call(
+        inverse_table_kernel,
+        jax.ShapeDtypeStruct((2240, 768), BF16),
+        12,
+        in_specs=[vmem],
+        out_specs=vmem,
+        scratch_shapes=[pltpu.VMEM((80, 768), F32), pltpu.VMEM((80, 768), F32)],
+        name="inverse_tables",
+    )(inverse_waves)
+
 
     late_half = (lat_at >= 16).astype(jnp.int32).reshape(1)
     grids = call(
@@ -665,7 +737,8 @@
         name="inverse",
     )(late_half, level_wire, table)
     grids = [jnp.transpose(g, (1, 0, 2)) for g in grids]
-    spectrum = jnp.transpose(spectrum.reshape(10, 2, fields, 641), (2, 1, 0, 3))
+    spectrum = jnp.concatenate([spectrum, rest_spectrum], axis=2).reshape(10, 2, fields, 641)
+    spectrum = jnp.transpose(spectrum, (2, 1, 0, 3))
     return (spectrum, *grids)
 
 

time: 149 us -> 144 us (0.966)
  waiting for transfers between devices: 65.4 us -> 54.1 us
  starting transfers between devices: 25.3 us -> 29.1 us
    ppermute x1, waiting for transfers between devices: 29.7 us -> 0.01 us  [on_device(): high_left = lax.ppermute(high, 'fld', right)]
    ppermute x0 -> x3, waiting for transfers between devices: none -> 20 us  [the longest x1 10.8 us: on_device(): rest_far = lax.ppermute(rest, 'fld', across)]
    ppermute x1, waiting for transfers between devices: 0.01 us -> 16.6 us  [on_device(): low_far = lax.ppermute(low_left, 'fld', right)]
    all_to_all x1, waiting for transfers between devices: 13.2 us -> 0.01 us  [on_device(): lax.all_to_all(level_wire, 'lat', split_axis=0, concat_axis=0, tiled=True)]
    ppermute x1, waiting for transfers between devices: 22.4 us -> 16.7 us  [on_device(): low_left = lax.ppermute(low, 'fld', right)]
    ppermute x0 -> x3, starting transfers between devices: none -> 3.99 us  [the longest x1 1.53 us: on_device(): rest_right = lax.ppermute(rest, 'fld', left)]
    unnamed x6 -> x18, local copies, waits for them, and re-layouts: 1.44 us -> 3.18 us
    pallas_call x2 -> x4, Pallas kernels: 19.2 us -> 20.3 us  [the longest x1 11.6 us: on_device(): call(slot_kernel, [jax.ShapeDtypeStruct((10, 2 * fields, 512), BF16), jax...]
  transfers between devices with their start and end apart: 8 -> 11, of which waited for: 3 -> 5; matrix products, arithmetic and copies ran while one was open for 2% -> 2% of each run, Pallas kernels for 10% -> 15%
where the time goes in v4:
time: 144 us; the launch traced here: 143 us
  waiting for transfers between devices  54.1 us (38%)
  Pallas kernels  51.2 us (36%)
  starting transfers between devices  29.1 us (20%)
  local copies, waits for them, and re-layouts  5.17 us (4%)
  other arithmetic  2.56 us (2%)
    ppermute x1, waiting for transfers between devices, on_device(): low_left = lax.ppermute(low, 'fld', right)  16.7 us
    ppermute x1, waiting for transfers between devices, on_device(): low_far = lax.ppermute(low_left, 'fld', right)  16.6 us
    pallas_call x1, Pallas kernels, on_device(): call(slot_kernel, [jax.ShapeDtypeStruct((10, 2 * fields, 512), BF16), jax...  11.6 us
    pallas_call x1, Pallas kernels, on_device(): call(dft_kernel, jax.ShapeDtypeStruct((32, 40, 1024), BF16), 60, in_specs...  11.3 us
    ppermute x1, waiting for transfers between devices, on_device(): rest_far = lax.ppermute(rest, 'fld', across)  10.8 us
    all_to_all x1, starting transfers between devices, on_device(): wire = lax.all_to_all(wire, 'lat', split_axis=0, concat_axis=0, tiled=True)  9.74 us
    ppermute x1, waiting for transfers between devices, on_device(): rest_left = lax.ppermute(rest, 'fld', right)  9.21 us
    pallas_call x1, Pallas kernels, on_device(): call(turn_tables_kernel, [jax.ShapeDtypeStruct(t.shape, BF16) for t in sy...  8.74 us
  transfers between devices with their start and end apart: 11, of which 5 were waited for; matrix products, arithmetic and copies ran while one was open for 2% of the time, Pallas kernels for 15%

profile of v4, /device:TPU:1, one launch (start us, length us, event | category | flops | bytes accessed | tf_op | source)
XLA Modules:
  0.0 143.2 jit_solution(18272680699215715494)
XLA Ops:
  0.7 2.5 %pack.1 = (bf16[800,512]{1,0:T(8,128)(2,1)}, bf16[800,512]{1,0:T(8,128)(2,1)}) custom-call(bf16[10,160,641]{2,1,0:T(8,128)(2,1)} %bitcast.12), custom_call_target="tpu_custom_call" | custom-call | tf_op jit(solution)/shard_map/pack/pallas_call | solution.py:548
  3.6 0.6 pad_maximum_fusion.4.waves_ref
  4.2 11.3 %dft.1 = bf16[32,40,1024]{2,1,0:T(8,128)(2,1)} custom-call(s32[1]{0:T(128)} %bitcast.2.info_ref, f32[2,768]{1,0:T(2,128)} %pad_maximum_fusion.4.waves_ref, bf16[960,2560]{1,0:T(8,128)(2,1)} %bitcast.14), custom_call_target="tpu_custom_call" | custom-call | tf_op jit(solution)/shard_map/dft/pallas_call | solution.py:583
  15.5 9.7 %all-to-all-start = ((bf16[32,40,1024]{2,1,0:T(8,128)(2,1)}), bf16[32,40,1024]{2,1,0:T(8,128)(2,1)S(1)}, u32[]{:S(2)}, u32[]{:S(2)}) async-start(bf16[32,40,1024]{2,1,0:T(8,128)(2,1)} %dft.1), calls=%async_computation | async-start | bytes 5242880 | tf_op jit(solution)/shard_map/all_to_all | solution.py:607
  25.3 1.3 collective-permute-start
  26.6 1.5 %collective-permute-start.4 = (bf16[800,512]{1,0:T(8,128)(2,1)}, bf16[800,512]{1,0:T(8,128)(2,1)}, u32[]{:S(2)}, u32[]{:S(2)}) collective-permute-start(bf16[800,512]{1,0:T(8,128)(2,1)} %get-tuple-element.36.own_high), channel_id=1, source_target_pairs={{0,3},{1,0},{2,1},{3,2},{4,7},{5,4},{6,5},{7,6},{8,11},{9,8},{10,9... | collective-permute-start | bytes 2457608 | tf_op jit(solution)/shard_map/ppermute | solution.py:567
  28.0 1.3 collective-permute-start.1
  29.3 0.2 collective-permute-start.3
  29.5 16.7 %collective-permute-done.left_low = bf16[800,512]{1,0:T(8,128)(2,1)} collective-permute-done((bf16[800,512]{1,0:T(8,128)(2,1)S(1)}, bf16[800,512]{1,0:T(8,128)(2,1)}, u32[]{:S(2)}, u32[]{:S(2)}) %collective-permute-start) | collective-permute-done | bytes 819232 | tf_op jit(solution)/shard_map/ppermute | solution.py:566
  46.3 2.7 %collective-permute-start.5 = (bf16[800,512]{1,0:T(8,128)(2,1)}, bf16[800,512]{1,0:T(8,128)(2,1)}, u32[]{:S(2)}, u32[]{:S(2)}) collective-permute-start(bf16[800,512]{1,0:T(8,128)(2,1)} %collective-permute-done.4.right_high), channel_id=1, source_target_pairs={{0,3},{1,0},{2,1},{3,2},{4,7},{5,4},{6,5},{7,6},{8,11},{9,8},{10,9... | collective-permute-start | bytes 2457608 | tf_op jit(solution)/shard_map/ppermute | solution.py:571
  49.0 8.7 %turn_tables.1 = (bf16[10,320,320]{2,1,0:T(8,128)(2,1)}, bf16[10,160,160]{2,1,0:T(8,128)(2,1)}, bf16[10,80,80]{2,1,0:T(8,128)(2,1)}) custom-call(bf16[10,320,320]{2,1,0:T(8,128)(2,1)} %one_ref, bf16[10,160,160]{2,1,0:T(8,128)(2,1)} %two_ref, bf16[10,80,80]{2,1,0:T(8,128)(2,1)} %three_ref), custom_call_target="tpu_custom_call" | custom-call | tf_op jit(solution)/shard_map/turn_tables/pallas_call | solution.py:629
  57.7 0.7 pad_add_fusion.info_ref
  58.4 0.8 all-to-all-done.wire_ref
  59.2 4.2 %lanes.1.waves_ref = bf16[10,192,640]{2,1,0:T(8,128)(2,1)S(1)} custom-call(bf16[32,40,1024]{2,1,0:T(8,128)(2,1)S(1)} %all-to-all-done.wire_ref), custom_call_target="tpu_custom_call" | custom-call | tf_op jit(solution)/shard_map/lanes/pallas_call | solution.py:640
  63.4 1.4 copy-done
  64.8 16.6 %collective-permute-done.2.far_low = bf16[800,512]{1,0:T(8,128)(2,1)} collective-permute-done((bf16[800,512]{1,0:T(8,128)(2,1)}, bf16[800,512]{1,0:T(8,128)(2,1)}, u32[]{:S(2)}, u32[]{:S(2)}) %collective-permute-start.2) | collective-permute-done | bytes 819232 | tf_op jit(solution)/shard_map/ppermute | solution.py:570
  81.4 11.6 %slots.1 = (bf16[10,48,512]{2,1,0:T(8,128)(2,1)}, bf16[32,144,128]{2,1,0:T(8,128)(2,1)}) custom-call(s32[14]{0:T(128)} %pad_add_fusion.info_ref, bf16[10,192,640]{2,1,0:T(8,128)(2,1)} %copy-done, bf16[800,512]{1,0:T(8,128)(2,1)} %get-tuple-element.35.own_low, bf16[800,512]{1,0:T(8,128)(2,1)} %collective-permute-done.left_low, ...), custom_call_target="tpu_custom_call" | custom-call | tf_op jit(solution)/shard_map/slots/pallas_call | solution.py:656
  93.0 8.5 %all-to-all-start.1 = ((bf16[32,144,128]{2,1,0:T(8,128)(2,1)}), bf16[32,144,128]{2,1,0:T(8,128)(2,1)}, u32[]{:S(2)}, u32[]{:S(2)}) async-start(bf16[32,144,128]{2,1,0:T(8,128)(2,1)} %get-tuple-element.49), calls=%async_computation.1 | async-start | bytes 2359296 | tf_op jit(solution)/shard_map/all_to_all | solution.py:704
  101.5 2.1 %pack_rest.1.own_ref = bf16[1760,128]{1,0:T(8,128)(2,1)} custom-call(bf16[10,160,641]{2,1,0:T(8,128)(2,1)} %bitcast.13), custom_call_target="tpu_custom_call" | custom-call | tf_op jit(solution)/shard_map/pack_rest/pallas_call | solution.py:609
  103.6 1.3 collective-permute-start.6
  104.9 1.5 %collective-permute-start.7 = (bf16[1760,128]{1,0:T(8,128)(2,1)}, bf16[1760,128]{1,0:T(8,128)(2,1)S(1)}, u32[]{:S(2)}, u32[]{:S(2)}) collective-permute-start(bf16[1760,128]{1,0:T(8,128)(2,1)} %pack_rest.1.own_ref), channel_id=1, source_target_pairs={{0,3},{1,0},{2,1},{3,2},{4,7},{5,4},{6,5},{7,6},{8,11},{9,8},{10,9... | collective-permute-start | bytes 1351688 | tf_op jit(solution)/shard_map/ppermute | solution.py:624
  106.4 1.2 collective-permute-start.8
  107.6 9.2 %collective-permute-done.6.left_ref = bf16[1760,128]{1,0:T(8,128)(2,1)S(1)} collective-permute-done((bf16[1760,128]{1,0:T(8,128)(2,1)}, bf16[1760,128]{1,0:T(8,128)(2,1)S(1)}, u32[]{:S(2)}, u32[]{:S(2)}) %collective-permute-start.6) | collective-permute-done | bytes 450592 | tf_op jit(solution)/shard_map/ppermute | solution.py:623
  116.8 10.8 %collective-permute-done.8.far_ref = bf16[1760,128]{1,0:T(8,128)(2,1)} collective-permute-done((bf16[1760,128]{1,0:T(8,128)(2,1)}, bf16[1760,128]{1,0:T(8,128)(2,1)}, u32[]{:S(2)}, u32[]{:S(2)}) %collective-permute-start.8) | collective-permute-done | bytes 450592 | tf_op jit(solution)/shard_map/ppermute | solution.py:625
  127.6 1.0 copy-done.2
  128.6 4.1 %rest.1 = bf16[10,48,129]{2,1,0:T(8,128)(2,1)S(1)} custom-call(s32[14]{0:T(128)S(1)} %copy-done.5, bf16[10,192,640]{2,1,0:T(8,128)(2,1)S(1)} %copy-done.1, bf16[1760,128]{1,0:T(8,128)(2,1)S(1)} %copy-done.2, bf16[1760,128]{1,0:T(8,128)(2,1)S(1)} %collective-permute-done.6.left_ref, bf16[1760,128]{1,0:T(8,128)(2,1)S(1)} %collective-permute-done.7.right_ref, ...), custom_call_target="tpu_custom_call" | custom-call | tf_op jit(solution)/shard_map/rest/pallas_call | solution.py:695
  132.7 0.7 copy-done.3
  133.6 0.1 reshape.45.waves_ref
  133.7 2.3 %inverse_tables.1.table_ref = bf16[2240,768]{1,0:T(8,128)(2,1)S(1)} custom-call(f32[1,768]{1,0:T(1,128)S(1)} %reshape.45.waves_ref), custom_call_target="tpu_custom_call" | custom-call | tf_op jit(solution)/shard_map/inverse_tables/pallas_call | solution.py:709
  136.1 1.1 pad_maximum_fusion
  137.2 1.4 %copy.14 = bf16[10,2,24,641]{3,1,0,2:T(2,128)(2,1)} copy(bf16[10,2,24,641]{3,2,1,0:T(8,128)(2,1)S(1)} %bitcast.15) | data formatting | bytes 1230720 | tf_op jit(solution)/shard_map/reshape | solution.py:740
  138.6 4.4 %inverse.1 = (f32[20,24,1280]{2,1,0:T(8,128)}, f32[10,24,640]{2,1,0:T(8,128)}, f32[5,24,320]{2,1,0:T(8,128)}) custom-call(s32[1]{0:T(128)} %bitcast.6.info_ref, bf16[32,144,128]{2,1,0:T(8,128)(2,1)} %all-to-all-done.1.wire_ref, bf16[2240,768]{1,0:T(8,128)(2,1)S(1)} %inverse_tables.1.table_ref), custom_call_target="tpu_custom_call" | custom-call | tf_op jit(solution)/shard_map/inverse/pallas_call | solution.py:721
  (32 shorter events, 0.7 us)
Async XLA Ops:
  0.6 2.6 %copy-start.7 = (s32[320]{0:T(512)S(1)}, s32[320]{0:T(512)}, u32[]{:S(2)}) copy-start(s32[320]{0:T(512)} %param.8) | copy-start | bytes 3844
  15.5 9.8 %copy-start.6 = (bf16[800,512]{1,0:T(8,128)(2,1)S(1)}, bf16[800,512]{1,0:T(8,128)(2,1)}, u32[]{:S(2)}) copy-start(bf16[800,512]{1,0:T(8,128)(2,1)} %get-tuple-element.35.own_low) | copy-start | bytes 2457604
  15.5 43.7 %all-to-all-start = ((bf16[32,40,1024]{2,1,0:T(8,128)(2,1)}), bf16[32,40,1024]{2,1,0:T(8,128)(2,1)S(1)}, u32[]{:S(2)}, u32[]{:S(2)}) async-start(bf16[32,40,1024]{2,1,0:T(8,128)(2,1)} %dft.1), calls=%async_computation | async-start | bytes 5242880 | tf_op jit(solution)/shard_map/all_to_all | solution.py:607
  25.3 32.5 %copy-start.8 = (s32[3]{0:T(128)S(1)}, s32[3]{0:T(128)}, u32[]{:S(2)}) copy-start(s32[3]{0:T(128)} %param.9) | copy-start | bytes 40
  25.3 21.0 %collective-permute-start = (bf16[800,512]{1,0:T(8,128)(2,1)S(1)}, bf16[800,512]{1,0:T(8,128)(2,1)}, u32[]{:S(2)}, u32[]{:S(2)}) collective-permute-start(bf16[800,512]{1,0:T(8,128)(2,1)S(1)} %copy-done.6), channel_id=1, source_target_pairs={{0,1},{1,2},{2,3},{3,0},{4,5},{5,6},{6,7},{7,4},{8,9},{9,10},{10,1... | collective-permute-start | bytes 2457608 | tf_op jit(solution)/shard_map/ppermute | solution.py:566
  26.6 19.7 %collective-permute-start.4 = (bf16[800,512]{1,0:T(8,128)(2,1)}, bf16[800,512]{1,0:T(8,128)(2,1)}, u32[]{:S(2)}, u32[]{:S(2)}) collective-permute-start(bf16[800,512]{1,0:T(8,128)(2,1)} %get-tuple-element.36.own_high), channel_id=1, source_target_pairs={{0,3},{1,0},{2,1},{3,2},{4,7},{5,4},{6,5},{7,6},{8,11},{9,8},{10,9... | collective-permute-start | bytes 2457608 | tf_op jit(solution)/shard_map/ppermute | solution.py:567
  28.0 36.8 %collective-permute-start.1 = (bf16[800,512]{1,0:T(8,128)(2,1)S(1)}, bf16[800,512]{1,0:T(8,128)(2,1)}, u32[]{:S(2)}, u32[]{:S(2)}) collective-permute-start(bf16[800,512]{1,0:T(8,128)(2,1)S(1)} %copy-done.6), channel_id=1, source_target_pairs={{0,3},{1,0},{2,1},{3,2},{4,7},{5,4},{6,5},{7,6},{8,11},{9,8},{10,9... | collective-permute-start | bytes 2457608 | tf_op jit(solution)/shard_map/ppermute | solution.py:568
  29.3 35.5 %collective-permute-start.3 = (bf16[800,512]{1,0:T(8,128)(2,1)}, bf16[800,512]{1,0:T(8,128)(2,1)}, u32[]{:S(2)}, u32[]{:S(2)}) collective-permute-start(bf16[800,512]{1,0:T(8,128)(2,1)} %get-tuple-element.36.own_high), channel_id=1, source_target_pairs={{0,1},{1,2},{2,3},{3,0},{4,5},{5,6},{6,7},{7,4},{8,9},{9,10},{10,1... | collective-permute-start | bytes 2457608 | tf_op jit(solution)/shard_map/ppermute | solution.py:569
  46.2 35.1 %collective-permute-start.2 = (bf16[800,512]{1,0:T(8,128)(2,1)}, bf16[800,512]{1,0:T(8,128)(2,1)}, u32[]{:S(2)}, u32[]{:S(2)}) collective-permute-start(bf16[800,512]{1,0:T(8,128)(2,1)} %collective-permute-done.left_low), channel_id=1, source_target_pairs={{0,1},{1,2},{2,3},{3,0},{4,5},{5,6},{6,7},{7,4},{8,9},{9,10},{10,1... | collective-permute-start | bytes 2457608 | tf_op jit(solution)/shard_map/ppermute | solution.py:570
  46.3 35.1 %collective-permute-start.5 = (bf16[800,512]{1,0:T(8,128)(2,1)}, bf16[800,512]{1,0:T(8,128)(2,1)}, u32[]{:S(2)}, u32[]{:S(2)}) collective-permute-start(bf16[800,512]{1,0:T(8,128)(2,1)} %collective-permute-done.4.right_high), channel_id=1, source_target_pairs={{0,3},{1,0},{2,1},{3,2},{4,7},{5,4},{6,5},{7,6},{8,11},{9,8},{10,9... | collective-permute-start | bytes 2457608 | tf_op jit(solution)/shard_map/ppermute | solution.py:571
  63.4 1.4 %copy-start = (bf16[10,192,640]{2,1,0:T(8,128)(2,1)}, bf16[10,192,640]{2,1,0:T(8,128)(2,1)S(1)}, u32[]{:S(2)}) copy-start(bf16[10,192,640]{2,1,0:T(8,128)(2,1)S(1)} %lanes.1.waves_ref) | copy-start | bytes 7372804
  93.0 34.6 %copy-start.1 = (bf16[10,192,640]{2,1,0:T(8,128)(2,1)S(1)}, bf16[10,192,640]{2,1,0:T(8,128)(2,1)}, u32[]{:S(2)}) copy-start(bf16[10,192,640]{2,1,0:T(8,128)(2,1)} %copy-done) | copy-start | bytes 7372804
  93.0 34.6 %copy-start.5 = (s32[14]{0:T(128)S(1)}, s32[14]{0:T(128)}, u32[]{:S(2)}) copy-start(s32[14]{0:T(128)} %pad_add_fusion.info_ref) | copy-start | bytes 172
  93.0 45.6 %all-to-all-start.1 = ((bf16[32,144,128]{2,1,0:T(8,128)(2,1)}), bf16[32,144,128]{2,1,0:T(8,128)(2,1)}, u32[]{:S(2)}, u32[]{:S(2)}) async-start(bf16[32,144,128]{2,1,0:T(8,128)(2,1)} %get-tuple-element.49), calls=%async_computation.1 | async-start | bytes 2359296 | tf_op jit(solution)/shard_map/all_to_all | solution.py:704
  103.6 13.2 %collective-permute-start.6 = (bf16[1760,128]{1,0:T(8,128)(2,1)}, bf16[1760,128]{1,0:T(8,128)(2,1)S(1)}, u32[]{:S(2)}, u32[]{:S(2)}) collective-permute-start(bf16[1760,128]{1,0:T(8,128)(2,1)} %pack_rest.1.own_ref), channel_id=1, source_target_pairs={{0,1},{1,2},{2,3},{3,0},{4,5},{5,6},{6,7},{7,4},{8,9},{9,10},{10,1... | collective-permute-start | bytes 1351688 | tf_op jit(solution)/shard_map/ppermute | solution.py:623
  104.9 11.9 %collective-permute-start.7 = (bf16[1760,128]{1,0:T(8,128)(2,1)}, bf16[1760,128]{1,0:T(8,128)(2,1)S(1)}, u32[]{:S(2)}, u32[]{:S(2)}) collective-permute-start(bf16[1760,128]{1,0:T(8,128)(2,1)} %pack_rest.1.own_ref), channel_id=1, source_target_pairs={{0,3},{1,0},{2,1},{3,2},{4,7},{5,4},{6,5},{7,6},{8,11},{9,8},{10,9... | collective-permute-start | bytes 1351688 | tf_op jit(solution)/shard_map/ppermute | solution.py:624
  106.4 21.2 %collective-permute-start.8 = (bf16[1760,128]{1,0:T(8,128)(2,1)}, bf16[1760,128]{1,0:T(8,128)(2,1)}, u32[]{:S(2)}, u32[]{:S(2)}) collective-permute-start(bf16[1760,128]{1,0:T(8,128)(2,1)} %pack_rest.1.own_ref), channel_id=1, source_target_pairs={{0,2},{1,3},{2,0},{3,1},{4,6},{5,7},{6,4},{7,5},{8,10},{9,11},{10,... | collective-permute-start | bytes 1351688 | tf_op jit(solution)/shard_map/ppermute | solution.py:625
  127.6 1.0 copy-start.2
  132.7 0.7 copy-start.3
  133.7 2.4 %copy-start.4 = (bf16[10,48,129]{2,1,0:T(8,128)(2,1)S(1)}, bf16[10,48,129]{2,1,0:T(8,128)(2,1)}, u32[]{:S(2)}) copy-start(bf16[10,48,129]{2,1,0:T(8,128)(2,1)} %copy-done.3) | copy-start | bytes 371524

commit v5 on v4

--- a/solution.py
+++ b/solution.py
@@ -203,19 +203,111 @@
     leaving.wait()
 
 
-def lanes_kernel(wire_ref, out_ref, north_ref, south_ref):
+def turn_tables_kernel(one_ref, two_ref, three_ref, out_one, out_two, out_three, *picks):
+    levels = ((one_ref, out_one, 4), (two_ref, out_two, 2), (three_ref, out_three, 1))
+
+    @pl.when(pl.program_id(0) == 0)
+    def _():
+        for pick_ref, (source, _, groups) in zip(picks, levels):
+            size = source.shape[1]
+            row = lax.broadcasted_iota(jnp.int32, (size, size), 0)
+            column = lax.broadcasted_iota(jnp.int32, (size, size), 1)
+            b = row // (16 * groups)
+            a = (row // 16) % groups
+            place = (row % 16) * (5 * groups) + 5 * a + b
+            pick_ref[...] = jnp.where(place == column, 1.0, 0.0).astype(BF16)
+
+    for pick_ref, (source, target, _) in zip(picks, levels):
+        target[0] = lax.dot_general(
+            pick_ref[...], source[0], NT, preferred_element_type=F32
+        ).astype(BF16)
+
+
+def row_mask(condition, rows):
+    value = jnp.where(condition, 1, 0)
+    return jnp.broadcast_to(value, (rows, value.shape[1])) == 1
+
+
+def level_kernel(
+    info_ref,
+    arrived_hbm,
+    own_low,
+    left_low,
+    right_low,
+    far_low,
+    own_high,
+    left_high,
+    right_high,
+    far_high,
+    one_hbm,
+    two_hbm,
+    three_hbm,
+    spectrum_hbm,
+    wire_hbm,
+    waves_hbm,
+    north_ref,
+    south_ref,
+    waves_ref,
+    block_ref,
+    one_ref,
+    two_ref,
+    three_ref,
+    spectrum_ref,
+    pack_ref,
+    wire_ref,
+    arrived_ref,
+    arrived_sem,
+    block_sem,
+    table_sem,
+    out_sem,
+):
+    x = info_ref[0]
+    arriving = [
+        pltpu.make_async_copy(
+            arrived_hbm.at[pl.ds(16 * k, 16)], arrived_ref.at[pl.ds(16 * k, 16)], arrived_sem.at[k]
+        )
+        for k in range(2)
+    ]
+    for copy in arriving:
+        copy.start()
+    lows = (own_low, right_low, far_low, left_low)
+    highs = (own_high, right_high, far_high, left_high)
+
+    def block_copy(source, q, place, k):
+        return pltpu.make_async_copy(
+            source.at[pl.ds(q % 5 * 160, 160), :],
+            block_ref.at[q, pl.ds(place, 160), :],
+            block_sem.at[q, k],
+        )
+
+    tables = [
+        pltpu.make_async_copy(source, target, table_sem.at[k])
+        for k, (source, target) in enumerate(
+            ((one_hbm, one_ref), (two_hbm, two_ref), (three_hbm, three_ref))
+        )
+    ]
+    for q in range(10):
+        for k, source in enumerate(lows if q < 5 else highs):
+            block_copy(source, q, pl.multiple_of(((x + k) % 4) * 160, 160), k).start()
+        if q == 1:
+            for copy in tables:
+                copy.start()
+    for row in range(140, 144):
+        pack_ref[pl.ds(row, 32, stride=144), :] = jnp.zeros((32, 128), F32)
+
     fields = north_ref.shape[1] // 40
     lane = lax.broadcasted_iota(jnp.int32, (40, 128), 1)
-    for f in range(fields):
-        offset = 40 * f % 128
-        for half, target in ((0, north_ref), (16, south_ref)):
+    for half, target in ((0, north_ref), (16, south_ref)):
+        arriving[half // 16].wait()
+        for f in range(fields):
+            offset = 40 * f % 128
             tiles = []
             for o in range(6 if offset else 5):
                 at = (40 * f // 128 + o) % 8 * 128
                 first = 128 * o - offset
                 tile = None
                 for k in range(max(first // 40, 0), min((first + 127) // 40, 15) + 1):
-                    piece = wire_ref[half + k, :, at : at + 128]
+                    piece = arrived_ref[half + k, :, at : at + 128]
                     tile = piece if tile is None else jnp.where(lane >= 40 * k - first, piece, tile)
                 tiles.append(tile.astype(F32))
             if offset:
@@ -253,178 +345,96 @@
                 for source in (north_ref, south_ref)
                 for g in range(4)
             ]
-            out_ref[q, :, 128 * t : 128 * t + 128] = jnp.concatenate(parts, axis=0).astype(BF16)
+            waves_ref[q, :, 128 * t : 128 * t + 128] = jnp.concatenate(parts, axis=0).astype(BF16)
         return carry
 
-    lax.fori_loop(0, out_ref.shape[0], slot, 0)
-
-
-def turn_tables_kernel(one_ref, two_ref, three_ref, out_one, out_two, out_three, *picks):
-    levels = ((one_ref, out_one, 4), (two_ref, out_two, 2), (three_ref, out_three, 1))
-
-    @pl.when(pl.program_id(0) == 0)
-    def _():
-        for pick_ref, (source, _, groups) in zip(picks, levels):
-            size = source.shape[1]
-            row = lax.broadcasted_iota(jnp.int32, (size, size), 0)
-            column = lax.broadcasted_iota(jnp.int32, (size, size), 1)
-            b = row // (16 * groups)
-            a = (row // 16) % groups
-            place = (row % 16) * (5 * groups) + 5 * a + b
-            pick_ref[...] = jnp.where(place == column, 1.0, 0.0).astype(BF16)
-
-    for pick_ref, (source, target, _) in zip(picks, levels):
-        target[0] = lax.dot_general(
-            pick_ref[...], source[0], NT, preferred_element_type=F32
-        ).astype(BF16)
-
-
-def row_mask(condition, rows):
-    value = jnp.where(condition, 1, 0)
-    return jnp.broadcast_to(value, (rows, value.shape[1])) == 1
-
-
-def slot_kernel(
-    info_ref,
-    waves_ref,
-    own_low,
-    left_low,
-    right_low,
-    far_low,
-    own_high,
-    left_high,
-    right_high,
-    far_high,
-    one_ref,
-    two_ref,
-    three_ref,
-    spectrum_hbm,
-    wire_hbm,
-    spectrum_ref,
-    block_ref,
-    pack_ref,
-    wire_ref,
-    spectrum_sem,
-    block_sem,
-    wire_sem,
-):
-    step = pl.program_id(0)
-    x = info_ref[0]
-    lows = (own_low, right_low, far_low, left_low)
-    highs = (own_high, right_high, far_high, left_high)
-
-    def copies(sources, q, first):
-        out = []
-        for k, source in enumerate(sources):
-            place = pl.multiple_of(((x + k) % 4) * 160, 160)
-            out.append(
-                pltpu.make_async_copy(
-                    source.at[pl.ds(pl.multiple_of((q - first) * 160, 160), 160), :],
-                    block_ref.at[q % 4, pl.ds(place, 160), :],
-                    block_sem.at[q % 4, k],
-                )
-            )
-        return out
-
-    def fetch(q):
-        @pl.when(q < 5)
-        def _():
-            for copy in copies(lows, q, 0):
-                copy.start()
-
-        @pl.when(q >= 5)
-        def _():
-            for copy in copies(highs, q, 5):
-                copy.start()
-
-    @pl.when(step == 0)
-    def _():
-        fetch(2 * step)
-        fetch(2 * step + 1)
-        for row in range(140, 144):
-            pack_ref[pl.ds(row, 32, stride=144), :] = jnp.zeros((32, 128), F32)
-
-    @pl.when(step < 4)
-    def _():
-        fetch(2 * step + 2)
-        fetch(2 * step + 3)
-
-    slots = [2 * step, 2 * step + 1]
-    orders = [info_ref[1 + q] for q in slots]
-    for q in slots:
-        for copy in copies(lows, q, q):
-            copy.wait()
-
+    lax.fori_loop(0, 10, slot, 0)
+
+    waves_out = pltpu.make_async_copy(waves_ref, waves_hbm, out_sem.at[0])
+    waves_out.start()
+    for copy in tables:
+        copy.wait()
     rank = lax.broadcasted_iota(jnp.int32, (1, 512), 1)
     sym = rank < 321
     place = jnp.where(sym, rank, rank - 321)
-    all_rows = []
-    for k, (q, p) in enumerate(zip(slots, orders)):
-        low = lax.dot_general(
-            waves_ref[k, :96, :], block_ref[q % 4, :, :256], NN, preferred_element_type=F32
-        )
-        high = lax.dot_general(
-            waves_ref[k], block_ref[q % 4, :, 256:], NN, preferred_element_type=F32
-        )
-        bound = jnp.where(sym, (641 - p) // 2, (640 - p) // 2)
-        first = row_mask((place < bound) == (p % 2 == 0), 48)
-        is_sym = row_mask(sym[:, 256:], 48)
-        low = jnp.where(first[:, :256], low[:48], low[48:])
-        high = jnp.where(
-            is_sym,
-            jnp.where(first[:, 256:], high[0:48], high[48:96]),
-            jnp.where(first[:, 256:], high[96:144], high[144:192]),
-        )
-        chosen = jnp.concatenate([low, high], axis=1).astype(BF16)
-        spectrum_ref[q] = chosen
-        all_rows.append(chosen.astype(F32))
-    group = 0
-    for level, table_ref, count in ((0, one_ref, 4), (1, two_ref, 2), (2, three_ref, 1)):
-        size = table_ref.shape[1]
-        half = size // 2
-        limit = info_ref[11 + level]
-        lane = lax.broadcasted_iota(jnp.int32, (1, size), 1)
-        is_sym = lane < half
-        sym_rows = row_mask(is_sym, 48)
-        extra = jnp.where(is_sym, 2 * lane, 2 * (lane - half) + 1)
-        many = 16 * count
-        wide = lax.broadcasted_iota(jnp.int32, (many, 128), 1)
-        for k, (q, p) in enumerate(zip(slots, orders)):
-            rows = all_rows[k]
-            later = pltpu.roll(rows, 512 - 321 + half, 1)[:, :size]
-            keep = row_mask(p + extra <= limit, 48)
-            kept = jnp.where(keep, jnp.where(sym_rows, rows[:, :size], later), 0.0)
-            both = jnp.concatenate(
-                [kept, jnp.where(sym_rows, kept, -kept), jnp.zeros((32, size), F32)], axis=0
-            ).astype(BF16)
-            value = lax.dot_general(table_ref[k], both, NT, preferred_element_type=F32)
-            for sign in range(2):
-                for c in range(2):
-                    packed = None
-                    for b in range(5):
-                        part = value[many * b : many * b + many]
-                        move = 24 * (b - 2 * sign - c) % 128
-                        if move:
-                            part = pltpu.roll(part, move, 1)
-                        packed = part if b == 0 else jnp.where(wide >= 24 * b, part, packed)
-                    for a in range(count):
-                        start = sign * 16 * 144 + 20 * (group + a) + 10 * c + q
-                        pack_ref[pl.ds(start, 16, stride=144), :] = packed[16 * a : 16 * a + 16]
-        group += count
-
-    @pl.when(step == pl.num_programs(0) - 1)
-    def _():
-        for d in range(16):
-            wire_ref[d] = pack_ref[144 * d : 144 * d + 144, :].astype(BF16)
-            wire_ref[31 - d] = pack_ref[144 * (16 + d) : 144 * (17 + d), :].astype(BF16)
-        leaving = [
-            pltpu.make_async_copy(wire_ref, wire_hbm, wire_sem),
-            pltpu.make_async_copy(spectrum_ref, spectrum_hbm, spectrum_sem),
-        ]
-        for copy in leaving:
-            copy.start()
-        for copy in leaving:
-            copy.wait()
+
+    def two_slots(step, carry):
+        slots = [2 * step, 2 * step + 1]
+        orders = [info_ref[1 + q] for q in slots]
+        for q in slots:
+            for k, source in enumerate(lows):
+                pltpu.make_async_copy(
+                    source.at[pl.ds(0, 160), :], block_ref.at[q, pl.ds(0, 160), :], block_sem.at[q, k]
+                ).wait()
+        all_rows = []
+        for q, p in zip(slots, orders):
+            low = lax.dot_general(
+                waves_ref[q, :96, :], block_ref[q, :, :256], NN, preferred_element_type=F32
+            )
+            high = lax.dot_general(
+                waves_ref[q], block_ref[q, :, 256:], NN, preferred_element_type=F32
+            )
+            bound = jnp.where(sym, (641 - p) // 2, (640 - p) // 2)
+            first = row_mask((place < bound) == (p % 2 == 0), 48)
+            is_sym = row_mask(sym[:, 256:], 48)
+            low = jnp.where(first[:, :256], low[:48], low[48:])
+            high = jnp.where(
+                is_sym,
+                jnp.where(first[:, 256:], high[0:48], high[48:96]),
+                jnp.where(first[:, 256:], high[96:144], high[144:192]),
+            )
+            chosen = jnp.concatenate([low, high], axis=1).astype(BF16)
+            spectrum_ref[q] = chosen
+            all_rows.append(chosen.astype(F32))
+        group = 0
+        for level, table_ref, count in ((0, one_ref, 4), (1, two_ref, 2), (2, three_ref, 1)):
+            size = table_ref.shape[1]
+            half = size // 2
+            limit = info_ref[11 + level]
+            lane = lax.broadcasted_iota(jnp.int32, (1, size), 1)
+            is_sym = lane < half
+            sym_rows = row_mask(is_sym, 48)
+            extra = jnp.where(is_sym, 2 * lane, 2 * (lane - half) + 1)
+            many = 16 * count
+            wide = lax.broadcasted_iota(jnp.int32, (many, 128), 1)
+            for k, (q, p) in enumerate(zip(slots, orders)):
+                rows = all_rows[k]
+                later = pltpu.roll(rows, 512 - 321 + half, 1)[:, :size]
+                keep = row_mask(p + extra <= limit, 48)
+                kept = jnp.where(keep, jnp.where(sym_rows, rows[:, :size], later), 0.0)
+                both = jnp.concatenate(
+                    [kept, jnp.where(sym_rows, kept, -kept), jnp.zeros((32, size), F32)], axis=0
+                ).astype(BF16)
+                value = lax.dot_general(table_ref[q], both, NT, preferred_element_type=F32)
+                for sign in range(2):
+                    for c in range(2):
+                        packed = None
+                        for b in range(5):
+                            part = value[many * b : many * b + many]
+                            move = 24 * (b - 2 * sign - c) % 128
+                            if move:
+                                part = pltpu.roll(part, move, 1)
+                            packed = part if b == 0 else jnp.where(wide >= 24 * b, part, packed)
+                        for a in range(count):
+                            start = sign * 16 * 144 + 20 * (group + a) + 10 * c + q
+                            pack_ref[pl.ds(start, 16, stride=144), :] = packed[16 * a : 16 * a + 16]
+            group += count
+
+        return carry
+
+    lax.fori_loop(0, 5, two_slots, 0)
+    for d in range(16):
+        wire_ref[d] = pack_ref[144 * d : 144 * d + 144, :].astype(BF16)
+        wire_ref[31 - d] = pack_ref[144 * (16 + d) : 144 * (17 + d), :].astype(BF16)
+    leaving = [
+        pltpu.make_async_copy(wire_ref, wire_hbm, out_sem.at[1]),
+        pltpu.make_async_copy(spectrum_ref, spectrum_hbm, out_sem.at[2]),
+    ]
+    for copy in leaving:
+        copy.start()
+    for copy in leaving:
+        copy.wait()
+    waves_out.wait()
 
 
 def rest_kernel(
@@ -637,50 +647,40 @@
         name="turn_tables",
     )(*synths)
 
-    waves = call(
-        lanes_kernel,
-        jax.ShapeDtypeStruct((10, 192, 640), BF16),
-        18,
-        in_specs=[vmem],
-        out_specs=vmem,
+    info = jnp.concatenate(
+        [fld_at.reshape(1), lax.dynamic_slice_in_dim(assign_after, lat_at * 10, 10), limits]
+    )
+    spectrum, level_wire, waves = call(
+        level_kernel,
+        [
+            jax.ShapeDtypeStruct((10, 2 * fields, 512), BF16),
+            jax.ShapeDtypeStruct((32, 144, 128), BF16),
+            jax.ShapeDtypeStruct((10, 192, 640), BF16),
+        ],
+        60,
+        in_specs=[pl.BlockSpec(memory_space=pltpu.SMEM)] + [hbm] * 12,
+        out_specs=[hbm, hbm, hbm],
         scratch_shapes=[
             pltpu.VMEM((5, fields * rows, 128), F32),
             pltpu.VMEM((5, fields * rows, 128), F32),
+            pltpu.VMEM((10, 192, 640), BF16),
+            pltpu.VMEM((10, 640, 512), BF16),
+        ]
+        + [pltpu.VMEM(t.shape, BF16) for t in turned]
+        + [
+            pltpu.VMEM((10, 2 * fields, 512), BF16),
+            pltpu.VMEM((32 * 144, 128), F32),
+            pltpu.VMEM((32, 144, 128), BF16),
+            pltpu.VMEM((32, 40, 1024), BF16),
+            pltpu.SemaphoreType.DMA((2,)),
+            pltpu.SemaphoreType.DMA((10, 4)),
+            pltpu.SemaphoreType.DMA((3,)),
+            pltpu.SemaphoreType.DMA((3,)),
         ],
-        name="lanes",
-    )(wire)
-
-    info = jnp.concatenate(
-        [fld_at.reshape(1), lax.dynamic_slice_in_dim(assign_after, lat_at * 10, 10), limits]
-    )
-    spectrum, level_wire = call(
-        slot_kernel,
-        [
-            jax.ShapeDtypeStruct((10, 2 * fields, 512), BF16),
-            jax.ShapeDtypeStruct((32, 144, 128), BF16),
-        ],
-        60,
-        grid_spec=pltpu.PrefetchScalarGridSpec(
-            num_scalar_prefetch=1,
-            grid=(5,),
-            in_specs=[pl.BlockSpec((2, 192, 640), lambda q, *_: (q, 0, 0))]
-            + [hbm] * 8
-            + [pl.BlockSpec((2,) + t.shape[1:], lambda q, *_: (q, 0, 0)) for t in turned],
-            out_specs=[hbm, hbm],
-            scratch_shapes=[
-                pltpu.VMEM((10, 2 * fields, 512), BF16),
-                pltpu.VMEM((4, 640, 512), BF16),
-                pltpu.VMEM((32 * 144, 128), F32),
-                pltpu.VMEM((32, 144, 128), BF16),
-                pltpu.SemaphoreType.DMA(()),
-                pltpu.SemaphoreType.DMA((4, 4)),
-                pltpu.SemaphoreType.DMA(()),
-            ],
-        ),
-        name="slots",
+        name="levels",
     )(
         info,
-        waves,
+        wire,
         low,
         low_left,
         low_right,

time: 144 us -> 151 us (1.049)
  waiting for transfers between devices: 54.1 us -> 59.8 us
  Pallas kernels: 51.2 us -> 53 us
    ppermute x1, waiting for transfers between devices: 0.01 us -> 5.36 us  [on_device(): low_right = lax.ppermute(low, 'fld', left)]
    pallas_call x2 -> x1, Pallas kernels: 15.8 us -> 17.5 us  [on_device(): call(level_kernel, [jax.ShapeDtypeStruct((10, 2 * fields, 512), BF16), ja...]
  transfers between devices with their start and end apart: 11 -> 11, of which waited for: 5 -> 6; matrix products, arithmetic and copies ran while one was open for 2% -> 2% of each run, Pallas kernels for 15% -> 11%
where the time goes in v5:
time: 151 us
  waiting for transfers between devices  59.8 us (40%)
  Pallas kernels  53 us (35%)
  starting transfers between devices  29.1 us (19%)
  local copies, waits for them, and re-layouts  5.24 us (3%)
  other arithmetic  2.53 us (2%)
    ppermute x1, waiting for transfers between devices, on_device(): low_far = lax.ppermute(low_left, 'fld', right)  17.6 us
    pallas_call x1, Pallas kernels, on_device(): call(level_kernel, [jax.ShapeDtypeStruct((10, 2 * fields, 512), BF16), ja...  17.5 us
    ppermute x1, waiting for transfers between devices, on_device(): low_left = lax.ppermute(low, 'fld', right)  16.7 us
    pallas_call x1, Pallas kernels, on_device(): call(dft_kernel, jax.ShapeDtypeStruct((32, 40, 1024), BF16), 60, in_specs...  11.3 us
    ppermute x1, waiting for transfers between devices, on_device(): rest_far = lax.ppermute(rest, 'fld', across)  10.8 us
    all_to_all x1, starting transfers between devices, on_device(): wire = lax.all_to_all(wire, 'lat', split_axis=0, concat_axis=0, tiled=True)  9.74 us
    ppermute x1, waiting for transfers between devices, on_device(): rest_left = lax.ppermute(rest, 'fld', right)  9.23 us
    pallas_call x1, Pallas kernels, on_device(): call(turn_tables_kernel, [jax.ShapeDtypeStruct(t.shape, BF16) for t in sy...  8.72 us
  transfers between devices with their start and end apart: 11, of which 6 were waited for; matrix products, arithmetic and copies ran while one was open for 2% of the time, Pallas kernels for 11%

profile of v5, /device:TPU:1, one launch (start us, length us, event | category | flops | bytes accessed | tf_op | source)
XLA Modules:
  0.0 150.6 jit_solution(7463449428177384539)
XLA Ops:
  0.7 2.5 %pack.1 = (bf16[800,512]{1,0:T(8,128)(2,1)}, bf16[800,512]{1,0:T(8,128)(2,1)}) custom-call(bf16[10,160,641]{2,1,0:T(8,128)(2,1)} %bitcast.12), custom_call_target="tpu_custom_call" | custom-call | tf_op jit(solution)/shard_map/pack/pallas_call | solution.py:558
  3.6 0.6 pad_maximum_fusion.4.waves_ref
  4.2 11.3 %dft.1 = bf16[32,40,1024]{2,1,0:T(8,128)(2,1)} custom-call(s32[1]{0:T(128)} %bitcast.2.info_ref, f32[2,768]{1,0:T(2,128)} %pad_maximum_fusion.4.waves_ref, bf16[960,2560]{1,0:T(8,128)(2,1)} %bitcast.14), custom_call_target="tpu_custom_call" | custom-call | tf_op jit(solution)/shard_map/dft/pallas_call | solution.py:593
  15.5 9.7 %all-to-all-start = ((bf16[32,40,1024]{2,1,0:T(8,128)(2,1)}), bf16[32,40,1024]{2,1,0:T(8,128)(2,1)S(1)}, u32[]{:S(2)}, u32[]{:S(2)}) async-start(bf16[32,40,1024]{2,1,0:T(8,128)(2,1)} %dft.1), calls=%async_computation | async-start | bytes 5242880 | tf_op jit(solution)/shard_map/all_to_all | solution.py:617
  25.3 1.3 collective-permute-start
  26.6 1.5 collective-permute-start.4
  28.0 1.3 collective-permute-start.1
  29.3 0.2 collective-permute-start.3
  29.5 16.7 %collective-permute-done.left_low = bf16[800,512]{1,0:T(8,128)(2,1)} collective-permute-done((bf16[800,512]{1,0:T(8,128)(2,1)S(1)}, bf16[800,512]{1,0:T(8,128)(2,1)}, u32[]{:S(2)}, u32[]{:S(2)}) %collective-permute-start) | collective-permute-done | bytes 819232 | tf_op jit(solution)/shard_map/ppermute | solution.py:576
  46.2 2.7 %collective-permute-start.5 = (bf16[800,512]{1,0:T(8,128)(2,1)}, bf16[800,512]{1,0:T(8,128)(2,1)}, u32[]{:S(2)}, u32[]{:S(2)}) collective-permute-start(bf16[800,512]{1,0:T(8,128)(2,1)} %collective-permute-done.4.right_high), channel_id=1, source_target_pairs={{0,3},{1,0},{2,1},{3,2},{4,7},{5,4},{6,5},{7,6},{8,11},{9,8},{10,9... | collective-permute-start | bytes 2457608 | tf_op jit(solution)/shard_map/ppermute | solution.py:581
  49.0 8.7 %turn_tables.1 = (bf16[10,320,320]{2,1,0:T(8,128)(2,1)}, bf16[10,160,160]{2,1,0:T(8,128)(2,1)}, bf16[10,80,80]{2,1,0:T(8,128)(2,1)}) custom-call(bf16[10,320,320]{2,1,0:T(8,128)(2,1)} %one_ref, bf16[10,160,160]{2,1,0:T(8,128)(2,1)} %two_ref, bf16[10,80,80]{2,1,0:T(8,128)(2,1)} %three_ref), custom_call_target="tpu_custom_call" | custom-call | tf_op jit(solution)/shard_map/turn_tables/pallas_call | solution.py:639
  57.7 0.6 pad_add_fusion.info_ref
  58.4 5.4 %collective-permute-done.1.right_low = bf16[800,512]{1,0:T(8,128)(2,1)} collective-permute-done((bf16[800,512]{1,0:T(8,128)(2,1)S(1)}, bf16[800,512]{1,0:T(8,128)(2,1)}, u32[]{:S(2)}, u32[]{:S(2)}) %collective-permute-start.1) | collective-permute-done | bytes 819232 | tf_op jit(solution)/shard_map/ppermute | solution.py:578
  63.8 17.6 %collective-permute-done.2.far_low = bf16[800,512]{1,0:T(8,128)(2,1)} collective-permute-done((bf16[800,512]{1,0:T(8,128)(2,1)}, bf16[800,512]{1,0:T(8,128)(2,1)}, u32[]{:S(2)}, u32[]{:S(2)}) %collective-permute-start.2) | collective-permute-done | bytes 819232 | tf_op jit(solution)/shard_map/ppermute | solution.py:580
  81.4 1.5 %copy-done.5 = bf16[32,40,1024]{2,1,0:T(8,128)(2,1)} copy-done((bf16[32,40,1024]{2,1,0:T(8,128)(2,1)}, bf16[32,40,1024]{2,1,0:T(8,128)(2,1)S(1)}, u32[]{:S(2)}) %copy-start.5) | copy-done | bytes 2621464
  82.9 17.5 %levels.1 = (bf16[10,48,512]{2,1,0:T(8,128)(2,1)}, bf16[32,144,128]{2,1,0:T(8,128)(2,1)}, bf16[10,192,640]{2,1,0:T(8,128)(2,1)}) custom-call(s32[14]{0:T(128)} %pad_add_fusion.info_ref, bf16[32,40,1024]{2,1,0:T(8,128)(2,1)} %copy-done.5, bf16[800,512]{1,0:T(8,128)(2,1)} %get-tuple-element.36.own_low, bf16[800,512]{1,0:T(8,128)(2,1)} %collective-permute-done.left_low, ...), custom_call_target="tpu_custom_call" | custom-call | tf_op jit(solution)/shard_map/levels/pallas_call | solution.py:653
  100.4 8.5 %all-to-all-start.1 = ((bf16[32,144,128]{2,1,0:T(8,128)(2,1)}), bf16[32,144,128]{2,1,0:T(8,128)(2,1)}, u32[]{:S(2)}, u32[]{:S(2)}) async-start(bf16[32,144,128]{2,1,0:T(8,128)(2,1)} %get-tuple-element.51), calls=%async_computation.1 | async-start | bytes 2359296 | tf_op jit(solution)/shard_map/all_to_all | solution.py:704
  108.9 2.1 %pack_rest.1.own_ref = bf16[1760,128]{1,0:T(8,128)(2,1)} custom-call(bf16[10,160,641]{2,1,0:T(8,128)(2,1)} %bitcast.13), custom_call_target="tpu_custom_call" | custom-call | tf_op jit(solution)/shard_map/pack_rest/pallas_call | solution.py:619
  111.0 1.3 collective-permute-start.6
  112.3 1.6 %collective-permute-start.7 = (bf16[1760,128]{1,0:T(8,128)(2,1)}, bf16[1760,128]{1,0:T(8,128)(2,1)S(1)}, u32[]{:S(2)}, u32[]{:S(2)}) collective-permute-start(bf16[1760,128]{1,0:T(8,128)(2,1)} %pack_rest.1.own_ref), channel_id=1, source_target_pairs={{0,3},{1,0},{2,1},{3,2},{4,7},{5,4},{6,5},{7,6},{8,11},{9,8},{10,9... | collective-permute-start | bytes 1351688 | tf_op jit(solution)/shard_map/ppermute | solution.py:634
  113.8 1.2 collective-permute-start.8
  115.0 9.2 %collective-permute-done.6.left_ref = bf16[1760,128]{1,0:T(8,128)(2,1)S(1)} collective-permute-done((bf16[1760,128]{1,0:T(8,128)(2,1)}, bf16[1760,128]{1,0:T(8,128)(2,1)S(1)}, u32[]{:S(2)}, u32[]{:S(2)}) %collective-permute-start.6) | collective-permute-done | bytes 450592 | tf_op jit(solution)/shard_map/ppermute | solution.py:633
  124.2 10.8 %collective-permute-done.8.far_ref = bf16[1760,128]{1,0:T(8,128)(2,1)} collective-permute-done((bf16[1760,128]{1,0:T(8,128)(2,1)}, bf16[1760,128]{1,0:T(8,128)(2,1)}, u32[]{:S(2)}, u32[]{:S(2)}) %collective-permute-start.8) | collective-permute-done | bytes 450592 | tf_op jit(solution)/shard_map/ppermute | solution.py:635
  135.0 1.0 copy-done.1
  136.1 4.1 %rest.1 = bf16[10,48,129]{2,1,0:T(8,128)(2,1)S(1)} custom-call(s32[14]{0:T(128)S(1)} %copy-done.4, bf16[10,192,640]{2,1,0:T(8,128)(2,1)S(1)} %copy-done, bf16[1760,128]{1,0:T(8,128)(2,1)S(1)} %copy-done.1, bf16[1760,128]{1,0:T(8,128)(2,1)S(1)} %collective-permute-done.6.left_ref, bf16[1760,128]{1,0:T(8,128)(2,1)S(1)} %collective-permute-done.7.right_ref, ...), custom_call_target="tpu_custom_call" | custom-call | tf_op jit(solution)/shard_map/rest/pallas_call | solution.py:695
  140.1 0.7 copy-done.2
  140.8 0.1 convert_element_type.12
  141.0 0.1 reshape.45.waves_ref
  141.1 2.3 %inverse_tables.1.table_ref = bf16[2240,768]{1,0:T(8,128)(2,1)S(1)} custom-call(f32[1,768]{1,0:T(1,128)S(1)} %reshape.45.waves_ref), custom_call_target="tpu_custom_call" | custom-call | tf_op jit(solution)/shard_map/inverse_tables/pallas_call | solution.py:709
  143.5 1.1 pad_maximum_fusion
  144.6 1.4 copy.14
  146.0 4.4 %inverse.1 = (f32[20,24,1280]{2,1,0:T(8,128)}, f32[10,24,640]{2,1,0:T(8,128)}, f32[5,24,320]{2,1,0:T(8,128)}) custom-call(s32[1]{0:T(128)} %bitcast.6.info_ref, bf16[32,144,128]{2,1,0:T(8,128)(2,1)} %all-to-all-done.1.wire_ref, bf16[2240,768]{1,0:T(8,128)(2,1)S(1)} %inverse_tables.1.table_ref), custom_call_target="tpu_custom_call" | custom-call | tf_op jit(solution)/shard_map/inverse/pallas_call | solution.py:721
  (31 shorter events, 0.7 us)
Async XLA Ops:
  0.6 2.5 %copy-start.7 = (s32[320]{0:T(512)S(1)}, s32[320]{0:T(512)}, u32[]{:S(2)}) copy-start(s32[320]{0:T(512)} %param.8) | copy-start | bytes 3844
  15.5 9.8 %copy-start.6 = (bf16[800,512]{1,0:T(8,128)(2,1)S(1)}, bf16[800,512]{1,0:T(8,128)(2,1)}, u32[]{:S(2)}) copy-start(bf16[800,512]{1,0:T(8,128)(2,1)} %get-tuple-element.36.own_low) | copy-start | bytes 2457604
  15.5 65.8 %all-to-all-start = ((bf16[32,40,1024]{2,1,0:T(8,128)(2,1)}), bf16[32,40,1024]{2,1,0:T(8,128)(2,1)S(1)}, u32[]{:S(2)}, u32[]{:S(2)}) async-start(bf16[32,40,1024]{2,1,0:T(8,128)(2,1)} %dft.1), calls=%async_computation | async-start | bytes 5242880 | tf_op jit(solution)/shard_map/all_to_all | solution.py:617
  25.3 32.4 %copy-start.8 = (s32[3]{0:T(128)S(1)}, s32[3]{0:T(128)}, u32[]{:S(2)}) copy-start(s32[3]{0:T(128)} %param.9) | copy-start | bytes 40
  25.3 21.0 %collective-permute-start = (bf16[800,512]{1,0:T(8,128)(2,1)S(1)}, bf16[800,512]{1,0:T(8,128)(2,1)}, u32[]{:S(2)}, u32[]{:S(2)}) collective-permute-start(bf16[800,512]{1,0:T(8,128)(2,1)S(1)} %copy-done.6), channel_id=1, source_target_pairs={{0,1},{1,2},{2,3},{3,0},{4,5},{5,6},{6,7},{7,4},{8,9},{9,10},{10,1... | collective-permute-start | bytes 2457608 | tf_op jit(solution)/shard_map/ppermute | solution.py:576
  26.6 19.7 %collective-permute-start.4 = (bf16[800,512]{1,0:T(8,128)(2,1)}, bf16[800,512]{1,0:T(8,128)(2,1)}, u32[]{:S(2)}, u32[]{:S(2)}) collective-permute-start(bf16[800,512]{1,0:T(8,128)(2,1)} %get-tuple-element.37.own_high), channel_id=1, source_target_pairs={{0,3},{1,0},{2,1},{3,2},{4,7},{5,4},{6,5},{7,6},{8,11},{9,8},{10,9... | collective-permute-start | bytes 2457608 | tf_op jit(solution)/shard_map/ppermute | solution.py:577
  28.0 35.7 %collective-permute-start.1 = (bf16[800,512]{1,0:T(8,128)(2,1)S(1)}, bf16[800,512]{1,0:T(8,128)(2,1)}, u32[]{:S(2)}, u32[]{:S(2)}) collective-permute-start(bf16[800,512]{1,0:T(8,128)(2,1)S(1)} %copy-done.6), channel_id=1, source_target_pairs={{0,3},{1,0},{2,1},{3,2},{4,7},{5,4},{6,5},{7,6},{8,11},{9,8},{10,9... | collective-permute-start | bytes 2457608 | tf_op jit(solution)/shard_map/ppermute | solution.py:578
  29.3 34.5 %collective-permute-start.3 = (bf16[800,512]{1,0:T(8,128)(2,1)}, bf16[800,512]{1,0:T(8,128)(2,1)}, u32[]{:S(2)}, u32[]{:S(2)}) collective-permute-start(bf16[800,512]{1,0:T(8,128)(2,1)} %get-tuple-element.37.own_high), channel_id=1, source_target_pairs={{0,1},{1,2},{2,3},{3,0},{4,5},{5,6},{6,7},{7,4},{8,9},{9,10},{10,1... | collective-permute-start | bytes 2457608 | tf_op jit(solution)/shard_map/ppermute | solution.py:579
  46.2 35.1 %collective-permute-start.2 = (bf16[800,512]{1,0:T(8,128)(2,1)}, bf16[800,512]{1,0:T(8,128)(2,1)}, u32[]{:S(2)}, u32[]{:S(2)}) collective-permute-start(bf16[800,512]{1,0:T(8,128)(2,1)} %collective-permute-done.left_low), channel_id=1, source_target_pairs={{0,1},{1,2},{2,3},{3,0},{4,5},{5,6},{6,7},{7,4},{8,9},{9,10},{10,1... | collective-permute-start | bytes 2457608 | tf_op jit(solution)/shard_map/ppermute | solution.py:580
  46.2 35.1 %collective-permute-start.5 = (bf16[800,512]{1,0:T(8,128)(2,1)}, bf16[800,512]{1,0:T(8,128)(2,1)}, u32[]{:S(2)}, u32[]{:S(2)}) collective-permute-start(bf16[800,512]{1,0:T(8,128)(2,1)} %collective-permute-done.4.right_high), channel_id=1, source_target_pairs={{0,3},{1,0},{2,1},{3,2},{4,7},{5,4},{6,5},{7,6},{8,11},{9,8},{10,9... | collective-permute-start | bytes 2457608 | tf_op jit(solution)/shard_map/ppermute | solution.py:581
  81.4 1.5 %copy-start.5 = (bf16[32,40,1024]{2,1,0:T(8,128)(2,1)}, bf16[32,40,1024]{2,1,0:T(8,128)(2,1)S(1)}, u32[]{:S(2)}) copy-start(bf16[32,40,1024]{2,1,0:T(8,128)(2,1)S(1)} %all-to-all-done.arrived_hbm) | copy-start | bytes 7864324
  100.4 34.6 %copy-start = (bf16[10,192,640]{2,1,0:T(8,128)(2,1)S(1)}, bf16[10,192,640]{2,1,0:T(8,128)(2,1)}, u32[]{:S(2)}) copy-start(bf16[10,192,640]{2,1,0:T(8,128)(2,1)} %get-tuple-element.48.waves_ref) | copy-start | bytes 7372804
  100.4 34.6 %copy-start.4 = (s32[14]{0:T(128)S(1)}, s32[14]{0:T(128)}, u32[]{:S(2)}) copy-start(s32[14]{0:T(128)} %pad_add_fusion.info_ref) | copy-start | bytes 172
  100.4 45.6 %all-to-all-start.1 = ((bf16[32,144,128]{2,1,0:T(8,128)(2,1)}), bf16[32,144,128]{2,1,0:T(8,128)(2,1)}, u32[]{:S(2)}, u32[]{:S(2)}) async-start(bf16[32,144,128]{2,1,0:T(8,128)(2,1)} %get-tuple-element.51), calls=%async_computation.1 | async-start | bytes 2359296 | tf_op jit(solution)/shard_map/all_to_all | solution.py:704
  111.0 13.2 %collective-permute-start.6 = (bf16[1760,128]{1,0:T(8,128)(2,1)}, bf16[1760,128]{1,0:T(8,128)(2,1)S(1)}, u32[]{:S(2)}, u32[]{:S(2)}) collective-permute-start(bf16[1760,128]{1,0:T(8,128)(2,1)} %pack_rest.1.own_ref), channel_id=1, source_target_pairs={{0,1},{1,2},{2,3},{3,0},{4,5},{5,6},{6,7},{7,4},{8,9},{9,10},{10,1... | collective-permute-start | bytes 1351688 | tf_op jit(solution)/shard_map/ppermute | solution.py:633
  112.3 12.0 %collective-permute-start.7 = (bf16[1760,128]{1,0:T(8,128)(2,1)}, bf16[1760,128]{1,0:T(8,128)(2,1)S(1)}, u32[]{:S(2)}, u32[]{:S(2)}) collective-permute-start(bf16[1760,128]{1,0:T(8,128)(2,1)} %pack_rest.1.own_ref), channel_id=1, source_target_pairs={{0,3},{1,0},{2,1},{3,2},{4,7},{5,4},{6,5},{7,6},{8,11},{9,8},{10,9... | collective-permute-start | bytes 1351688 | tf_op jit(solution)/shard_map/ppermute | solution.py:634
  113.8 21.2 %collective-permute-start.8 = (bf16[1760,128]{1,0:T(8,128)(2,1)}, bf16[1760,128]{1,0:T(8,128)(2,1)}, u32[]{:S(2)}, u32[]{:S(2)}) collective-permute-start(bf16[1760,128]{1,0:T(8,128)(2,1)} %pack_rest.1.own_ref), channel_id=1, source_target_pairs={{0,2},{1,3},{2,0},{3,1},{4,6},{5,7},{6,4},{7,5},{8,10},{9,11},{10,... | collective-permute-start | bytes 1351688 | tf_op jit(solution)/shard_map/ppermute | solution.py:635
  135.0 1.0 copy-start.1
  140.1 0.7 copy-start.2
  141.1 2.4 %copy-start.3 = (bf16[10,48,129]{2,1,0:T(8,128)(2,1)S(1)}, bf16[10,48,129]{2,1,0:T(8,128)(2,1)}, u32[]{:S(2)}) copy-start(bf16[10,48,129]{2,1,0:T(8,128)(2,1)} %copy-done.2) | copy-start | bytes 371524

commit v6 on v5

--- a/solution.py
+++ b/solution.py
@@ -124,19 +124,27 @@
     shift = lax.rem(turn_by, 128)
     tile_shift = lax.div(turn_by, 128)
     lane = lax.broadcasted_iota(jnp.int32, (40, 128), 1)
+    for at, table_ref, folded_ref in ((0, even_ref, add_ref), (768, odd_ref, sub_ref)):
+        turned_ref[:, at : at + 768] = lax.dot_general(
+            folded_ref[...], table_ref[...], NN, preferred_element_type=F32
+        ).astype(BF16)
     leaving = []
     for k in range(2):
-        results = []
-        for table_ref, folded_ref in ((even_ref, add_ref), (odd_ref, sub_ref)):
-            for t in range(3):
-                columns = slice(k * 384 + 128 * t, k * 384 + 128 * t + 128)
-                turned_ref[128 * t : 128 * t + 128, :] = lax.dot_general(
-                    same, table_ref[:, columns], NT, preferred_element_type=F32
-                ).astype(BF16)
-            results.append(
-                lax.dot_general(turned_ref[...], folded_ref[...], NT, preferred_element_type=F32)
+        even, odd = (
+            jnp.concatenate(
+                [
+                    lax.dot_general(
+                        same,
+                        turned_ref[:, at + 128 * t : at + 128 * t + 128],
+                        NT,
+                        preferred_element_type=F32,
+                    )
+                    for t in range(3)
+                ],
+                axis=0,
             )
-        even, odd = results
+            for at in (384 * k, 768 + 384 * k)
+        )
         for d in range(16):
             one = even[24 * d : 24 * d + 24]
             two = odd[24 * d : 24 * d + 24]
@@ -145,10 +153,15 @@
             for t in range(8):
                 tile = jnp.where(lane < shift, tiles[t - 1], tiles[t])
                 place = pl.multiple_of(lax.rem(tile_shift + t, 8) * 128, 128)
-                out_ref[k * 16 + d, :, pl.ds(place, 128)] = tile.astype(BF16)
-        part = pl.ds(16 * k, 16)
-        leaving.append(pltpu.make_async_copy(out_ref.at[part], wire_hbm.at[part], out_sem.at[k]))
-        leaving[-1].start()
+                out_ref[16 * k + d, :, pl.ds(place, 128)] = tile.astype(BF16)
+            if d % 8 == 7:
+                part = pl.ds(16 * k + d - 7, 8)
+                leaving.append(
+                    pltpu.make_async_copy(
+                        out_ref.at[part], wire_hbm.at[part], out_sem.at[2 * k + d // 8]
+                    )
+                )
+                leaving[-1].start()
     for copy in leaving:
         copy.wait()
 
@@ -259,6 +272,7 @@
     arrived_sem,
     block_sem,
     table_sem,
+    spectrum_sem,
     out_sem,
 ):
     x = info_ref[0]
@@ -286,12 +300,6 @@
             ((one_hbm, one_ref), (two_hbm, two_ref), (three_hbm, three_ref))
         )
     ]
-    for q in range(10):
-        for k, source in enumerate(lows if q < 5 else highs):
-            block_copy(source, q, pl.multiple_of(((x + k) % 4) * 160, 160), k).start()
-        if q == 1:
-            for copy in tables:
-                copy.start()
     for row in range(140, 144):
         pack_ref[pl.ds(row, 32, stride=144), :] = jnp.zeros((32, 128), F32)
 
@@ -299,6 +307,13 @@
     lane = lax.broadcasted_iota(jnp.int32, (40, 128), 1)
     for half, target in ((0, north_ref), (16, south_ref)):
         arriving[half // 16].wait()
+        if half:
+            for q in range(10):
+                for k, source in enumerate(lows if q < 5 else highs):
+                    block_copy(source, q, pl.multiple_of(((x + k) % 4) * 160, 160), k).start()
+                if q == 1:
+                    for copy in tables:
+                        copy.start()
         for f in range(fields):
             offset = 40 * f % 128
             tiles = []
@@ -385,6 +400,9 @@
             )
             chosen = jnp.concatenate([low, high], axis=1).astype(BF16)
             spectrum_ref[q] = chosen
+            pltpu.make_async_copy(
+                spectrum_ref.at[q], spectrum_hbm.at[q], spectrum_sem.at[q]
+            ).start()
             all_rows.append(chosen.astype(F32))
         group = 0
         for level, table_ref, count in ((0, one_ref, 4), (1, two_ref, 2), (2, three_ref, 1)):
@@ -426,14 +444,11 @@
     for d in range(16):
         wire_ref[d] = pack_ref[144 * d : 144 * d + 144, :].astype(BF16)
         wire_ref[31 - d] = pack_ref[144 * (16 + d) : 144 * (17 + d), :].astype(BF16)
-    leaving = [
-        pltpu.make_async_copy(wire_ref, wire_hbm, out_sem.at[1]),
-        pltpu.make_async_copy(spectrum_ref, spectrum_hbm, out_sem.at[2]),
-    ]
-    for copy in leaving:
-        copy.start()
-    for copy in leaving:
-        copy.wait()
+    wire_out = pltpu.make_async_copy(wire_ref, wire_hbm, out_sem.at[1])
+    wire_out.start()
+    for q in range(10):
+        pltpu.make_async_copy(spectrum_ref.at[q], spectrum_hbm.at[q], spectrum_sem.at[q]).wait()
+    wire_out.wait()
     waves_out.wait()
 
 
@@ -603,11 +618,11 @@
             pltpu.VMEM((lon // 2, 768), BF16),
             pltpu.VMEM((1024, lon // 2), BF16),
             pltpu.VMEM((1024, lon // 2), BF16),
-            pltpu.VMEM((384, lon // 2), BF16),
+            pltpu.VMEM((1024, 1536), BF16),
             pltpu.VMEM((80, 768), F32),
             pltpu.VMEM((80, 768), F32),
             pltpu.SemaphoreType.DMA(()),
-            pltpu.SemaphoreType.DMA((2,)),
+            pltpu.SemaphoreType.DMA((4,)),
         ],
         name="dft",
     )((lat_at % 16 * 40).reshape(1), forward_waves, grid_fields.reshape(fields * rows, lon))
@@ -675,7 +690,8 @@
             pltpu.SemaphoreType.DMA((2,)),
             pltpu.SemaphoreType.DMA((10, 4)),
             pltpu.SemaphoreType.DMA((3,)),
-            pltpu.SemaphoreType.DMA((3,)),
+            pltpu.SemaphoreType.DMA((10,)),
+            pltpu.SemaphoreType.DMA((2,)),
         ],
         name="levels",
     )(

time: 151 us -> 149 us (0.987)
  Pallas kernels: 53 us -> 50.7 us
    pallas_call x1, Pallas kernels: 17.5 us -> 15.7 us  [on_device(): call(level_kernel, [jax.ShapeDtypeStruct((10, 2 * fields, 512), BF16), ja...]
  transfers between devices with their start and end apart: 11 -> 11, of which waited for: 6 -> 6; matrix products, arithmetic and copies ran while one was open for 2% -> 2% of each run, Pallas kernels for 11% -> 12%
where the time goes in v6:
time: 149 us; the launch traced here: 148 us
  waiting for transfers between devices  59.8 us (40%)
  Pallas kernels  50.7 us (34%)
  starting transfers between devices  29.1 us (20%)
  local copies, waits for them, and re-layouts  5.24 us (4%)
  other arithmetic  2.53 us (2%)
    ppermute x1, waiting for transfers between devices, on_device(): low_far = lax.ppermute(low_left, 'fld', right)  17.6 us
    ppermute x1, waiting for transfers between devices, on_device(): low_left = lax.ppermute(low, 'fld', right)  16.7 us
    pallas_call x1, Pallas kernels, on_device(): call(level_kernel, [jax.ShapeDtypeStruct((10, 2 * fields, 512), BF16), ja...  15.7 us
    pallas_call x1, Pallas kernels, on_device(): call(dft_kernel, jax.ShapeDtypeStruct((32, 40, 1024), BF16), 60, in_specs...  10.9 us
    ppermute x1, waiting for transfers between devices, on_device(): rest_far = lax.ppermute(rest, 'fld', across)  10.8 us
    all_to_all x1, starting transfers between devices, on_device(): wire = lax.all_to_all(wire, 'lat', split_axis=0, concat_axis=0, tiled=True)  9.74 us
    ppermute x1, waiting for transfers between devices, on_device(): rest_left = lax.ppermute(rest, 'fld', right)  9.22 us
    pallas_call x1, Pallas kernels, on_device(): call(turn_tables_kernel, [jax.ShapeDtypeStruct(t.shape, BF16) for t in sy...  8.72 us
  transfers between devices with their start and end apart: 11, of which 6 were waited for; matrix products, arithmetic and copies ran while one was open for 2% of the time, Pallas kernels for 12%

profile of v6, /device:TPU:1, one launch (start us, length us, event | category | flops | bytes accessed | tf_op | source)
XLA Modules:
  0.0 148.4 jit_solution(10894649618237191268)
XLA Ops:
  0.7 2.5 %pack.1 = (bf16[800,512]{1,0:T(8,128)(2,1)}, bf16[800,512]{1,0:T(8,128)(2,1)}) custom-call(bf16[10,160,641]{2,1,0:T(8,128)(2,1)} %bitcast.12), custom_call_target="tpu_custom_call" | custom-call | tf_op jit(solution)/shard_map/pack/pallas_call | solution.py:573
  3.6 0.6 pad_maximum_fusion.4.waves_ref
  4.2 10.9 %dft.1 = bf16[32,40,1024]{2,1,0:T(8,128)(2,1)} custom-call(s32[1]{0:T(128)} %bitcast.2.info_ref, f32[2,768]{1,0:T(2,128)} %pad_maximum_fusion.4.waves_ref, bf16[960,2560]{1,0:T(8,128)(2,1)} %bitcast.14), custom_call_target="tpu_custom_call" | custom-call | tf_op jit(solution)/shard_map/dft/pallas_call | solution.py:608
  15.1 9.7 %all-to-all-start = ((bf16[32,40,1024]{2,1,0:T(8,128)(2,1)}), bf16[32,40,1024]{2,1,0:T(8,128)(2,1)S(1)}, u32[]{:S(2)}, u32[]{:S(2)}) async-start(bf16[32,40,1024]{2,1,0:T(8,128)(2,1)} %dft.1), calls=%async_computation | async-start | bytes 5242880 | tf_op jit(solution)/shard_map/all_to_all | solution.py:632
  24.9 1.3 collective-permute-start
  26.2 1.5 collective-permute-start.4
  27.6 1.3 collective-permute-start.1
  28.9 0.2 collective-permute-start.3
  29.1 16.7 %collective-permute-done.left_low = bf16[800,512]{1,0:T(8,128)(2,1)} collective-permute-done((bf16[800,512]{1,0:T(8,128)(2,1)S(1)}, bf16[800,512]{1,0:T(8,128)(2,1)}, u32[]{:S(2)}, u32[]{:S(2)}) %collective-permute-start) | collective-permute-done | bytes 819232 | tf_op jit(solution)/shard_map/ppermute | solution.py:591
  45.9 2.7 %collective-permute-start.5 = (bf16[800,512]{1,0:T(8,128)(2,1)}, bf16[800,512]{1,0:T(8,128)(2,1)}, u32[]{:S(2)}, u32[]{:S(2)}) collective-permute-start(bf16[800,512]{1,0:T(8,128)(2,1)} %collective-permute-done.4.right_high), channel_id=1, source_target_pairs={{0,3},{1,0},{2,1},{3,2},{4,7},{5,4},{6,5},{7,6},{8,11},{9,8},{10,9... | collective-permute-start | bytes 2457608 | tf_op jit(solution)/shard_map/ppermute | solution.py:596
  48.6 8.7 %turn_tables.1 = (bf16[10,320,320]{2,1,0:T(8,128)(2,1)}, bf16[10,160,160]{2,1,0:T(8,128)(2,1)}, bf16[10,80,80]{2,1,0:T(8,128)(2,1)}) custom-call(bf16[10,320,320]{2,1,0:T(8,128)(2,1)} %one_ref, bf16[10,160,160]{2,1,0:T(8,128)(2,1)} %two_ref, bf16[10,80,80]{2,1,0:T(8,128)(2,1)} %three_ref), custom_call_target="tpu_custom_call" | custom-call | tf_op jit(solution)/shard_map/turn_tables/pallas_call | solution.py:654
  57.3 0.6 pad_add_fusion.info_ref
  58.0 5.4 %collective-permute-done.1.right_low = bf16[800,512]{1,0:T(8,128)(2,1)} collective-permute-done((bf16[800,512]{1,0:T(8,128)(2,1)S(1)}, bf16[800,512]{1,0:T(8,128)(2,1)}, u32[]{:S(2)}, u32[]{:S(2)}) %collective-permute-start.1) | collective-permute-done | bytes 819232 | tf_op jit(solution)/shard_map/ppermute | solution.py:593
  63.4 17.6 %collective-permute-done.2.far_low = bf16[800,512]{1,0:T(8,128)(2,1)} collective-permute-done((bf16[800,512]{1,0:T(8,128)(2,1)}, bf16[800,512]{1,0:T(8,128)(2,1)}, u32[]{:S(2)}, u32[]{:S(2)}) %collective-permute-start.2) | collective-permute-done | bytes 819232 | tf_op jit(solution)/shard_map/ppermute | solution.py:595
  81.0 1.5 %copy-done.5 = bf16[32,40,1024]{2,1,0:T(8,128)(2,1)} copy-done((bf16[32,40,1024]{2,1,0:T(8,128)(2,1)}, bf16[32,40,1024]{2,1,0:T(8,128)(2,1)S(1)}, u32[]{:S(2)}) %copy-start.5) | copy-done | bytes 2621464
  82.5 15.7 %levels.1 = (bf16[10,48,512]{2,1,0:T(8,128)(2,1)}, bf16[32,144,128]{2,1,0:T(8,128)(2,1)}, bf16[10,192,640]{2,1,0:T(8,128)(2,1)}) custom-call(s32[14]{0:T(128)} %pad_add_fusion.info_ref, bf16[32,40,1024]{2,1,0:T(8,128)(2,1)} %copy-done.5, bf16[800,512]{1,0:T(8,128)(2,1)} %get-tuple-element.36.own_low, bf16[800,512]{1,0:T(8,128)(2,1)} %collective-permute-done.left_low, ...), custom_call_target="tpu_custom_call" | custom-call | tf_op jit(solution)/shard_map/levels/pallas_call | solution.py:668
  98.2 8.5 %all-to-all-start.1 = ((bf16[32,144,128]{2,1,0:T(8,128)(2,1)}), bf16[32,144,128]{2,1,0:T(8,128)(2,1)}, u32[]{:S(2)}, u32[]{:S(2)}) async-start(bf16[32,144,128]{2,1,0:T(8,128)(2,1)} %get-tuple-element.51), calls=%async_computation.1 | async-start | bytes 2359296 | tf_op jit(solution)/shard_map/all_to_all | solution.py:720
  106.7 2.1 %pack_rest.1.own_ref = bf16[1760,128]{1,0:T(8,128)(2,1)} custom-call(bf16[10,160,641]{2,1,0:T(8,128)(2,1)} %bitcast.13), custom_call_target="tpu_custom_call" | custom-call | tf_op jit(solution)/shard_map/pack_rest/pallas_call | solution.py:634
  108.8 1.2 collective-permute-start.6
  110.0 1.6 %collective-permute-start.7 = (bf16[1760,128]{1,0:T(8,128)(2,1)}, bf16[1760,128]{1,0:T(8,128)(2,1)S(1)}, u32[]{:S(2)}, u32[]{:S(2)}) collective-permute-start(bf16[1760,128]{1,0:T(8,128)(2,1)} %pack_rest.1.own_ref), channel_id=1, source_target_pairs={{0,3},{1,0},{2,1},{3,2},{4,7},{5,4},{6,5},{7,6},{8,11},{9,8},{10,9... | collective-permute-start | bytes 1351688 | tf_op jit(solution)/shard_map/ppermute | solution.py:649
  111.6 1.2 collective-permute-start.8
  112.7 9.2 %collective-permute-done.6.left_ref = bf16[1760,128]{1,0:T(8,128)(2,1)S(1)} collective-permute-done((bf16[1760,128]{1,0:T(8,128)(2,1)}, bf16[1760,128]{1,0:T(8,128)(2,1)S(1)}, u32[]{:S(2)}, u32[]{:S(2)}) %collective-permute-start.6) | collective-permute-done | bytes 450592 | tf_op jit(solution)/shard_map/ppermute | solution.py:648
  122.0 10.8 %collective-permute-done.8.far_ref = bf16[1760,128]{1,0:T(8,128)(2,1)} collective-permute-done((bf16[1760,128]{1,0:T(8,128)(2,1)}, bf16[1760,128]{1,0:T(8,128)(2,1)}, u32[]{:S(2)}, u32[]{:S(2)}) %collective-permute-start.8) | collective-permute-done | bytes 450592 | tf_op jit(solution)/shard_map/ppermute | solution.py:650
  132.8 1.0 copy-done.1
  133.8 4.1 %rest.1 = bf16[10,48,129]{2,1,0:T(8,128)(2,1)S(1)} custom-call(s32[14]{0:T(128)S(1)} %copy-done.4, bf16[10,192,640]{2,1,0:T(8,128)(2,1)S(1)} %copy-done, bf16[1760,128]{1,0:T(8,128)(2,1)S(1)} %copy-done.1, bf16[1760,128]{1,0:T(8,128)(2,1)S(1)} %collective-permute-done.6.left_ref, bf16[1760,128]{1,0:T(8,128)(2,1)S(1)} %collective-permute-done.7.right_ref, ...), custom_call_target="tpu_custom_call" | custom-call | tf_op jit(solution)/shard_map/rest/pallas_call | solution.py:711
  137.9 0.7 copy-done.2
  138.6 0.1 convert_element_type.12
  138.8 0.1 reshape.45.waves_ref
  138.9 2.3 %inverse_tables.1.table_ref = bf16[2240,768]{1,0:T(8,128)(2,1)S(1)} custom-call(f32[1,768]{1,0:T(1,128)S(1)} %reshape.45.waves_ref), custom_call_target="tpu_custom_call" | custom-call | tf_op jit(solution)/shard_map/inverse_tables/pallas_call | solution.py:725
  141.2 1.1 pad_maximum_fusion
  142.3 1.4 copy.14
  143.8 4.4 %inverse.1 = (f32[20,24,1280]{2,1,0:T(8,128)}, f32[10,24,640]{2,1,0:T(8,128)}, f32[5,24,320]{2,1,0:T(8,128)}) custom-call(s32[1]{0:T(128)} %bitcast.6.info_ref, bf16[32,144,128]{2,1,0:T(8,128)(2,1)} %all-to-all-done.1.wire_ref, bf16[2240,768]{1,0:T(8,128)(2,1)S(1)} %inverse_tables.1.table_ref), custom_call_target="tpu_custom_call" | custom-call | tf_op jit(solution)/shard_map/inverse/pallas_call | solution.py:737
  (31 shorter events, 0.7 us)
Async XLA Ops:
  0.6 2.5 %copy-start.7 = (s32[320]{0:T(512)S(1)}, s32[320]{0:T(512)}, u32[]{:S(2)}) copy-start(s32[320]{0:T(512)} %param.8) | copy-start | bytes 3844
  15.1 9.8 %copy-start.6 = (bf16[800,512]{1,0:T(8,128)(2,1)S(1)}, bf16[800,512]{1,0:T(8,128)(2,1)}, u32[]{:S(2)}) copy-start(bf16[800,512]{1,0:T(8,128)(2,1)} %get-tuple-element.36.own_low) | copy-start | bytes 2457604
  15.1 65.8 %all-to-all-start = ((bf16[32,40,1024]{2,1,0:T(8,128)(2,1)}), bf16[32,40,1024]{2,1,0:T(8,128)(2,1)S(1)}, u32[]{:S(2)}, u32[]{:S(2)}) async-start(bf16[32,40,1024]{2,1,0:T(8,128)(2,1)} %dft.1), calls=%async_computation | async-start | bytes 5242880 | tf_op jit(solution)/shard_map/all_to_all | solution.py:632
  24.9 32.4 %copy-start.8 = (s32[3]{0:T(128)S(1)}, s32[3]{0:T(128)}, u32[]{:S(2)}) copy-start(s32[3]{0:T(128)} %param.9) | copy-start | bytes 40
  24.9 21.0 %collective-permute-start = (bf16[800,512]{1,0:T(8,128)(2,1)S(1)}, bf16[800,512]{1,0:T(8,128)(2,1)}, u32[]{:S(2)}, u32[]{:S(2)}) collective-permute-start(bf16[800,512]{1,0:T(8,128)(2,1)S(1)} %copy-done.6), channel_id=1, source_target_pairs={{0,1},{1,2},{2,3},{3,0},{4,5},{5,6},{6,7},{7,4},{8,9},{9,10},{10,1... | collective-permute-start | bytes 2457608 | tf_op jit(solution)/shard_map/ppermute | solution.py:591
  26.2 19.7 %collective-permute-start.4 = (bf16[800,512]{1,0:T(8,128)(2,1)}, bf16[800,512]{1,0:T(8,128)(2,1)}, u32[]{:S(2)}, u32[]{:S(2)}) collective-permute-start(bf16[800,512]{1,0:T(8,128)(2,1)} %get-tuple-element.37.own_high), channel_id=1, source_target_pairs={{0,3},{1,0},{2,1},{3,2},{4,7},{5,4},{6,5},{7,6},{8,11},{9,8},{10,9... | collective-permute-start | bytes 2457608 | tf_op jit(solution)/shard_map/ppermute | solution.py:592
  27.6 35.7 %collective-permute-start.1 = (bf16[800,512]{1,0:T(8,128)(2,1)S(1)}, bf16[800,512]{1,0:T(8,128)(2,1)}, u32[]{:S(2)}, u32[]{:S(2)}) collective-permute-start(bf16[800,512]{1,0:T(8,128)(2,1)S(1)} %copy-done.6), channel_id=1, source_target_pairs={{0,3},{1,0},{2,1},{3,2},{4,7},{5,4},{6,5},{7,6},{8,11},{9,8},{10,9... | collective-permute-start | bytes 2457608 | tf_op jit(solution)/shard_map/ppermute | solution.py:593
  28.9 34.5 %collective-permute-start.3 = (bf16[800,512]{1,0:T(8,128)(2,1)}, bf16[800,512]{1,0:T(8,128)(2,1)}, u32[]{:S(2)}, u32[]{:S(2)}) collective-permute-start(bf16[800,512]{1,0:T(8,128)(2,1)} %get-tuple-element.37.own_high), channel_id=1, source_target_pairs={{0,1},{1,2},{2,3},{3,0},{4,5},{5,6},{6,7},{7,4},{8,9},{9,10},{10,1... | collective-permute-start | bytes 2457608 | tf_op jit(solution)/shard_map/ppermute | solution.py:594
  45.9 35.1 %collective-permute-start.2 = (bf16[800,512]{1,0:T(8,128)(2,1)}, bf16[800,512]{1,0:T(8,128)(2,1)}, u32[]{:S(2)}, u32[]{:S(2)}) collective-permute-start(bf16[800,512]{1,0:T(8,128)(2,1)} %collective-permute-done.left_low), channel_id=1, source_target_pairs={{0,1},{1,2},{2,3},{3,0},{4,5},{5,6},{6,7},{7,4},{8,9},{9,10},{10,1... | collective-permute-start | bytes 2457608 | tf_op jit(solution)/shard_map/ppermute | solution.py:595
  45.9 35.1 %collective-permute-start.5 = (bf16[800,512]{1,0:T(8,128)(2,1)}, bf16[800,512]{1,0:T(8,128)(2,1)}, u32[]{:S(2)}, u32[]{:S(2)}) collective-permute-start(bf16[800,512]{1,0:T(8,128)(2,1)} %collective-permute-done.4.right_high), channel_id=1, source_target_pairs={{0,3},{1,0},{2,1},{3,2},{4,7},{5,4},{6,5},{7,6},{8,11},{9,8},{10,9... | collective-permute-start | bytes 2457608 | tf_op jit(solution)/shard_map/ppermute | solution.py:596
  81.0 1.5 %copy-start.5 = (bf16[32,40,1024]{2,1,0:T(8,128)(2,1)}, bf16[32,40,1024]{2,1,0:T(8,128)(2,1)S(1)}, u32[]{:S(2)}) copy-start(bf16[32,40,1024]{2,1,0:T(8,128)(2,1)S(1)} %all-to-all-done.arrived_hbm) | copy-start | bytes 7864324
  98.2 34.6 %copy-start = (bf16[10,192,640]{2,1,0:T(8,128)(2,1)S(1)}, bf16[10,192,640]{2,1,0:T(8,128)(2,1)}, u32[]{:S(2)}) copy-start(bf16[10,192,640]{2,1,0:T(8,128)(2,1)} %get-tuple-element.48.waves_ref) | copy-start | bytes 7372804
  98.2 34.6 %copy-start.4 = (s32[14]{0:T(128)S(1)}, s32[14]{0:T(128)}, u32[]{:S(2)}) copy-start(s32[14]{0:T(128)} %pad_add_fusion.info_ref) | copy-start | bytes 172
  98.2 45.6 %all-to-all-start.1 = ((bf16[32,144,128]{2,1,0:T(8,128)(2,1)}), bf16[32,144,128]{2,1,0:T(8,128)(2,1)}, u32[]{:S(2)}, u32[]{:S(2)}) async-start(bf16[32,144,128]{2,1,0:T(8,128)(2,1)} %get-tuple-element.51), calls=%async_computation.1 | async-start | bytes 2359296 | tf_op jit(solution)/shard_map/all_to_all | solution.py:720
  108.8 13.2 %collective-permute-start.6 = (bf16[1760,128]{1,0:T(8,128)(2,1)}, bf16[1760,128]{1,0:T(8,128)(2,1)S(1)}, u32[]{:S(2)}, u32[]{:S(2)}) collective-permute-start(bf16[1760,128]{1,0:T(8,128)(2,1)} %pack_rest.1.own_ref), channel_id=1, source_target_pairs={{0,1},{1,2},{2,3},{3,0},{4,5},{5,6},{6,7},{7,4},{8,9},{9,10},{10,1... | collective-permute-start | bytes 1351688 | tf_op jit(solution)/shard_map/ppermute | solution.py:648
  110.0 12.0 %collective-permute-start.7 = (bf16[1760,128]{1,0:T(8,128)(2,1)}, bf16[1760,128]{1,0:T(8,128)(2,1)S(1)}, u32[]{:S(2)}, u32[]{:S(2)}) collective-permute-start(bf16[1760,128]{1,0:T(8,128)(2,1)} %pack_rest.1.own_ref), channel_id=1, source_target_pairs={{0,3},{1,0},{2,1},{3,2},{4,7},{5,4},{6,5},{7,6},{8,11},{9,8},{10,9... | collective-permute-start | bytes 1351688 | tf_op jit(solution)/shard_map/ppermute | solution.py:649
  111.6 21.2 %collective-permute-start.8 = (bf16[1760,128]{1,0:T(8,128)(2,1)}, bf16[1760,128]{1,0:T(8,128)(2,1)}, u32[]{:S(2)}, u32[]{:S(2)}) collective-permute-start(bf16[1760,128]{1,0:T(8,128)(2,1)} %pack_rest.1.own_ref), channel_id=1, source_target_pairs={{0,2},{1,3},{2,0},{3,1},{4,6},{5,7},{6,4},{7,5},{8,10},{9,11},{10,... | collective-permute-start | bytes 1351688 | tf_op jit(solution)/shard_map/ppermute | solution.py:650
  132.8 1.0 copy-start.1
  137.9 0.7 copy-start.2
  138.9 2.4 %copy-start.3 = (bf16[10,48,129]{2,1,0:T(8,128)(2,1)S(1)}, bf16[10,48,129]{2,1,0:T(8,128)(2,1)}, u32[]{:S(2)}) copy-start(bf16[10,48,129]{2,1,0:T(8,128)(2,1)} %copy-done.2) | copy-start | bytes 371524
